TPU v7x, 32 devices: a whole 2x2x4 slice. The times are simulated.
32 devices in a mesh: row: 8 (over z, core), col: 4 (over y, x).
Axes of the slice: x: 2, y: 2, z: 4, core: 2. Of those that a mesh axis runs over, the one named last changes fastest.
Arguments:
- blocks: bfloat16 [128, 8, 256, 256], P('row', 'col'), may hold values from -0.125 to 0.125
- block_cols: int32 [128, 8], P('row', 'col'), may hold values from 0 to 48, as said below
- objective: float32 [49152], P(('col', 'row')), may hold values from -6 to 6
- lower_bound: float32 [49152], P(('col', 'row')), may hold values from -1 to -0.2
- upper_bound: float32 [49152], P(('col', 'row')), may hold values from 0.2 to 1
- right_side: float32 [32768], P(('row', 'col')), may hold values from -6 to 6
- primal_init: float32 [49152], P(('col', 'row')), may hold values from -0.2 to 0.2
- dual_init: float32 [32768], P(('row', 'col')), may hold values from 0 to 1
Outputs:
- primal_final: float32 [49152], P(('col', 'row'))
- dual_final: float32 [32768], P(('row', 'col'))
- step_norms: float32 [8, 2], replicated
Inputs may be any that keep to these rules, and one draw needn't show every extreme that they name: `block_cols`: entry j of a row block indexes column group j // 2; its live entries (below 48) are distinct within one row block and group, 48 marks an empty slot, and in every draw some row block has all 2 slots of some group live.
All inputs are finite; a program needn't handle non-finite values.
Results may differ from a plain program's by a relative error of at most 0.0015.
Values may be sent and summed in bfloat16 or wider, within the bound.
No kernel may reach another device: no remote copies, remote signals or barrier semaphores. Data moves between devices by JAX's collectives and lax.ppermute only.
A program may use at most 64 MiB of HBM per device.

v0:
```python
import jax
import jax.numpy as jnp
from jax import lax
from jax.sharding import PartitionSpec as P

ITERS = 8


step_primal = 0.5
step_dual = 0.5


def per_device(
    blocks, block_cols, objective, lower_bound, upper_bound, right_side, primal_init, dual_init
):
    row_blocks = blocks.shape[0]
    slots = blocks.shape[1]
    width = blocks.shape[2]
    row_devices = lax.axis_size("row")
    col_devices = lax.axis_size("col")
    primal_len = objective.shape[0]
    dual_len = right_side.shape[0]
    col_blocks = primal_len * row_devices // width
    primal_total = float(primal_len * row_devices * col_devices)
    dual_total = float(dual_len * row_devices * col_devices)
    flat_cols = block_cols.reshape(-1)
    chosen = flat_cols[:, None] == jnp.arange(col_blocks, dtype=jnp.int32)[None, :]
    chosen_half = chosen.astype(jnp.bfloat16)
    chosen_full = chosen.astype(jnp.float32)
    history = []
    primal_slab, objective_slab, lower_slab, upper_slab = (
        lax.all_gather(primal_init, "row", axis=0, tiled=True),
        lax.all_gather(objective, "row", axis=0, tiled=True),
        lax.all_gather(lower_bound, "row", axis=0, tiled=True),
        lax.all_gather(upper_bound, "row", axis=0, tiled=True),
    )
    dual_slab, right_slab = (
        lax.all_gather(dual_init, "col", axis=0, tiled=True),
        lax.all_gather(right_side, "col", axis=0, tiled=True),
    )
    primal_offset = lax.axis_index("row") * primal_len
    dual_offset = lax.axis_index("col") * dual_len
    for iteration in range(ITERS):
        dual_half = dual_slab.astype(jnp.bfloat16)
        dual_amount = dual_half.shape[0] // width
        products = jnp.einsum(
            "rsab,ra->rsb",
            blocks,
            dual_half.reshape(dual_amount, width),
            preferred_element_type=jnp.float32,
        ).reshape(dual_amount * slots, width)
        gradient = lax.psum(
            jnp.dot(
                chosen_full.T,
                products,
                precision=lax.Precision.HIGHEST,
                preferred_element_type=jnp.float32,
            ).reshape(-1),
            "row",
        )
        primal_next = jnp.minimum(
            upper_slab,
            jnp.maximum(lower_slab, primal_slab - step_primal * (objective_slab - gradient)),
        )
        extrapolated = (2.0 * primal_next - primal_slab).astype(jnp.bfloat16)
        pick_amount = extrapolated.shape[0] // width
        picked = jnp.dot(
            chosen_half,
            extrapolated.reshape(pick_amount, width),
            preferred_element_type=jnp.float32,
        )
        shaped = picked.astype(jnp.bfloat16).reshape(row_blocks, slots, width)
        image_dual = lax.psum(
            jnp.einsum("rsab,rsb->ra", blocks, shaped, preferred_element_type=jnp.float32).reshape(
                -1
            ),
            "col",
        )
        dual_next = jnp.maximum(dual_slab + step_dual * (right_slab - image_dual), 0.0)
        primal_step = lax.dynamic_slice_in_dim(
            primal_next - primal_slab, primal_offset, primal_len, 0
        )
        dual_step = lax.dynamic_slice_in_dim(dual_next - dual_slab, dual_offset, dual_len, 0)
        summed = lax.psum(
            (jnp.sum(primal_step * primal_step), jnp.sum(dual_step * dual_step)), ("row", "col")
        )
        history.append(jnp.stack(summed))
        primal_slab = primal_next
        dual_slab = dual_next
    primal_out = lax.dynamic_slice_in_dim(primal_slab, primal_offset, primal_len, 0)
    dual_out = lax.dynamic_slice_in_dim(dual_slab, dual_offset, dual_len, 0)
    stacked = jnp.stack(history)
    totals = jnp.array([primal_total, dual_total], jnp.float32)
    step_norms = jnp.sqrt(stacked / totals[None, :])
    return (primal_out, dual_out, step_norms)


def solution(mesh):
    in_specs = (
        P("row", "col", None, None),
        P("row", "col"),
        P(("col", "row")),
        P(("col", "row")),
        P(("col", "row")),
        P(("row", "col")),
        P(("col", "row")),
        P(("row", "col")),
    )
    out_specs = (P(("col", "row")), P(("row", "col")), P())
    return jax.shard_map(
        per_device, mesh=mesh, in_specs=in_specs, out_specs=out_specs, check_vma=False
    )
```

profile of v0, /device:TPU:0, one launch (start us, length us, event | category | flops | bytes accessed | tf_op | source)
XLA Modules:
  0.0 512.1 jit_solution(17273579642622578398)
XLA Ops:
  1.5 9.8 %all_gather.22 = f32[4096]{0:T(1024)S(1)} all-gather(f32[1024]{0:T(1024)} %param.16), channel_id=1, replica_groups=mesh['row'=8,'col'=4] {'col'}, dimensions={0}, use_global_device_ids=true | all-gather | bytes 20480 | tf_op jit(solution)/shard_map/all_gather | solution.py:38
  14.6 27.5 %psum.224 = f32[12288]{0:T(1024)S(1)} all-reduce(f32[12288]{0:T(1024)S(1)} %bitcast.198), channel_id=1, replica_groups=mesh['row'=8,'col'=4] {'row'}, use_global_device_ids=true, to_apply=%region_0.0 | all-reduce | flops 12288 | bytes 98304 | tf_op jit(solution)/shard_map/psum | solution.py:52
  42.2 14.0 %all-gather = f32[8,1,1536]{2,1,0:T(1,128)S(1)} all-gather(f32[1,1,1536]{2,1,0:T(1,128)S(1)} %reshape.200), channel_id=1, replica_groups=mesh['row'=8,'col'=4] {'row'}, dimensions={0}, use_global_device_ids=true | all-gather | bytes 55296 | tf_op jit(solution)/shard_map/all_gather | solution.py:35
  56.2 14.0 %all-gather.1 = f32[8,1,1536]{2,1,0:T(1,128)S(1)} all-gather(f32[1,1,1536]{2,1,0:T(1,128)S(1)} %reshape.202), channel_id=1, replica_groups=mesh['row'=8,'col'=4] {'row'}, dimensions={0}, use_global_device_ids=true | all-gather | bytes 55296 | tf_op jit(solution)/shard_map/all_gather | solution.py:34
  70.2 14.0 %all-gather.3 = f32[8,1,1536]{2,1,0:T(1,128)S(1)} all-gather(f32[1,1,1536]{2,1,0:T(1,128)S(1)} %reshape.206), channel_id=1, replica_groups=mesh['row'=8,'col'=4] {'row'}, dimensions={0}, use_global_device_ids=true | all-gather | bytes 55296 | tf_op jit(solution)/shard_map/all_gather | solution.py:33
  84.3 14.0 %all-gather.2 = f32[8,1,1536]{2,1,0:T(1,128)S(1)} all-gather(f32[1,1,1536]{2,1,0:T(1,128)S(1)} %reshape.204), channel_id=1, replica_groups=mesh['row'=8,'col'=4] {'row'}, dimensions={0}, use_global_device_ids=true | all-gather | bytes 55296 | tf_op jit(solution)/shard_map/all_gather | solution.py:32
  98.5 3.4 fusion.28
  101.9 14.7 %psum.225 = f32[4096]{0:T(1024)S(1)} all-reduce(f32[4096]{0:T(1024)S(1)} %bitcast.215), channel_id=1, replica_groups=mesh['row'=8,'col'=4] {'col'}, use_global_device_ids=true, to_apply=%region_1.0 | all-reduce | flops 4096 | bytes 32768 | tf_op jit(solution)/shard_map/psum | solution.py:73
  116.7 8.1 %all_gather.23 = f32[4096]{0:T(1024)S(1)} all-gather(f32[1024]{0:T(1024)S(1)} %copy-done.4), channel_id=1, replica_groups=mesh['row'=8,'col'=4] {'col'}, dimensions={0}, use_global_device_ids=true | all-gather | bytes 20480 | tf_op jit(solution)/shard_map/all_gather | solution.py:39
  128.1 26.3 %psum.226 = f32[12288]{0:T(1024)S(1)} all-reduce(f32[12288]{0:T(1024)S(1)} %bitcast.199), channel_id=1, replica_groups=mesh['row'=8,'col'=4] {'row'}, use_global_device_ids=true, to_apply=%region_2.0 | all-reduce | flops 12288 | bytes 98304 | tf_op jit(solution)/shard_map/psum | solution.py:52
  158.1 15.1 %psum.227 = f32[4096]{0:T(1024)S(1)} all-reduce(f32[4096]{0:T(1024)S(1)} %bitcast.217), channel_id=1, replica_groups=mesh['row'=8,'col'=4] {'col'}, use_global_device_ids=true, to_apply=%region_3.0 | all-reduce | flops 4096 | bytes 32768 | tf_op jit(solution)/shard_map/psum | solution.py:73
  176.4 26.3 %psum.228 = f32[12288]{0:T(1024)S(1)} all-reduce(f32[12288]{0:T(1024)S(1)} %bitcast.200), channel_id=1, replica_groups=mesh['row'=8,'col'=4] {'row'}, use_global_device_ids=true, to_apply=%region_4.0 | all-reduce | flops 12288 | bytes 98304 | tf_op jit(solution)/shard_map/psum | solution.py:52
  206.4 14.1 %psum.229 = f32[4096]{0:T(1024)S(1)} all-reduce(f32[4096]{0:T(1024)S(1)} %bitcast.219), channel_id=1, replica_groups=mesh['row'=8,'col'=4] {'col'}, use_global_device_ids=true, to_apply=%region_5.0 | all-reduce | flops 4096 | bytes 32768 | tf_op jit(solution)/shard_map/psum | solution.py:73
  223.7 26.3 %psum.230 = f32[12288]{0:T(1024)S(1)} all-reduce(f32[12288]{0:T(1024)S(1)} %bitcast.201), channel_id=1, replica_groups=mesh['row'=8,'col'=4] {'row'}, use_global_device_ids=true, to_apply=%region_6.0 | all-reduce | flops 12288 | bytes 98304 | tf_op jit(solution)/shard_map/psum | solution.py:52
  253.7 15.1 %psum.231 = f32[4096]{0:T(1024)S(1)} all-reduce(f32[4096]{0:T(1024)S(1)} %bitcast.221), channel_id=1, replica_groups=mesh['row'=8,'col'=4] {'col'}, use_global_device_ids=true, to_apply=%region_7.0 | all-reduce | flops 4096 | bytes 32768 | tf_op jit(solution)/shard_map/psum | solution.py:73
  272.0 26.3 %psum.232 = f32[12288]{0:T(1024)S(1)} all-reduce(f32[12288]{0:T(1024)S(1)} %bitcast.202), channel_id=1, replica_groups=mesh['row'=8,'col'=4] {'row'}, use_global_device_ids=true, to_apply=%region_8.0 | all-reduce | flops 12288 | bytes 98304 | tf_op jit(solution)/shard_map/psum | solution.py:52
  302.0 14.1 %psum.233 = f32[4096]{0:T(1024)S(1)} all-reduce(f32[4096]{0:T(1024)S(1)} %bitcast.223), channel_id=1, replica_groups=mesh['row'=8,'col'=4] {'col'}, use_global_device_ids=true, to_apply=%region_9.0 | all-reduce | flops 4096 | bytes 32768 | tf_op jit(solution)/shard_map/psum | solution.py:73
  319.4 26.3 %psum.234 = f32[12288]{0:T(1024)S(1)} all-reduce(f32[12288]{0:T(1024)S(1)} %bitcast.203), channel_id=1, replica_groups=mesh['row'=8,'col'=4] {'row'}, use_global_device_ids=true, to_apply=%region_10.0 | all-reduce | flops 12288 | bytes 98304 | tf_op jit(solution)/shard_map/psum | solution.py:52
  349.4 15.0 %psum.235 = f32[4096]{0:T(1024)S(1)} all-reduce(f32[4096]{0:T(1024)S(1)} %bitcast.225), channel_id=1, replica_groups=mesh['row'=8,'col'=4] {'col'}, use_global_device_ids=true, to_apply=%region_11.0 | all-reduce | flops 4096 | bytes 32768 | tf_op jit(solution)/shard_map/psum | solution.py:73
  367.7 26.3 %psum.236 = f32[12288]{0:T(1024)S(1)} all-reduce(f32[12288]{0:T(1024)S(1)} %bitcast.204), channel_id=1, replica_groups=mesh['row'=8,'col'=4] {'row'}, use_global_device_ids=true, to_apply=%region_12.0 | all-reduce | flops 12288 | bytes 98304 | tf_op jit(solution)/shard_map/psum | solution.py:52
  397.7 14.1 %psum.237 = f32[4096]{0:T(1024)S(1)} all-reduce(f32[4096]{0:T(1024)S(1)} %bitcast.227), channel_id=1, replica_groups=mesh['row'=8,'col'=4] {'col'}, use_global_device_ids=true, to_apply=%region_13.0 | all-reduce | flops 4096 | bytes 32768 | tf_op jit(solution)/shard_map/psum | solution.py:73
  415.1 26.3 %psum.238 = f32[12288]{0:T(1024)S(1)} all-reduce(f32[12288]{0:T(1024)S(1)} %bitcast.205), channel_id=1, replica_groups=mesh['row'=8,'col'=4] {'row'}, use_global_device_ids=true, to_apply=%region_14.0 | all-reduce | flops 12288 | bytes 98304 | tf_op jit(solution)/shard_map/psum | solution.py:52
  445.1 15.0 %psum.239 = f32[4096]{0:T(1024)S(1)} all-reduce(f32[4096]{0:T(1024)S(1)} %bitcast.229), channel_id=1, replica_groups=mesh['row'=8,'col'=4] {'col'}, use_global_device_ids=true, to_apply=%region_15.0 | all-reduce | flops 4096 | bytes 32768 | tf_op jit(solution)/shard_map/psum | solution.py:73
  462.8 37.4 %all-reduce = (f32[1]{0:T(128)}, f32[1]{0:T(128)}, f32[1]{0:T(128)}, f32[1]{0:T(128)}, f32[1]{0:T(128)}, /*index=5*/f32[1]{0:T(128)}, f32[1]{0:T(128)}, f32[1]{0...) all-reduce(f32[1]{0:T(128)} %bitcast.21, ...), channel_id=1, replica_groups=mesh['row'=8,'col'=4] {'row','col'}, use_global_device_ids=true, to_apply=%region_19.0 | all-reduce | flops 16 | bytes 128 | tf_op jit(solution)/shard_map/psum | solution.py:84
  (146 shorter events, 67.0 us)
Async XLA Ops:
  0.6 41.5 %copy-start = (f32[1536]{0:T(1024)S(1)}, f32[1536]{0:T(1024)}, u32[]{:S(2)}) copy-start(f32[1536]{0:T(1024)} %param.13) | copy-start | bytes 18436
  0.6 55.6 %copy-start.1 = (f32[1536]{0:T(1024)S(1)}, f32[1536]{0:T(1024)}, u32[]{:S(2)}) copy-start(f32[1536]{0:T(1024)} %param.12) | copy-start | bytes 18436
  0.7 69.6 %copy-start.2 = (f32[1536]{0:T(1024)S(1)}, f32[1536]{0:T(1024)}, u32[]{:S(2)}) copy-start(f32[1536]{0:T(1024)} %param.11) | copy-start | bytes 18436
  0.7 83.6 %copy-start.3 = (f32[1536]{0:T(1024)S(1)}, f32[1536]{0:T(1024)}, u32[]{:S(2)}) copy-start(f32[1536]{0:T(1024)} %param.15) | copy-start | bytes 18436
  11.4 105.3 %copy-start.4 = (f32[1024]{0:T(1024)S(1)}, f32[1024]{0:T(1024)}, u32[]{:S(2)}) copy-start(f32[1024]{0:T(1024)} %param.14) | copy-start | bytes 12292
  411.9 99.6 %copy-start.5 = (f32[2]{0:T(128)S(1)}, f32[2]{0:T(128)}, u32[]{:S(2)}) copy-start(f32[2]{0:T(128)} %constant.32) | copy-start | bytes 28
where the time goes:
time: 514 us; the launch traced here: 512 us
  blocking collectives  441 us (86%)
  matrix products  53.4 us (10%)
  other arithmetic  14 us (3%)
    psum x8, blocking collectives, per_device(): lax.psum(jnp.dot(chosen_full.T, products, precision=lax.Precision.HIGHEST...  212 us
    psum x8, blocking collectives, per_device(): lax.psum(jnp.einsum('rsab,rsb->ra', blocks, shaped, preferred_element_typ...  117 us
    psum x1, blocking collectives, per_device(): lax.psum((jnp.sum(primal_step * primal_step), jnp.sum(dual_step * dual_st...  37.4 us
    dot_general x8, matrix products, per_device(): jnp.einsum('rsab,rsb->ra', blocks, shaped, preferred_element_type=jnp.flo...  26.9 us
    dot_general x8, matrix products, per_device(): jnp.einsum('rsab,ra->rsb', blocks, dual_half.reshape(dual_amount, width),...  22.7 us
    all_gather x1, blocking collectives, per_device(): lax.all_gather(upper_bound, 'row', axis=0, tiled=True)  14 us
    all_gather x1, blocking collectives, per_device(): lax.all_gather(lower_bound, 'row', axis=0, tiled=True)  14 us
    all_gather x1, blocking collectives, per_device(): lax.all_gather(objective, 'row', axis=0, tiled=True)  14 us

commit v1 on v0

v1 whole, which is shorter than its diff:
```python
import functools

import jax
import jax.numpy as jnp
from jax import lax
from jax.experimental import pallas as pl
from jax.experimental.pallas import tpu as pltpu
from jax.sharding import PartitionSpec as P

ITERS = 8
STEP_PRIMAL = 0.5
STEP_DUAL = 0.5
PAD = 8

F32 = jnp.float32
BF16 = jnp.bfloat16


def is_dual_core():
    return lax.axis_index("row") % 2 == 0


def assemble(ref, parts, first, rows, stride, me):
    for j in range(len(parts)):
        piece = parts[0]
        for o in range(1, len(parts)):
            piece = jnp.where(me == (j ^ o), parts[o], piece)
        ref[pl.ds(first + j * stride, rows), :] = piece


def total_of(refs, rows):
    total = refs[0][pl.ds(0, rows), :]
    for ref in refs[1:]:
        total = total + ref[pl.ds(0, rows), :]
    return total


def dual_body(iteration, last, n_msgs, slots, *refs):
    msgs = refs[:n_msgs]
    (dual_ref, hist_ref, cost_ref, one_ref, mine_ref, theirs_ref) = refs[n_msgs : n_msgs + 6]
    (out_ref, dual_out, hist_out, prod_ref) = refs[n_msgs + 6 :]
    rows = dual_out.shape[0]
    blocks = cost_ref.shape[0]

    @pl.when(is_dual_core())
    def _():
        if iteration == 0:
            each = rows // (2 * n_msgs)
            me = lax.axis_index("col")
            for slab in range(2):
                parts = [m[pl.ds(slab * each, each), :] for m in msgs]
                assemble(dual_out, parts, slab * (rows // 2), each, each, me)
            dual_next = dual_out[...]
            norm = jnp.zeros((1, dual_next.shape[1]), F32)
            hist_out[...] = jnp.zeros_like(hist_out)
        else:
            total = total_of(msgs, rows + PAD)
            dual = dual_ref[...]
            dual_next = jnp.maximum(dual - STEP_DUAL * total[:rows], 0.0)
            step = dual_next - dual
            norm = jnp.sum(step * step, axis=0, keepdims=True)
            dual_out[...] = dual_next
            hist_out[...] = hist_ref[...]
            hist_out[pl.ds(iteration - 1, 1), :] = total[rows : rows + 1]
        if last:
            out_ref[...] = jnp.zeros_like(out_ref)
            out_ref[pl.ds(0, 1), :] = norm
            return
        half = dual_next.astype(BF16)
        for slab, blk_ref in enumerate((mine_ref, theirs_ref)):
            for b in range(blk_ref.shape[0]):
                e = slab * blk_ref.shape[0] + b
                r = e // slots
                prod_ref[pl.ds(e, 1), :] = jnp.dot(
                    half[r : r + 1], blk_ref[b], preferred_element_type=F32
                )
        prod = prod_ref[...]
        high = prod.astype(BF16)
        rest = prod - high.astype(F32)
        mid = rest.astype(BF16)
        low = (rest - mid.astype(F32)).astype(BF16)
        stacked = jnp.concatenate([high, mid, low], axis=0)
        grad = jnp.dot(one_ref[...], stacked, preferred_element_type=F32)
        out_ref[pl.ds(0, blocks), :] = grad - cost_ref[...]
        out_ref[pl.ds(blocks, PAD), :] = jnp.concatenate(
            [norm, jnp.zeros((PAD - 1, norm.shape[1]), F32)], axis=0
        )


def primal_body(iteration, n_msgs, slots, *refs):
    msgs = refs[:n_msgs]
    (primal_ref, low_ref, up_ref, hist_ref, right_ref, pick_ref, mine_ref, theirs_ref) = refs[
        n_msgs : n_msgs + 8
    ]
    (out_ref, primal_out, low_out, up_out, hist_out) = refs[n_msgs + 8 : n_msgs + 13]
    blocks = primal_out.shape[0]
    rows = right_ref.shape[0]

    @pl.when(jnp.logical_not(is_dual_core()))
    def _():
        total = total_of(msgs, blocks + PAD)
        if iteration == 0:
            each = blocks // n_msgs
            me = lax.axis_index("row") // 2
            for k, ref in enumerate((primal_out, low_out, up_out)):
                parts = [m[pl.ds(blocks + PAD + k * each, each), :] for m in msgs]
                assemble(ref, parts, 0, each, each, me)
            primal, low, up = primal_out[...], low_out[...], up_out[...]
            hist_out[...] = jnp.zeros_like(hist_out)
        else:
            primal, low, up = primal_ref[...], low_ref[...], up_ref[...]
            low_out[...] = low
            up_out[...] = up
            hist_out[...] = hist_ref[...]
            hist_out[pl.ds(iteration - 1, 1), :] = total[blocks : blocks + 1]
        primal_next = jnp.minimum(up, jnp.maximum(low, primal + STEP_PRIMAL * total[:blocks]))
        step = primal_next - primal
        norm = jnp.sum(step * step, axis=0, keepdims=True)
        primal_out[...] = primal_next
        ext = (2.0 * primal_next - primal).astype(BF16)
        picked = jnp.dot(pick_ref[...], ext, preferred_element_type=F32).astype(BF16)
        for slab, blk_ref in enumerate((theirs_ref, mine_ref)):
            for r in range(blk_ref.shape[0] // slots):
                acc = None
                for s in range(slots):
                    b = r * slots + s
                    e = slab * blk_ref.shape[0] + b
                    term = lax.dot_general(
                        picked[e : e + 1],
                        blk_ref[b],
                        (((1,), (1,)), ((), ())),
                        preferred_element_type=F32,
                    )
                    acc = term if acc is None else acc + term
                row = slab * (rows // 2) + r
                out_ref[pl.ds(row, 1), :] = acc - right_ref[pl.ds(row, 1), :]
        out_ref[pl.ds(rows, PAD), :] = jnp.concatenate(
            [norm, jnp.zeros((PAD - 1, norm.shape[1]), F32)], axis=0
        )


def local_call(body, outs, scratch, n_in):
    return pl.pallas_call(
        body,
        out_shape=outs,
        in_specs=[pl.BlockSpec(memory_space=pltpu.VMEM)] * n_in,
        out_specs=[pl.BlockSpec(memory_space=pltpu.VMEM)] * len(outs),
        scratch_shapes=scratch,
        compiler_params=pltpu.CompilerParams(vmem_limit_bytes=24 * 2**20),
    )


def per_device(
    blocks, block_cols, objective, lower_bound, upper_bound, right_side, primal_init, dual_init
):
    slab_rows, slots, width = blocks.shape[0], blocks.shape[1], blocks.shape[2]
    n_row, n_col = lax.axis_size("row"), lax.axis_size("col")
    n_z = n_row // 2
    p_rows = primal_init.shape[0] // width
    d_rows = dual_init.shape[0] // width
    col_blocks = p_rows * n_row
    rows = 2 * slab_rows
    row, col = lax.axis_index("row"), lax.axis_index("col")
    core, z = row % 2, row // 2
    is_dual = core == 0

    swap_pairs = [(r, r ^ 1) for r in range(n_row)]

    def over_z(src, o):
        away = [(2 * k + src, 2 * (k ^ o) + 1 - src) for k in range(n_z)]
        return away + [(2 * k + 1 - src, 2 * k + src) for k in range(n_z)]

    def over_col(src, o):
        pairs = []
        for k in range(n_z):
            for c in range(n_col):
                pairs.append(((2 * k + src) * n_col + c, (2 * k + 1 - src) * n_col + (c ^ o)))
                pairs.append(((2 * k + 1 - src) * n_col + c, (2 * k + src) * n_col + c))
        return pairs

    def to_primal(x):
        return [lax.ppermute(x, "row", over_z(0, o)) for o in range(n_z)]

    def to_dual(x):
        return [lax.ppermute(x, ("row", "col"), over_col(1, o)) for o in range(n_col)]

    own = jnp.concatenate(
        [
            dual_init.reshape(d_rows, width),
            right_side.reshape(d_rows, width),
            objective.reshape(p_rows, width),
            primal_init.reshape(p_rows, width),
            lower_bound.reshape(p_rows, width),
            upper_bound.reshape(p_rows, width),
            jnp.pad(
                block_cols.astype(F32).reshape(-1, slab_rows * slots),
                ((0, 0), (0, width - slab_rows * slots)),
            ),
        ],
        axis=0,
    )
    other = lax.ppermute(own, "row", swap_pairs)
    mine = blocks.reshape(slab_rows * slots, width, width)
    theirs = lax.ppermute(mine, "row", swap_pairs)
    first = jnp.where(is_dual, own, other)
    second = jnp.where(is_dual, other, own)

    def both(lo, n):
        return jnp.concatenate([first[lo : lo + n], second[lo : lo + n]], axis=0)

    at = 0
    parts = []
    for n in (d_rows, d_rows, p_rows, p_rows, p_rows, p_rows):
        parts.append(both(at, n))
        at += n
    dual_part, right_part, cost_part, primal_part, low_part, up_part = parts
    cols = both(at, 1)[:, : slab_rows * slots].reshape(1, -1)
    one_hot = (cols == jnp.arange(col_blocks, dtype=F32)[:, None]).astype(BF16)
    one_three = jnp.concatenate([one_hot] * 3, axis=1)
    pick = one_hot.T
    cost = lax.dynamic_update_slice_in_dim(
        jnp.zeros((col_blocks, width), F32), cost_part, z * 2 * p_rows, 0
    )
    right = jnp.zeros((rows, width), F32)
    for slab in range(2):
        right = lax.dynamic_update_slice_in_dim(
            right,
            right_part[slab * d_rows : (slab + 1) * d_rows],
            slab * slab_rows + col * d_rows,
            0,
        )

    def shape(n, dtype=F32):
        return jax.ShapeDtypeStruct((n, width), dtype)

    hist_rows = -(-ITERS // 8) * 8
    dual = jnp.zeros((rows, width), F32)
    primal_hist = jnp.zeros((hist_rows, width), F32)
    dual_hist = primal_hist
    primal = low = up = jnp.zeros((col_blocks, width), F32)
    products = pltpu.VMEM((2 * slab_rows * slots, width), F32)

    arrived = to_dual(dual_part)
    for iteration in range(ITERS):
        message, dual, primal_hist = local_call(
            functools.partial(dual_body, iteration, False, n_col, slots),
            [shape(col_blocks + PAD), shape(rows), shape(hist_rows)],
            [products],
            n_col + 6,
        )(*arrived, dual, primal_hist, cost, one_three, mine, theirs)
        if iteration == 0:
            message = jnp.concatenate([message, primal_part, low_part, up_part], axis=0)
        arrived = to_primal(message)
        message, primal, low, up, dual_hist = local_call(
            functools.partial(primal_body, iteration, n_z, slots),
            [shape(rows + PAD), shape(col_blocks), shape(col_blocks), shape(col_blocks), shape(hist_rows)],
            [],
            n_z + 8,
        )(*arrived, primal, low, up, dual_hist, right, pick, mine, theirs)
        arrived = to_dual(message)
    message, dual, primal_hist = local_call(
        functools.partial(dual_body, ITERS, True, n_col, slots),
        [shape(PAD), shape(rows), shape(hist_rows)],
        [products],
        n_col + 6,
    )(*arrived, dual, primal_hist, cost, one_three, mine, theirs)

    send_rows = max(p_rows, d_rows)
    dual_away = lax.dynamic_slice_in_dim(dual, slab_rows + col * d_rows, d_rows, 0)
    primal_away = lax.dynamic_slice_in_dim(primal, z * 2 * p_rows, p_rows, 0)
    away = jnp.where(
        is_dual,
        jnp.pad(dual_away, ((0, send_rows - d_rows), (0, 0))),
        jnp.pad(primal_away, ((0, send_rows - p_rows), (0, 0))),
    )
    back = lax.ppermute(away, "row", swap_pairs)
    dual_mine = lax.dynamic_slice_in_dim(dual, col * d_rows, d_rows, 0)
    primal_mine = lax.dynamic_slice_in_dim(primal, z * 2 * p_rows + p_rows, p_rows, 0)
    dual_out = jnp.where(is_dual, dual_mine, back[:d_rows]).reshape(-1)
    primal_out = jnp.where(is_dual, back[:p_rows], primal_mine).reshape(-1)

    arrived = to_primal(jnp.concatenate([message, primal_hist], axis=0))
    last_dual = sum(a[:1] for a in arrived)
    primal_sq = jnp.sum(arrived[0][PAD : PAD + ITERS], axis=1)
    dual_sq = jnp.sum(
        lax.dynamic_update_slice_in_dim(dual_hist, last_dual, ITERS - 1, 0)[:ITERS], axis=1
    )
    totals = jnp.array(
        [float(primal_init.shape[0] * n_row * n_col), float(dual_init.shape[0] * n_row * n_col)], F32
    )
    norms = jnp.sqrt(jnp.stack([primal_sq, dual_sq], axis=1) / totals[None, :])
    norms = jnp.where(is_dual, lax.ppermute(norms, "row", swap_pairs), norms)
    return (primal_out, dual_out, norms)


def solution(mesh):
    in_specs = (
        P("row", "col", None, None),
        P("row", "col"),
        P(("col", "row")),
        P(("col", "row")),
        P(("col", "row")),
        P(("row", "col")),
        P(("col", "row")),
        P(("row", "col")),
    )
    out_specs = (P(("col", "row")), P(("row", "col")), P())
    return jax.shard_map(
        per_device, mesh=mesh, in_specs=in_specs, out_specs=out_specs, check_vma=False
    )
```

time: 514 us -> 200 us (0.39)
  blocking collectives: 441 us -> 0 us
  starting transfers between devices: 0 us -> 83.3 us
  matrix products: 53.4 us -> 0 us
  waiting for transfers between devices: 0 us -> 50.9 us
  Pallas kernels: 0 us -> 48.8 us
  other arithmetic: 14 us -> 1.88 us
  local copies, waits for them, and re-layouts: 2.91 us -> 13.1 us
    psum x17 -> x0, blocking collectives: 367 us -> none  [the longest x8 212 us: per_device(): lax.psum(jnp.dot(chosen_full.T, products, precision=lax.Precision.HIGHEST...]
    ppermute x0 -> x76, starting transfers between devices: none -> 83.3 us  [the longest x36 51.4 us: to_dual(): lax.ppermute(x, ('row', 'col'), over_col(1, o))]
    all_gather x6 -> x0, blocking collectives: 74 us -> none  [the longest x1 14 us: per_device(): lax.all_gather(upper_bound, 'row', axis=0, tiled=True)]
    dot_general x32 -> x0, matrix products: 53.4 us -> none  [the longest x8 26.9 us: per_device(): jnp.einsum('rsab,rsb->ra', blocks, shaped, preferred_element_type=jnp.flo...]
    ppermute x0 -> x76, waiting for transfers between devices: none -> 50.9 us  [the longest x36 33.2 us: to_dual(): lax.ppermute(x, ('row', 'col'), over_col(1, o))]
    pallas_call x0 -> x17, Pallas kernels: none -> 48.8 us  [the longest x8 28.3 us: per_device(): local_call(functools.partial(dual_body, iteration, False, n_col, slots),...]
    another operation x4 -> x0, other arithmetic: 10.4 us -> none  [per_device(): stacked = jnp.stack(history)]
    unnamed x33 -> x12, local copies, waits for them, and re-layouts: 1.23 us -> 7.17 us
  transfers between devices with their start and end apart: 0 -> 76, of which waited for: 0 -> 45; matrix products, arithmetic and copies ran while one was open for 0% -> 4% of each run, Pallas kernels for 0% -> 0%
where the time goes in v1:
time: 200 us; the launch traced here: 199 us
  starting transfers between devices  83.3 us (42%)
  waiting for transfers between devices  50.9 us (25%)
  Pallas kernels  48.8 us (24%)
  local copies, waits for them, and re-layouts  13.1 us (7%)
    ppermute x36, starting transfers between devices, to_dual(): lax.ppermute(x, ('row', 'col'), over_col(1, o))  51.4 us
    ppermute x36, waiting for transfers between devices, to_dual(): lax.ppermute(x, ('row', 'col'), over_col(1, o))  33.2 us
    ppermute x36, starting transfers between devices, to_primal(): return [lax.ppermute(x, 'row', over_z(0, o)) for o in range(n_z)]  29.7 us
    pallas_call x8, Pallas kernels, per_device(): local_call(functools.partial(dual_body, iteration, False, n_col, slots),...  28.3 us
    pallas_call x8, Pallas kernels, per_device(): local_call(functools.partial(primal_body, iteration, n_z, slots), [shape(...  18.3 us
    ppermute x36, waiting for transfers between devices, to_primal(): return [lax.ppermute(x, 'row', over_z(0, o)) for o in range(n_z)]  15.7 us
    unnamed x12, local copies, waits for them, and re-layouts  7.17 us
  transfers between devices with their start and end apart: 76, of which 45 were waited for; matrix products, arithmetic and copies ran while one was open for 4% of the time, Pallas kernels for 0%

profile of v1, /device:TPU:0, one launch (start us, length us, event | category | flops | bytes accessed | tf_op | source)
XLA Modules:
  0.0 199.0 jit_solution(8026132411519524943)
XLA Ops:
  9.0 2.6 %collective-permute-start.3 = (f32[8,256]{1,0:T(8,128)S(1)}, f32[8,256]{1,0:T(8,128)S(1)}, u32[]{:S(2)}, u32[]{:S(2)}) collective-permute-start(f32[8,256]{1,0:T(8,128)S(1)} %pad_maximum_fusion.1), channel_id=1, source_target_pairs={{4,2},{0,4},{5,3},{1,5},{6,0},{2,6},{7,1},{3,7},{12,10},{8,12},{13... | collective-permute-start | bytes 24584 | tf_op jit(solution)/shard_map/ppermute | solution.py:185
  17.7 3.5 %shard_map.112 = (f32[56,256]{1,0:T(8,128)S(1)}, f32[32,256]{1,0:T(8,128)S(1)}, f32[8,256]{1,0:T(8,128)S(1)}) custom-call(f32[8,256]{1,0:T(8,128)S(1)} %collective-permute-done.1.refs_0_, f32[8,256]{1,0:T(8,128)S(1)} %collective-permute-done.2.refs_1_, f32[8,256]{1,0:T(8,128)S(1)} %collective-permute-done.3.refs_2_, ...), custom_call_target="tpu_custom_call" | custom-call | tf_op jit(solution)/shard_map/pallas_call | solution.py:245
  30.3 2.3 %shard_map.113 = (f32[40,256]{1,0:T(8,128)S(1)}, f32[48,256]{1,0:T(8,128)S(1)}, f32[48,256]{1,0:T(8,128)S(1)}, f32[48,256]{1,0:T(8,128)S(1)}, f32[8,256]{1,0:T(8,128)S(1)}) custom-call(f32[92,256]{1,0:T(8,128)S(1)} %collective-permute-done.6.refs_0_, f32[92,256]{1,0:T(8,128)S(1)} %collective-permute-done.7.refs_1_, ...), custom_call_target="tpu_custom_call" | custom-call | tf_op jit(solution)/shard_map/pallas_call | solution.py:254
  32.7 4.7 %collective-permute-start.10 = (f32[40,256]{1,0:T(8,128)S(1)}, f32[40,256]{1,0:T(8,128)S(1)}, u32[]{:S(2)}, u32[]{:S(2)}) collective-permute-start(f32[40,256]{1,0:T(8,128)S(1)} %get-tuple-element.69), channel_id=1, source_target_pairs={{4,0},{0,4},{5,1},{1,5},{6,2},{2,6},{7,3},{3,7},{12,8},{8,12},{13,... | collective-permute-start | bytes 122888 | tf_op jit(solution)/shard_map/ppermute | solution.py:185
  42.4 3.5 %shard_map.114 = (f32[56,256]{1,0:T(8,128)S(1)}, f32[32,256]{1,0:T(8,128)S(1)}, f32[8,256]{1,0:T(8,128)S(1)}) custom-call(f32[40,256]{1,0:T(8,128)S(1)} %collective-permute-done.10.refs_0_, f32[40,256]{1,0:T(8,128)S(1)} %collective-permute-done.11.refs_1_, f32[40,256]{1,0:T(8,128)S(1)} %collective-permute-done.12.refs_2_, ...), custom_call_target="tpu_custom_call" | custom-call | tf_op jit(solution)/shard_map/pallas_call | solution.py:245
  54.1 4.0 %collective-permute-start.18 = (f32[40,256]{1,0:T(8,128)S(1)}, f32[40,256]{1,0:T(8,128)S(1)}, u32[]{:S(2)}, u32[]{:S(2)}) collective-permute-start(f32[40,256]{1,0:T(8,128)S(1)} %get-tuple-element.77), channel_id=1, source_target_pairs={{4,0},{0,4},{5,1},{1,5},{6,2},{2,6},{7,3},{3,7},{12,8},{8,12},{13,... | collective-permute-start | bytes 122888 | tf_op jit(solution)/shard_map/ppermute | solution.py:185
  64.1 3.5 %shard_map.116 = (f32[56,256]{1,0:T(8,128)S(1)}, f32[32,256]{1,0:T(8,128)S(1)}, f32[8,256]{1,0:T(8,128)S(1)}) custom-call(f32[40,256]{1,0:T(8,128)S(1)} %collective-permute-done.18.refs_0_, f32[40,256]{1,0:T(8,128)S(1)} %collective-permute-done.19.refs_1_, f32[40,256]{1,0:T(8,128)S(1)} %collective-permute-done.20.refs_2_, ...), custom_call_target="tpu_custom_call" | custom-call | tf_op jit(solution)/shard_map/pallas_call | solution.py:245
  67.9 2.3 %collective-permute-start.25 = (f32[56,256]{1,0:T(8,128)S(1)}, f32[56,256]{1,0:T(8,128)S(1)}, u32[]{:S(2)}, u32[]{:S(2)}) collective-permute-start(f32[56,256]{1,0:T(8,128)S(1)} %get-tuple-element.80), channel_id=1, source_target_pairs={{0,28},{8,20},{16,12},{24,4},{4,0},{12,8},{20,16},{28,24},{1,29},{... | collective-permute-start | bytes 172040 | tf_op jit(solution)/shard_map/ppermute | solution.py:182
  72.0 2.2 %shard_map.117 = (f32[40,256]{1,0:T(8,128)S(1)}, f32[48,256]{1,0:T(8,128)S(1)}, f32[48,256]{1,0:T(8,128)S(1)}, f32[48,256]{1,0:T(8,128)S(1)}, f32[8,256]{1,0:T(8,128)S(1)}) custom-call(f32[56,256]{1,0:T(8,128)S(1)} %collective-permute-done.22.refs_0_, f32[56,256]{1,0:T(8,128)S(1)} %collective-permute-done.23.refs_1_, ...), custom_call_target="tpu_custom_call" | custom-call | tf_op jit(solution)/shard_map/pallas_call | solution.py:254
  74.2 4.2 %collective-permute-start.26 = (f32[40,256]{1,0:T(8,128)S(1)}, f32[40,256]{1,0:T(8,128)S(1)}, u32[]{:S(2)}, u32[]{:S(2)}) collective-permute-start(f32[40,256]{1,0:T(8,128)S(1)} %get-tuple-element.85), channel_id=1, source_target_pairs={{4,0},{0,4},{5,1},{1,5},{6,2},{2,6},{7,3},{3,7},{12,8},{8,12},{13,... | collective-permute-start | bytes 122888 | tf_op jit(solution)/shard_map/ppermute | solution.py:185
  83.4 3.5 %shard_map.118 = (f32[56,256]{1,0:T(8,128)S(1)}, f32[32,256]{1,0:T(8,128)S(1)}, f32[8,256]{1,0:T(8,128)S(1)}) custom-call(f32[40,256]{1,0:T(8,128)S(1)} %collective-permute-done.26.refs_0_, f32[40,256]{1,0:T(8,128)S(1)} %collective-permute-done.27.refs_1_, f32[40,256]{1,0:T(8,128)S(1)} %collective-permute-done.28.refs_2_, ...), custom_call_target="tpu_custom_call" | custom-call | tf_op jit(solution)/shard_map/pallas_call | solution.py:245
  92.0 2.2 %shard_map.119 = (f32[40,256]{1,0:T(8,128)S(1)}, f32[48,256]{1,0:T(8,128)S(1)}, f32[48,256]{1,0:T(8,128)S(1)}, f32[48,256]{1,0:T(8,128)S(1)}, f32[8,256]{1,0:T(8,128)S(1)}) custom-call(f32[56,256]{1,0:T(8,128)S(1)} %collective-permute-done.30.refs_0_, f32[56,256]{1,0:T(8,128)S(1)} %collective-permute-done.31.refs_1_, ...), custom_call_target="tpu_custom_call" | custom-call | tf_op jit(solution)/shard_map/pallas_call | solution.py:254
  94.2 4.5 %collective-permute-start.34 = (f32[40,256]{1,0:T(8,128)S(1)}, f32[40,256]{1,0:T(8,128)S(1)}, u32[]{:S(2)}, u32[]{:S(2)}) collective-permute-start(f32[40,256]{1,0:T(8,128)S(1)} %get-tuple-element.93), channel_id=1, source_target_pairs={{4,0},{0,4},{5,1},{1,5},{6,2},{2,6},{7,3},{3,7},{12,8},{8,12},{13,... | collective-permute-start | bytes 122888 | tf_op jit(solution)/shard_map/ppermute | solution.py:185
  104.6 3.5 %shard_map.120 = (f32[56,256]{1,0:T(8,128)S(1)}, f32[32,256]{1,0:T(8,128)S(1)}, f32[8,256]{1,0:T(8,128)S(1)}) custom-call(f32[40,256]{1,0:T(8,128)S(1)} %collective-permute-done.34.refs_0_, f32[40,256]{1,0:T(8,128)S(1)} %collective-permute-done.35.refs_1_, f32[40,256]{1,0:T(8,128)S(1)} %collective-permute-done.36.refs_2_, ...), custom_call_target="tpu_custom_call" | custom-call | tf_op jit(solution)/shard_map/pallas_call | solution.py:245
  112.8 2.2 %shard_map.121 = (f32[40,256]{1,0:T(8,128)S(1)}, f32[48,256]{1,0:T(8,128)S(1)}, f32[48,256]{1,0:T(8,128)S(1)}, f32[48,256]{1,0:T(8,128)S(1)}, f32[8,256]{1,0:T(8,128)S(1)}) custom-call(f32[56,256]{1,0:T(8,128)S(1)} %collective-permute-done.38.refs_0_, f32[56,256]{1,0:T(8,128)S(1)} %collective-permute-done.39.refs_1_, ...), custom_call_target="tpu_custom_call" | custom-call | tf_op jit(solution)/shard_map/pallas_call | solution.py:254
  115.0 4.1 %collective-permute-start.42 = (f32[40,256]{1,0:T(8,128)S(1)}, f32[40,256]{1,0:T(8,128)S(1)}, u32[]{:S(2)}, u32[]{:S(2)}) collective-permute-start(f32[40,256]{1,0:T(8,128)S(1)} %get-tuple-element.101), channel_id=1, source_target_pairs={{4,0},{0,4},{5,1},{1,5},{6,2},{2,6},{7,3},{3,7},{12,8},{8,12},{13,... | collective-permute-start | bytes 122888 | tf_op jit(solution)/shard_map/ppermute | solution.py:185
  124.1 3.5 %shard_map.122 = (f32[56,256]{1,0:T(8,128)S(1)}, f32[32,256]{1,0:T(8,128)S(1)}, f32[8,256]{1,0:T(8,128)S(1)}) custom-call(f32[40,256]{1,0:T(8,128)S(1)} %collective-permute-done.42.refs_0_, f32[40,256]{1,0:T(8,128)S(1)} %collective-permute-done.43.refs_1_, f32[40,256]{1,0:T(8,128)S(1)} %collective-permute-done.44.refs_2_, ...), custom_call_target="tpu_custom_call" | custom-call | tf_op jit(solution)/shard_map/pallas_call | solution.py:245
  134.9 4.4 %collective-permute-start.50 = (f32[40,256]{1,0:T(8,128)S(1)}, f32[40,256]{1,0:T(8,128)S(1)}, u32[]{:S(2)}, u32[]{:S(2)}) collective-permute-start(f32[40,256]{1,0:T(8,128)S(1)} %get-tuple-element.109), channel_id=1, source_target_pairs={{4,0},{0,4},{5,1},{1,5},{6,2},{2,6},{7,3},{3,7},{12,8},{8,12},{13,... | collective-permute-start | bytes 122888 | tf_op jit(solution)/shard_map/ppermute | solution.py:185
  145.3 3.5 %shard_map.124 = (f32[56,256]{1,0:T(8,128)S(1)}, f32[32,256]{1,0:T(8,128)S(1)}, f32[8,256]{1,0:T(8,128)S(1)}) custom-call(f32[40,256]{1,0:T(8,128)S(1)} %collective-permute-done.50.refs_0_, f32[40,256]{1,0:T(8,128)S(1)} %collective-permute-done.51.refs_1_, f32[40,256]{1,0:T(8,128)S(1)} %collective-permute-done.52.refs_2_, ...), custom_call_target="tpu_custom_call" | custom-call | tf_op jit(solution)/shard_map/pallas_call | solution.py:245
  155.8 4.0 %collective-permute-start.58 = (f32[40,256]{1,0:T(8,128)S(1)}, f32[40,256]{1,0:T(8,128)S(1)}, u32[]{:S(2)}, u32[]{:S(2)}) collective-permute-start(f32[40,256]{1,0:T(8,128)S(1)} %get-tuple-element.117), channel_id=1, source_target_pairs={{4,0},{0,4},{5,1},{1,5},{6,2},{2,6},{7,3},{3,7},{12,8},{8,12},{13,... | collective-permute-start | bytes 122888 | tf_op jit(solution)/shard_map/ppermute | solution.py:185
  164.7 3.5 %shard_map.126 = (f32[56,256]{1,0:T(8,128)S(1)}, f32[32,256]{1,0:T(8,128)S(1)}, f32[8,256]{1,0:T(8,128)S(1)}) custom-call(f32[40,256]{1,0:T(8,128)S(1)} %collective-permute-done.58.refs_0_, f32[40,256]{1,0:T(8,128)S(1)} %collective-permute-done.59.refs_1_, f32[40,256]{1,0:T(8,128)S(1)} %collective-permute-done.60.refs_2_, ...), custom_call_target="tpu_custom_call" | custom-call | tf_op jit(solution)/shard_map/pallas_call | solution.py:245
  173.5 2.8 %shard_map.127 = (f32[40,256]{1,0:T(8,128)S(1)}, f32[48,256]{1,0:T(8,128)S(1)}, f32[48,256]{1,0:T(8,128)}, f32[48,256]{1,0:T(8,128)}, f32[8,256]{1,0:T(8,128)S(1)}) custom-call(f32[56,256]{1,0:T(8,128)S(1)} %collective-permute-done.62.refs_0_, f32[56,256]{1,0:T(8,128)S(1)} %collective-permute-done.63.refs_1_, f32[56,256]{1,0:T(8,128)S(1)} %collective-permute-done.64.refs_2_, ...), custom_call_target="tpu_custom_call" | custom-call | tf_op jit(solution)/shard_map/pallas_call | solution.py:254
  176.4 4.3 %collective-permute-start.66 = (f32[40,256]{1,0:T(8,128)S(1)}, f32[40,256]{1,0:T(8,128)S(1)}, u32[]{:S(2)}, u32[]{:S(2)}) collective-permute-start(f32[40,256]{1,0:T(8,128)S(1)} %get-tuple-element.125), channel_id=1, source_target_pairs={{4,0},{0,4},{5,1},{1,5},{6,2},{2,6},{7,3},{3,7},{12,8},{8,12},{13,... | collective-permute-start | bytes 122888 | tf_op jit(solution)/shard_map/ppermute | solution.py:185
  188.8 2.2 %shard_map.128 = (f32[8,256]{1,0:T(8,128)S(1)}, f32[32,256]{1,0:T(8,128)S(1)}, f32[8,256]{1,0:T(8,128)S(1)}) custom-call(f32[40,256]{1,0:T(8,128)S(1)} %collective-permute-done.66.refs_0_, f32[40,256]{1,0:T(8,128)S(1)} %collective-permute-done.67.refs_1_, f32[40,256]{1,0:T(8,128)S(1)} %collective-permute-done.68.refs_2_, ...), custom_call_target="tpu_custom_call" | custom-call | tf_op jit(solution)/shard_map/pallas_call | solution.py:261
  (200 shorter events, 116.4 us)
Async XLA Ops:
  0.6 14.9 %collective-permute-start.5 = (bf16[32,256,256]{2,1,0:T(8,128)(2,1)}, bf16[32,256,256]{2,1,0:T(8,128)(2,1)}, u32[]{:S(2)}, u32[]{:S(2)}) collective-permute-start(bf16[32,256,256]{2,1,0:T(8,128)(2,1)} %bitcast.6), channel_id=1, source_target_pairs={{0,4},{4,0},{8,12},{12,8},{16,20},{20,16},{24,28},{28,24},{1,5},{5... | collective-permute-start | bytes 12582920 | tf_op jit(solution)/shard_map/ppermute | solution.py:204
  9.0 5.0 %collective-permute-start.3 = (f32[8,256]{1,0:T(8,128)S(1)}, f32[8,256]{1,0:T(8,128)S(1)}, u32[]{:S(2)}, u32[]{:S(2)}) collective-permute-start(f32[8,256]{1,0:T(8,128)S(1)} %pad_maximum_fusion.1), channel_id=1, source_target_pairs={{4,2},{0,4},{5,3},{1,5},{6,0},{2,6},{7,1},{3,7},{12,10},{8,12},{13... | collective-permute-start | bytes 24584 | tf_op jit(solution)/shard_map/ppermute | solution.py:185
  21.6 4.4 %collective-permute-start.6 = (f32[92,256]{1,0:T(8,128)S(1)}, f32[92,256]{1,0:T(8,128)S(1)}, u32[]{:S(2)}, u32[]{:S(2)}) collective-permute-start(f32[92,256]{1,0:T(8,128)S(1)} %concatenate.29), channel_id=1, source_target_pairs={{0,4},{8,12},{16,20},{24,28},{4,0},{12,8},{20,16},{28,24},{1,5},{9... | collective-permute-start | bytes 282632 | tf_op jit(solution)/shard_map/ppermute | solution.py:182
  21.7 4.4 %collective-permute-start.7 = (f32[92,256]{1,0:T(8,128)S(1)}, f32[92,256]{1,0:T(8,128)S(1)}, u32[]{:S(2)}, u32[]{:S(2)}) collective-permute-start(f32[92,256]{1,0:T(8,128)S(1)} %concatenate.29), channel_id=1, source_target_pairs={{0,12},{8,4},{16,28},{24,20},{4,0},{12,8},{20,16},{28,24},{1,13},{... | collective-permute-start | bytes 282632 | tf_op jit(solution)/shard_map/ppermute | solution.py:182
  32.7 6.4 %collective-permute-start.10 = (f32[40,256]{1,0:T(8,128)S(1)}, f32[40,256]{1,0:T(8,128)S(1)}, u32[]{:S(2)}, u32[]{:S(2)}) collective-permute-start(f32[40,256]{1,0:T(8,128)S(1)} %get-tuple-element.69), channel_id=1, source_target_pairs={{4,0},{0,4},{5,1},{1,5},{6,2},{2,6},{7,3},{3,7},{12,8},{8,12},{13,... | collective-permute-start | bytes 122888 | tf_op jit(solution)/shard_map/ppermute | solution.py:185
  38.1 4.3 %collective-permute-start.13 = (f32[40,256]{1,0:T(8,128)S(1)}, f32[40,256]{1,0:T(8,128)S(1)}, u32[]{:S(2)}, u32[]{:S(2)}) collective-permute-start(f32[40,256]{1,0:T(8,128)S(1)} %get-tuple-element.69), channel_id=1, source_target_pairs={{4,3},{0,4},{5,2},{1,5},{6,1},{2,6},{7,0},{3,7},{12,11},{8,12},{13... | collective-permute-start | bytes 122888 | tf_op jit(solution)/shard_map/ppermute | solution.py:185
  54.1 5.7 %collective-permute-start.18 = (f32[40,256]{1,0:T(8,128)S(1)}, f32[40,256]{1,0:T(8,128)S(1)}, u32[]{:S(2)}, u32[]{:S(2)}) collective-permute-start(f32[40,256]{1,0:T(8,128)S(1)} %get-tuple-element.77), channel_id=1, source_target_pairs={{4,0},{0,4},{5,1},{1,5},{6,2},{2,6},{7,3},{3,7},{12,8},{8,12},{13,... | collective-permute-start | bytes 122888 | tf_op jit(solution)/shard_map/ppermute | solution.py:185
  58.2 4.4 %collective-permute-start.20 = (f32[40,256]{1,0:T(8,128)S(1)}, f32[40,256]{1,0:T(8,128)S(1)}, u32[]{:S(2)}, u32[]{:S(2)}) collective-permute-start(f32[40,256]{1,0:T(8,128)S(1)} %get-tuple-element.77), channel_id=1, source_target_pairs={{4,2},{0,4},{5,3},{1,5},{6,0},{2,6},{7,1},{3,7},{12,10},{8,12},{13... | collective-permute-start | bytes 122888 | tf_op jit(solution)/shard_map/ppermute | solution.py:185
  59.8 4.3 %collective-permute-start.21 = (f32[40,256]{1,0:T(8,128)S(1)}, f32[40,256]{1,0:T(8,128)S(1)}, u32[]{:S(2)}, u32[]{:S(2)}) collective-permute-start(f32[40,256]{1,0:T(8,128)S(1)} %get-tuple-element.77), channel_id=1, source_target_pairs={{4,3},{0,4},{5,2},{1,5},{6,1},{2,6},{7,0},{3,7},{12,11},{8,12},{13... | collective-permute-start | bytes 122888 | tf_op jit(solution)/shard_map/ppermute | solution.py:185
  74.2 5.9 %collective-permute-start.26 = (f32[40,256]{1,0:T(8,128)S(1)}, f32[40,256]{1,0:T(8,128)S(1)}, u32[]{:S(2)}, u32[]{:S(2)}) collective-permute-start(f32[40,256]{1,0:T(8,128)S(1)} %get-tuple-element.85), channel_id=1, source_target_pairs={{4,0},{0,4},{5,1},{1,5},{6,2},{2,6},{7,3},{3,7},{12,8},{8,12},{13,... | collective-permute-start | bytes 122888 | tf_op jit(solution)/shard_map/ppermute | solution.py:185
  79.1 4.3 %collective-permute-start.29 = (f32[40,256]{1,0:T(8,128)S(1)}, f32[40,256]{1,0:T(8,128)S(1)}, u32[]{:S(2)}, u32[]{:S(2)}) collective-permute-start(f32[40,256]{1,0:T(8,128)S(1)} %get-tuple-element.85), channel_id=1, source_target_pairs={{4,3},{0,4},{5,2},{1,5},{6,1},{2,6},{7,0},{3,7},{12,11},{8,12},{13... | collective-permute-start | bytes 122888 | tf_op jit(solution)/shard_map/ppermute | solution.py:185
  94.2 6.2 %collective-permute-start.34 = (f32[40,256]{1,0:T(8,128)S(1)}, f32[40,256]{1,0:T(8,128)S(1)}, u32[]{:S(2)}, u32[]{:S(2)}) collective-permute-start(f32[40,256]{1,0:T(8,128)S(1)} %get-tuple-element.93), channel_id=1, source_target_pairs={{4,0},{0,4},{5,1},{1,5},{6,2},{2,6},{7,3},{3,7},{12,8},{8,12},{13,... | collective-permute-start | bytes 122888 | tf_op jit(solution)/shard_map/ppermute | solution.py:185
  98.8 4.4 %collective-permute-start.36 = (f32[40,256]{1,0:T(8,128)S(1)}, f32[40,256]{1,0:T(8,128)S(1)}, u32[]{:S(2)}, u32[]{:S(2)}) collective-permute-start(f32[40,256]{1,0:T(8,128)S(1)} %get-tuple-element.93), channel_id=1, source_target_pairs={{4,2},{0,4},{5,3},{1,5},{6,0},{2,6},{7,1},{3,7},{12,10},{8,12},{13... | collective-permute-start | bytes 122888 | tf_op jit(solution)/shard_map/ppermute | solution.py:185
  100.3 4.3 %collective-permute-start.37 = (f32[40,256]{1,0:T(8,128)S(1)}, f32[40,256]{1,0:T(8,128)S(1)}, u32[]{:S(2)}, u32[]{:S(2)}) collective-permute-start(f32[40,256]{1,0:T(8,128)S(1)} %get-tuple-element.93), channel_id=1, source_target_pairs={{4,3},{0,4},{5,2},{1,5},{6,1},{2,6},{7,0},{3,7},{12,11},{8,12},{13... | collective-permute-start | bytes 122888 | tf_op jit(solution)/shard_map/ppermute | solution.py:185
  115.0 5.8 %collective-permute-start.42 = (f32[40,256]{1,0:T(8,128)S(1)}, f32[40,256]{1,0:T(8,128)S(1)}, u32[]{:S(2)}, u32[]{:S(2)}) collective-permute-start(f32[40,256]{1,0:T(8,128)S(1)} %get-tuple-element.101), channel_id=1, source_target_pairs={{4,0},{0,4},{5,1},{1,5},{6,2},{2,6},{7,3},{3,7},{12,8},{8,12},{13,... | collective-permute-start | bytes 122888 | tf_op jit(solution)/shard_map/ppermute | solution.py:185
  119.7 4.3 %collective-permute-start.45 = (f32[40,256]{1,0:T(8,128)S(1)}, f32[40,256]{1,0:T(8,128)S(1)}, u32[]{:S(2)}, u32[]{:S(2)}) collective-permute-start(f32[40,256]{1,0:T(8,128)S(1)} %get-tuple-element.101), channel_id=1, source_target_pairs={{4,3},{0,4},{5,2},{1,5},{6,1},{2,6},{7,0},{3,7},{12,11},{8,12},{13... | collective-permute-start | bytes 122888 | tf_op jit(solution)/shard_map/ppermute | solution.py:185
  134.9 6.1 %collective-permute-start.50 = (f32[40,256]{1,0:T(8,128)S(1)}, f32[40,256]{1,0:T(8,128)S(1)}, u32[]{:S(2)}, u32[]{:S(2)}) collective-permute-start(f32[40,256]{1,0:T(8,128)S(1)} %get-tuple-element.109), channel_id=1, source_target_pairs={{4,0},{0,4},{5,1},{1,5},{6,2},{2,6},{7,3},{3,7},{12,8},{8,12},{13,... | collective-permute-start | bytes 122888 | tf_op jit(solution)/shard_map/ppermute | solution.py:185
  139.4 4.4 %collective-permute-start.52 = (f32[40,256]{1,0:T(8,128)S(1)}, f32[40,256]{1,0:T(8,128)S(1)}, u32[]{:S(2)}, u32[]{:S(2)}) collective-permute-start(f32[40,256]{1,0:T(8,128)S(1)} %get-tuple-element.109), channel_id=1, source_target_pairs={{4,2},{0,4},{5,3},{1,5},{6,0},{2,6},{7,1},{3,7},{12,10},{8,12},{13... | collective-permute-start | bytes 122888 | tf_op jit(solution)/shard_map/ppermute | solution.py:185
  141.0 4.3 %collective-permute-start.53 = (f32[40,256]{1,0:T(8,128)S(1)}, f32[40,256]{1,0:T(8,128)S(1)}, u32[]{:S(2)}, u32[]{:S(2)}) collective-permute-start(f32[40,256]{1,0:T(8,128)S(1)} %get-tuple-element.109), channel_id=1, source_target_pairs={{4,3},{0,4},{5,2},{1,5},{6,1},{2,6},{7,0},{3,7},{12,11},{8,12},{13... | collective-permute-start | bytes 122888 | tf_op jit(solution)/shard_map/ppermute | solution.py:185
  155.8 5.7 %collective-permute-start.58 = (f32[40,256]{1,0:T(8,128)S(1)}, f32[40,256]{1,0:T(8,128)S(1)}, u32[]{:S(2)}, u32[]{:S(2)}) collective-permute-start(f32[40,256]{1,0:T(8,128)S(1)} %get-tuple-element.117), channel_id=1, source_target_pairs={{4,0},{0,4},{5,1},{1,5},{6,2},{2,6},{7,3},{3,7},{12,8},{8,12},{13,... | collective-permute-start | bytes 122888 | tf_op jit(solution)/shard_map/ppermute | solution.py:185
  160.4 4.3 %collective-permute-start.61 = (f32[40,256]{1,0:T(8,128)S(1)}, f32[40,256]{1,0:T(8,128)S(1)}, u32[]{:S(2)}, u32[]{:S(2)}) collective-permute-start(f32[40,256]{1,0:T(8,128)S(1)} %get-tuple-element.117), channel_id=1, source_target_pairs={{4,3},{0,4},{5,2},{1,5},{6,1},{2,6},{7,0},{3,7},{12,11},{8,12},{13... | collective-permute-start | bytes 122888 | tf_op jit(solution)/shard_map/ppermute | solution.py:185
  176.4 6.0 %collective-permute-start.66 = (f32[40,256]{1,0:T(8,128)S(1)}, f32[40,256]{1,0:T(8,128)S(1)}, u32[]{:S(2)}, u32[]{:S(2)}) collective-permute-start(f32[40,256]{1,0:T(8,128)S(1)} %get-tuple-element.125), channel_id=1, source_target_pairs={{4,0},{0,4},{5,1},{1,5},{6,2},{2,6},{7,3},{3,7},{12,8},{8,12},{13,... | collective-permute-start | bytes 122888 | tf_op jit(solution)/shard_map/ppermute | solution.py:185
  180.7 4.4 %collective-permute-start.68 = (f32[40,256]{1,0:T(8,128)S(1)}, f32[40,256]{1,0:T(8,128)S(1)}, u32[]{:S(2)}, u32[]{:S(2)}) collective-permute-start(f32[40,256]{1,0:T(8,128)S(1)} %get-tuple-element.125), channel_id=1, source_target_pairs={{4,2},{0,4},{5,3},{1,5},{6,0},{2,6},{7,1},{3,7},{12,10},{8,12},{13... | collective-permute-start | bytes 122888 | tf_op jit(solution)/shard_map/ppermute | solution.py:185
  182.3 4.3 %collective-permute-start.69 = (f32[40,256]{1,0:T(8,128)S(1)}, f32[40,256]{1,0:T(8,128)S(1)}, u32[]{:S(2)}, u32[]{:S(2)}) collective-permute-start(f32[40,256]{1,0:T(8,128)S(1)} %get-tuple-element.125), channel_id=1, source_target_pairs={{4,3},{0,4},{5,2},{1,5},{6,1},{2,6},{7,0},{3,7},{12,11},{8,12},{13... | collective-permute-start | bytes 122888 | tf_op jit(solution)/shard_map/ppermute | solution.py:185
  (57 other events, 193.2 us)

commit v2 on v1

v2 whole, which is shorter than its diff:
```python
import functools

import jax
import jax.numpy as jnp
from jax import lax
from jax.experimental import pallas as pl
from jax.experimental.pallas import tpu as pltpu
from jax.sharding import PartitionSpec as P

ITERS = 8
STEP_PRIMAL = 0.5
STEP_DUAL = 0.5
PAD = 8

F32 = jnp.float32
BF16 = jnp.bfloat16


def is_dual_core():
    return lax.axis_index("row") % 2 == 0


def assemble(ref, parts, first, rows, stride, me):
    for j in range(len(parts)):
        piece = parts[0]
        for o in range(1, len(parts)):
            piece = jnp.where(me == (j ^ o), parts[o], piece)
        ref[pl.ds(first + j * stride, rows), :] = piece


def by_offset(refs, order):
    return [refs[order.index(o)] for o in range(len(order))]


def total_of(refs, rows):
    level = [ref[pl.ds(0, rows), :] for ref in refs]
    while len(level) > 1:
        level = [level[i] + level[i + 1] for i in range(0, len(level), 2)]
    return level[0]


def z_order(n):
    return [3, 1, 2, 0] if n == 4 else list(range(n))


def col_order(n):
    return [3, 1, 2, 0] if n == 4 else list(range(n))


def update_dual(iteration, msgs, dual_ref, hist_ref, dual_out, hist_out):
    rows = dual_out.shape[0]
    total = total_of(msgs, rows + PAD)
    dual = dual_ref[...]
    dual_next = jnp.maximum(dual - STEP_DUAL * total[:rows], 0.0)
    step = dual_next - dual
    dual_out[...] = dual_next
    hist_out[...] = hist_ref[...]
    hist_out[pl.ds(iteration - 1, 1), :] = total[rows : rows + 1]
    return dual_next, jnp.sum(step * step, axis=0, keepdims=True)


def dual_body(iteration, n_msgs, slots, *refs):
    msgs = by_offset(refs[:n_msgs], col_order(n_msgs))
    (dual_ref, hist_ref, cost_ref, one_ref, extra_ref, *blk_refs) = refs[n_msgs : n_msgs + 7]
    (out_ref, dual_out, hist_out, prod_ref) = refs[n_msgs + 7 :]
    rows, width = dual_out.shape
    blocks = cost_ref.shape[0]

    @pl.when(is_dual_core())
    def _():
        if iteration == 0:
            each = rows // (2 * n_msgs)
            me = lax.axis_index("col")
            for slab in range(2):
                parts = [m[pl.ds(slab * each, each), :] for m in msgs]
                assemble(dual_out, parts, slab * (rows // 2), each, each, me)
            dual_next = dual_out[...]
            norm = jnp.zeros((1, width), F32)
            hist_out[...] = jnp.zeros_like(hist_out)
            out_ref[pl.ds(blocks + PAD, extra_ref.shape[0]), :] = extra_ref[...]
        else:
            dual_next, norm = update_dual(iteration, msgs, dual_ref, hist_ref, dual_out, hist_out)
        half = dual_next.astype(BF16)
        slab_rows = rows // 2
        for r in range(rows):
            for s in range(slots):
                at = (r // slab_rows * slots + s) * slab_rows + r % slab_rows
                prod_ref[pl.ds(at, 1), :] = jnp.dot(
                    half[r : r + 1], blk_refs[r // slab_rows][r % slab_rows * slots + s], preferred_element_type=F32
                )
        prod = prod_ref[...]
        high = prod.astype(BF16)
        rest = prod - high.astype(F32)
        mid = rest.astype(BF16)
        low = (rest - mid.astype(F32)).astype(BF16)
        stacked = jnp.concatenate([high, mid, low], axis=0)
        grad = jnp.dot(one_ref[...], stacked, preferred_element_type=F32)
        out_ref[pl.ds(0, blocks), :] = grad - cost_ref[...]
        out_ref[pl.ds(blocks, PAD), :] = jnp.concatenate(
            [norm, jnp.zeros((PAD - 1, width), F32)], axis=0
        )


def take(ref, index, count, first, rows, stride):
    piece = ref[pl.ds(first, rows), :]
    for j in range(1, count):
        piece = jnp.where(index == j, ref[pl.ds(first + j * stride, rows), :], piece)
    return piece


def last_body(iterations, n_msgs, d_rows, p_rows, n_z, *refs):
    msgs = by_offset(refs[:n_msgs], col_order(n_msgs))
    (dual_ref, hist_ref, primal_ref) = refs[n_msgs : n_msgs + 3]
    (out_ref, dual_out, away_ref) = refs[n_msgs + 3 :]
    half = dual_out.shape[0] // 2
    dual_core = is_dual_core()

    @pl.when(dual_core)
    def _():
        hist_out = out_ref.at[pl.ds(PAD, hist_ref.shape[0])]
        _, norm = update_dual(iterations, msgs, dual_ref, hist_ref, dual_out, hist_out)
        out_ref[pl.ds(0, PAD), :] = jnp.concatenate(
            [norm, jnp.zeros((PAD - 1, norm.shape[1]), F32)], axis=0
        )
        away_ref[pl.ds(0, d_rows), :] = take(
            dual_out, lax.axis_index("col"), n_msgs, half, d_rows, d_rows
        )

    @pl.when(jnp.logical_not(dual_core))
    def _():
        away_ref[pl.ds(0, p_rows), :] = take(
            primal_ref, lax.axis_index("row") // 2, n_z, 0, p_rows, 2 * p_rows
        )


def finish_body(iterations, n_msgs, n_col, p_total, d_total, *refs):
    msgs = by_offset(refs[:n_msgs], z_order(n_msgs))
    (hist_ref, dual_ref, primal_ref, back_ref) = refs[n_msgs : n_msgs + 4]
    (primal_out, dual_out, norm_out, keep_ref) = refs[n_msgs + 4 :]
    width = dual_ref.shape[1]
    d_rows, p_rows = dual_out.shape[0] // width, primal_out.shape[0] // width
    dual_core = is_dual_core()

    def give(out_ref, rows):
        for r in range(rows.shape[0]):
            out_ref[pl.ds(r * width, width)] = rows[r]

    @pl.when(dual_core)
    def _():
        give(dual_out, take(dual_ref, lax.axis_index("col"), n_col, 0, d_rows, d_rows))
        give(primal_out, back_ref[pl.ds(0, p_rows), :])

    @pl.when(jnp.logical_not(dual_core))
    def _():
        give(dual_out, back_ref[pl.ds(0, d_rows), :])
        give(
            primal_out,
            take(primal_ref, lax.axis_index("row") // 2, n_msgs, p_rows, p_rows, 2 * p_rows),
        )
        last = total_of(msgs, 1)
        keep_ref[...] = hist_ref[...]
        keep_ref[pl.ds(iterations - 1, 1), :] = last
        primal_sq = jnp.sum(msgs[0][pl.ds(PAD, hist_ref.shape[0]), :], axis=1, keepdims=True)
        dual_sq = jnp.sum(keep_ref[...], axis=1, keepdims=True)
        lane = lax.broadcasted_iota(jnp.int32, norm_out.shape, 1)
        norm_out[...] = jnp.sqrt(
            jnp.where(lane == 0, primal_sq * (1.0 / p_total), dual_sq * (1.0 / d_total))
        )


def pack_body(n, *refs):
    (sources, out_ref, held, sem) = (refs[:n], refs[n], refs[n + 1 : 2 * n + 1], refs[2 * n + 1])
    copies = [
        pltpu.make_async_copy(source, ref, sem.at[i])
        for i, (source, ref) in enumerate(zip(sources, held, strict=True))
    ]
    for copy in copies:
        copy.start()
    for copy in copies:
        copy.wait()
    (cols_ref, *vectors) = held
    width = out_ref.shape[1]
    at = 0
    for ref in vectors:
        for i in range(ref.shape[0] // width):
            out_ref[at, :] = ref[pl.ds(i * width, width)]
            at += 1
    out_ref[pl.ds(at, cols_ref.shape[0]), pl.ds(0, cols_ref.shape[1])] = cols_ref[...].astype(F32)


def pack_call(out, *arrays):
    n = len(arrays)
    return pl.pallas_call(
        functools.partial(pack_body, n),
        out_shape=out,
        in_specs=[pl.BlockSpec(memory_space=pltpu.HBM)] * n,
        out_specs=pl.BlockSpec(memory_space=pltpu.VMEM),
        scratch_shapes=[pltpu.VMEM(a.shape, a.dtype) for a in arrays]
        + [pltpu.SemaphoreType.DMA((n,))],
        compiler_params=pltpu.CompilerParams(vmem_limit_bytes=4 * 2**20),
    )(*arrays)


def setup_body(d_rows, p_rows, slab_rows, slots, n_z, n_col, *refs):
    (own_ref, other_ref, dual_out, extra_out, cost_out, right_out, one_out, pick_out) = refs
    dual_core = is_dual_core()
    first = jnp.where(dual_core, own_ref[...], other_ref[...])
    second = jnp.where(dual_core, other_ref[...], own_ref[...])
    z, col = lax.axis_index("row") // 2, lax.axis_index("col")
    at = 0
    for slab, part in enumerate((first, second)):
        dual_out[pl.ds(slab * d_rows, d_rows), :] = part[:d_rows]
    at += d_rows
    for slab, part in enumerate((first, second)):
        piece = part[at : at + d_rows]
        for j in range(n_col):
            right_out[pl.ds(slab * slab_rows + j * d_rows, d_rows), :] = jnp.where(
                col == j, piece, 0.0
            )
    at += d_rows
    for slab, part in enumerate((first, second)):
        piece = part[at : at + p_rows]
        for j in range(n_z):
            cost_out[pl.ds((2 * j + slab) * p_rows, p_rows), :] = jnp.where(z == j, piece, 0.0)
    at += p_rows
    for k in range(3):
        for slab, part in enumerate((first, second)):
            extra_out[pl.ds((2 * k + slab) * p_rows, p_rows), :] = part[at : at + p_rows]
        at += p_rows
    entries, blocks = pick_out.shape
    columns = [
        part[at : at + slab_rows, s : s + 1] for part in (first, second) for s in range(slots)
    ]
    side = -(-entries // 128) * 128
    columns.append(jnp.full((side - entries, 1), -1.0, F32))
    column = jnp.concatenate(columns, axis=0)
    lanes = -(-blocks // 128) * 128
    iota = lax.broadcasted_iota(jnp.int32, (side, lanes), 1).astype(F32)
    pick = jnp.where(jnp.broadcast_to(column, (side, lanes)) == iota, 1.0, 0.0)
    pick_out[...] = pick[:entries, :blocks].astype(BF16)
    one = pick.T[:blocks, :entries]
    one_out[...] = jnp.concatenate([one] * 3, axis=1).astype(BF16)


def primal_body(iteration, n_msgs, slots, *refs):
    msgs = by_offset(refs[:n_msgs], z_order(n_msgs))
    (primal_ref, low_ref, up_ref, hist_ref, right_ref, pick_ref, *blk_refs) = refs[
        n_msgs : n_msgs + 8
    ]
    (out_ref, primal_out, low_out, up_out, hist_out) = refs[n_msgs + 8 :]
    blk_refs = blk_refs[::-1]
    blocks = primal_out.shape[0]
    rows = right_ref.shape[0]
    slab_rows = rows // 2

    @pl.when(jnp.logical_not(is_dual_core()))
    def _():
        total = total_of(msgs, blocks + PAD)
        if iteration == 0:
            each = blocks // n_msgs
            me = lax.axis_index("row") // 2
            for k, ref in enumerate((primal_out, low_out, up_out)):
                parts = [m[pl.ds(blocks + PAD + k * each, each), :] for m in msgs]
                assemble(ref, parts, 0, each, each, me)
            primal, low, up = primal_out[...], low_out[...], up_out[...]
            hist_out[...] = jnp.zeros_like(hist_out)
        else:
            primal, low, up = primal_ref[...], low_ref[...], up_ref[...]
            low_out[...] = low
            up_out[...] = up
            hist_out[...] = hist_ref[...]
            hist_out[pl.ds(iteration - 1, 1), :] = total[blocks : blocks + 1]
        primal_next = jnp.minimum(up, jnp.maximum(low, primal + STEP_PRIMAL * total[:blocks]))
        step = primal_next - primal
        norm = jnp.sum(step * step, axis=0, keepdims=True)
        primal_out[...] = primal_next
        ext = (2.0 * primal_next - primal).astype(BF16)
        picked = jnp.dot(pick_ref[...], ext, preferred_element_type=F32).astype(BF16)
        for r in range(rows):
            acc = -right_ref[pl.ds(r, 1), :]
            for s in range(slots):
                at = (r // slab_rows * slots + s) * slab_rows + r % slab_rows
                acc = acc + jnp.dot(
                    picked[at : at + 1],
                    blk_refs[r // slab_rows][r % slab_rows * slots + s],
                    preferred_element_type=F32,
                )
            out_ref[pl.ds(r, 1), :] = acc
        out_ref[pl.ds(rows, PAD), :] = jnp.concatenate(
            [norm, jnp.zeros((PAD - 1, norm.shape[1]), F32)], axis=0
        )


def weights_body(in_ref, out_ref, sem):
    copy = pltpu.make_async_copy(in_ref, out_ref, sem)
    copy.start()
    copy.wait()

    @pl.when(jnp.logical_not(is_dual_core()))
    def _():
        def step(i, carry):
            for k in range(4):
                out_ref[i * 4 + k] = out_ref[i * 4 + k].T
            return carry

        lax.fori_loop(0, in_ref.shape[0] // 4, step, 0)


def weights_call(blocks):
    return pl.pallas_call(
        weights_body,
        out_shape=jax.ShapeDtypeStruct(blocks.shape, BF16),
        in_specs=[pl.BlockSpec(memory_space=pltpu.HBM)],
        out_specs=pl.BlockSpec(memory_space=pltpu.VMEM),
        scratch_shapes=[pltpu.SemaphoreType.DMA],
        compiler_params=pltpu.CompilerParams(vmem_limit_bytes=8 * 2**20),
    )(blocks)


def local_call(body, outs, scratch, n_in):
    return pl.pallas_call(
        body,
        out_shape=outs,
        in_specs=[pl.BlockSpec(memory_space=pltpu.VMEM)] * n_in,
        out_specs=[pl.BlockSpec(memory_space=pltpu.VMEM)] * len(outs),
        scratch_shapes=scratch,
        compiler_params=pltpu.CompilerParams(vmem_limit_bytes=4 * 2**20),
    )


def per_device(
    blocks, block_cols, objective, lower_bound, upper_bound, right_side, primal_init, dual_init
):
    slab_rows, slots, width = blocks.shape[0], blocks.shape[1], blocks.shape[2]
    n_row, n_col = lax.axis_size("row"), lax.axis_size("col")
    n_z = n_row // 2
    p_rows = primal_init.shape[0] // width
    d_rows = dual_init.shape[0] // width
    col_blocks = p_rows * n_row
    rows = 2 * slab_rows
    entries = rows * slots
    is_dual = is_dual_core()

    swap_pairs = [(r, r ^ 1) for r in range(n_row)]

    def over_z(src, o):
        away = [(2 * k + src, 2 * (k ^ o) + 1 - src) for k in range(n_z)]
        return away + [(2 * k + 1 - src, 2 * k + src) for k in range(n_z)]

    def over_col(src, o):
        pairs = []
        for k in range(n_z):
            for c in range(n_col):
                pairs.append(((2 * k + src) * n_col + c, (2 * k + 1 - src) * n_col + (c ^ o)))
                pairs.append(((2 * k + 1 - src) * n_col + c, (2 * k + src) * n_col + c))
        return pairs

    def to_primal(x):
        return [lax.ppermute(x, "row", over_z(0, o)) for o in z_order(n_z)]

    def to_dual(x):
        return [lax.ppermute(x, ("row", "col"), over_col(1, o)) for o in col_order(n_col)]

    def shape(n, wide=width, dtype=F32):
        return jax.ShapeDtypeStruct((n, wide), dtype)

    mine = blocks.reshape(slab_rows * slots, width, width)
    own = pack_call(
        shape(2 * d_rows + 4 * p_rows + slab_rows),
        block_cols, dual_init, right_side, objective, primal_init, lower_bound, upper_bound,
    )
    other = lax.ppermute(own, "row", swap_pairs)
    gated, other = lax.optimization_barrier((mine, other))
    theirs = lax.ppermute(gated, "row", swap_pairs)
    dual_part, extra, cost, right, one_three, pick = local_call(
        functools.partial(setup_body, d_rows, p_rows, slab_rows, slots, n_z, n_col),
        [
            shape(2 * d_rows),
            shape(6 * p_rows),
            shape(col_blocks),
            shape(rows),
            shape(col_blocks, 3 * entries, BF16),
            shape(entries, col_blocks, BF16),
        ],
        [],
        2,
    )(own, other)
    weights = (weights_call(mine), weights_call(theirs))

    hist_rows = -(-ITERS // 8) * 8
    dual = right
    primal = low = up = cost
    primal_hist = dual_hist = jnp.zeros((hist_rows, width), F32)
    products = pltpu.VMEM((entries, width), F32)

    arrived = to_dual(dual_part)
    for iteration in range(ITERS):
        message, dual, primal_hist = local_call(
            functools.partial(dual_body, iteration, n_col, slots),
            [
                shape(col_blocks + PAD + (6 * p_rows if iteration == 0 else 0)),
                shape(rows),
                shape(hist_rows),
            ],
            [products],
            n_col + 7,
        )(*arrived, dual, primal_hist, cost, one_three, extra, *weights)
        arrived = to_primal(message)
        message, primal, low, up, dual_hist = local_call(
            functools.partial(primal_body, iteration, n_z, slots),
            [
                shape(rows + PAD),
                shape(col_blocks),
                shape(col_blocks),
                shape(col_blocks),
                shape(hist_rows),
            ],
            [],
            n_z + 8,
        )(*arrived, primal, low, up, dual_hist, right, pick, *weights)
        arrived = to_dual(message)
    message, dual, away = local_call(
        functools.partial(last_body, ITERS, n_col, d_rows, p_rows, n_z),
        [shape(PAD + hist_rows), shape(rows), shape(max(p_rows, d_rows))],
        [],
        n_col + 3,
    )(*arrived, dual, primal_hist, primal)
    back = lax.ppermute(away, "row", swap_pairs)
    arrived = to_primal(message)
    primal_out, dual_out, norms = local_call(
        functools.partial(
            finish_body,
            ITERS,
            n_z,
            n_col,
            float(primal_init.shape[0] * n_row * n_col),
            float(dual_init.shape[0] * n_row * n_col),
        ),
        [
            jax.ShapeDtypeStruct(primal_init.shape, F32),
            jax.ShapeDtypeStruct(dual_init.shape, F32),
            shape(hist_rows, 2),
        ],
        [pltpu.VMEM((hist_rows, width), F32)],
        n_z + 4,
    )(*arrived, dual_hist, dual, primal, back)
    norms = jnp.where(is_dual, lax.ppermute(norms, "row", swap_pairs), norms)[:ITERS]
    return (primal_out, dual_out, norms)


def solution(mesh):
    in_specs = (
        P("row", "col", None, None),
        P("row", "col"),
        P(("col", "row")),
        P(("col", "row")),
        P(("col", "row")),
        P(("row", "col")),
        P(("col", "row")),
        P(("row", "col")),
    )
    out_specs = (P(("col", "row")), P(("row", "col")), P())
    return jax.shard_map(
        per_device, mesh=mesh, in_specs=in_specs, out_specs=out_specs, check_vma=False
    )
```

time: 200 us -> 121 us (0.60)
  Pallas kernels: 48.8 us -> 13.1 us
  starting transfers between devices: 83.3 us -> 58.8 us
  waiting for transfers between devices: 50.9 us -> 39.9 us
  local copies, waits for them, and re-layouts: 13.1 us -> 7.74 us
    pallas_call x9 -> x14, Pallas kernels: 30.5 us -> 12.5 us  [the longest x8 10.8 us: per_device(): local_call(functools.partial(dual_body, iteration, n_col, slots), [shape(...]
    pallas_call x8, Pallas kernels: 18.3 us -> 0.64 us  [per_device(): local_call(functools.partial(primal_body, iteration, n_z, slots), [shape(...]
    ppermute x36, starting transfers between devices: 51.4 us -> 34.3 us  [to_dual(): lax.ppermute(x, ('row', 'col'), over_col(1, o))]
    ppermute x36, waiting for transfers between devices: 33.2 us -> 20.6 us  [to_dual(): lax.ppermute(x, ('row', 'col'), over_col(1, o))]
    ppermute x38, starting transfers between devices: 31.7 us -> 23.5 us  [the longest x36 21.6 us: to_primal(): return [lax.ppermute(x, 'row', over_z(0, o)) for o in z_order(n_z)]]
    reshape x8 -> x0, local copies, waits for them, and re-layouts: 4.87 us -> none  [the longest x1 0.7 us: per_device(): objective.reshape(p_rows, width)]
    unnamed x12 -> x16, local copies, waits for them, and re-layouts: 7.17 us -> 7.74 us
  transfers between devices with their start and end apart: 76 -> 76, of which waited for: 45 -> 44; matrix products, arithmetic and copies ran while one was open for 4% -> 0% of each run, Pallas kernels for 0% -> 1%
where the time goes in v2:
time: 121 us; the launch traced here: 120 us
  starting transfers between devices  58.8 us (49%)
  waiting for transfers between devices  39.9 us (33%)
  Pallas kernels  13.1 us (11%)
  local copies, waits for them, and re-layouts  7.74 us (6%)
    ppermute x36, starting transfers between devices, to_dual(): lax.ppermute(x, ('row', 'col'), over_col(1, o))  34.3 us
    ppermute x36, starting transfers between devices, to_primal(): return [lax.ppermute(x, 'row', over_z(0, o)) for o in z_order(n_z)]  21.6 us
    ppermute x36, waiting for transfers between devices, to_dual(): lax.ppermute(x, ('row', 'col'), over_col(1, o))  20.6 us
    ppermute x36, waiting for transfers between devices, to_primal(): return [lax.ppermute(x, 'row', over_z(0, o)) for o in z_order(n_z)]  16.8 us
    pallas_call x8, Pallas kernels, per_device(): local_call(functools.partial(dual_body, iteration, n_col, slots), [shape(...  10.8 us
    unnamed x16, local copies, waits for them, and re-layouts  7.74 us
  transfers between devices with their start and end apart: 76, of which 44 were waited for; matrix products, arithmetic and copies ran while one was open for 0% of the time, Pallas kernels for 1%

profile of v2, /device:TPU:0, one launch (start us, length us, event | category | flops | bytes accessed | tf_op | source)
XLA Modules:
  0.0 120.3 jit_solution(6634929612102627644)
XLA Ops:
  7.9 3.5 %collective-permute-start.2 = (f32[8,256]{1,0:T(8,128)S(1)}, f32[8,256]{1,0:T(8,128)S(1)}, u32[]{:S(2)}, u32[]{:S(2)}) collective-permute-start(f32[8,256]{1,0:T(8,128)S(1)} %get-tuple-element.80), channel_id=1, source_target_pairs={{4,1},{0,4},{5,0},{1,5},{6,3},{2,6},{7,2},{3,7},{12,9},{8,12},{13,... | collective-permute-start | bytes 24584 | tf_op jit(solution)/shard_map/ppermute | solution.py:362
  12.1 2.2 %copy-done = bf16[16,2,256,256]{3,2,1,0:T(8,128)(2,1)S(1)} copy-done((bf16[16,2,256,256]{3,2,1,0:T(8,128)(2,1)S(1)}, bf16[16,2,256,256]{3,2,1,0:T(8,128)(2,1)}, u32[]{:S(2)}) %copy-start) | copy-done | bytes 4194328
  16.3 5.0 %collective-permute-start.6 = (f32[92,256]{1,0:T(8,128)S(1)}, f32[92,256]{1,0:T(8,128)S(1)}, u32[]{:S(2)}, u32[]{:S(2)}) collective-permute-start(f32[92,256]{1,0:T(8,128)S(1)} %get-tuple-element.86), channel_id=1, source_target_pairs={{0,28},{8,20},{16,12},{24,4},{4,0},{12,8},{20,16},{28,24},{1,29},{... | collective-permute-start | bytes 282632 | tf_op jit(solution)/shard_map/ppermute | solution.py:359
  21.8 1.7 %collective-permute-done.6.refs_0_ = f32[92,256]{1,0:T(8,128)S(1)} collective-permute-done((f32[92,256]{1,0:T(8,128)S(1)}, f32[92,256]{1,0:T(8,128)S(1)}, u32[]{:S(2)}, u32[]{:S(2)}) %collective-permute-start.6) | collective-permute-done | bytes 94240 | tf_op jit(solution)/shard_map/ppermute | solution.py:359
  25.6 2.9 %collective-permute-start.10 = (f32[40,256]{1,0:T(8,128)S(1)}, f32[40,256]{1,0:T(8,128)S(1)}, u32[]{:S(2)}, u32[]{:S(2)}) collective-permute-start(f32[40,256]{1,0:T(8,128)S(1)} %get-tuple-element.88), channel_id=1, source_target_pairs={{4,3},{0,4},{5,2},{1,5},{6,1},{2,6},{7,0},{3,7},{12,11},{8,12},{13... | collective-permute-start | bytes 122888 | tf_op jit(solution)/shard_map/ppermute | solution.py:362
  30.2 1.9 %collective-permute-done.10.refs_0_ = f32[40,256]{1,0:T(8,128)S(1)} collective-permute-done((f32[40,256]{1,0:T(8,128)S(1)}, f32[40,256]{1,0:T(8,128)S(1)}, u32[]{:S(2)}, u32[]{:S(2)}) %collective-permute-start.10) | collective-permute-done | bytes 40992 | tf_op jit(solution)/shard_map/ppermute | solution.py:362
  34.2 1.8 %collective-permute-start.16 = (f32[56,256]{1,0:T(8,128)S(1)}, f32[56,256]{1,0:T(8,128)S(1)}, u32[]{:S(2)}, u32[]{:S(2)}) collective-permute-start(f32[56,256]{1,0:T(8,128)S(1)} %get-tuple-element.91), channel_id=1, source_target_pairs={{0,20},{8,28},{16,4},{24,12},{4,0},{12,8},{20,16},{28,24},{1,21},{... | collective-permute-start | bytes 172040 | tf_op jit(solution)/shard_map/ppermute | solution.py:359
  37.8 2.8 %collective-permute-start.18 = (f32[40,256]{1,0:T(8,128)S(1)}, f32[40,256]{1,0:T(8,128)S(1)}, u32[]{:S(2)}, u32[]{:S(2)}) collective-permute-start(f32[40,256]{1,0:T(8,128)S(1)} %get-tuple-element.96), channel_id=1, source_target_pairs={{4,3},{0,4},{5,2},{1,5},{6,1},{2,6},{7,0},{3,7},{12,11},{8,12},{13... | collective-permute-start | bytes 122888 | tf_op jit(solution)/shard_map/ppermute | solution.py:362
  41.5 1.9 %collective-permute-done.18.refs_0_ = f32[40,256]{1,0:T(8,128)S(1)} collective-permute-done((f32[40,256]{1,0:T(8,128)S(1)}, f32[40,256]{1,0:T(8,128)S(1)}, u32[]{:S(2)}, u32[]{:S(2)}) %collective-permute-start.18) | collective-permute-done | bytes 40992 | tf_op jit(solution)/shard_map/ppermute | solution.py:362
  49.2 2.6 %collective-permute-start.26 = (f32[40,256]{1,0:T(8,128)S(1)}, f32[40,256]{1,0:T(8,128)S(1)}, u32[]{:S(2)}, u32[]{:S(2)}) collective-permute-start(f32[40,256]{1,0:T(8,128)S(1)} %get-tuple-element.104), channel_id=1, source_target_pairs={{4,3},{0,4},{5,2},{1,5},{6,1},{2,6},{7,0},{3,7},{12,11},{8,12},{13... | collective-permute-start | bytes 122888 | tf_op jit(solution)/shard_map/ppermute | solution.py:362
  52.8 1.9 %collective-permute-done.26.refs_0_ = f32[40,256]{1,0:T(8,128)S(1)} collective-permute-done((f32[40,256]{1,0:T(8,128)S(1)}, f32[40,256]{1,0:T(8,128)S(1)}, u32[]{:S(2)}, u32[]{:S(2)}) %collective-permute-start.26) | collective-permute-done | bytes 40992 | tf_op jit(solution)/shard_map/ppermute | solution.py:362
  60.6 2.7 %collective-permute-start.34 = (f32[40,256]{1,0:T(8,128)S(1)}, f32[40,256]{1,0:T(8,128)S(1)}, u32[]{:S(2)}, u32[]{:S(2)}) collective-permute-start(f32[40,256]{1,0:T(8,128)S(1)} %get-tuple-element.112), channel_id=1, source_target_pairs={{4,3},{0,4},{5,2},{1,5},{6,1},{2,6},{7,0},{3,7},{12,11},{8,12},{13... | collective-permute-start | bytes 122888 | tf_op jit(solution)/shard_map/ppermute | solution.py:362
  64.3 1.9 %collective-permute-done.34.refs_0_ = f32[40,256]{1,0:T(8,128)S(1)} collective-permute-done((f32[40,256]{1,0:T(8,128)S(1)}, f32[40,256]{1,0:T(8,128)S(1)}, u32[]{:S(2)}, u32[]{:S(2)}) %collective-permute-start.34) | collective-permute-done | bytes 40992 | tf_op jit(solution)/shard_map/ppermute | solution.py:362
  68.2 1.6 %collective-permute-start.39 = (f32[56,256]{1,0:T(8,128)S(1)}, f32[56,256]{1,0:T(8,128)S(1)}, u32[]{:S(2)}, u32[]{:S(2)}) collective-permute-start(f32[56,256]{1,0:T(8,128)S(1)} %get-tuple-element.115), channel_id=1, source_target_pairs={{0,12},{8,4},{16,28},{24,20},{4,0},{12,8},{20,16},{28,24},{1,13},{... | collective-permute-start | bytes 172040 | tf_op jit(solution)/shard_map/ppermute | solution.py:359
  72.2 2.7 %collective-permute-start.42 = (f32[40,256]{1,0:T(8,128)S(1)}, f32[40,256]{1,0:T(8,128)S(1)}, u32[]{:S(2)}, u32[]{:S(2)}) collective-permute-start(f32[40,256]{1,0:T(8,128)S(1)} %get-tuple-element.120), channel_id=1, source_target_pairs={{4,3},{0,4},{5,2},{1,5},{6,1},{2,6},{7,0},{3,7},{12,11},{8,12},{13... | collective-permute-start | bytes 122888 | tf_op jit(solution)/shard_map/ppermute | solution.py:362
  75.8 1.9 %collective-permute-done.42.refs_0_ = f32[40,256]{1,0:T(8,128)S(1)} collective-permute-done((f32[40,256]{1,0:T(8,128)S(1)}, f32[40,256]{1,0:T(8,128)S(1)}, u32[]{:S(2)}, u32[]{:S(2)}) %collective-permute-start.42) | collective-permute-done | bytes 40992 | tf_op jit(solution)/shard_map/ppermute | solution.py:362
  83.6 2.6 %collective-permute-start.50 = (f32[40,256]{1,0:T(8,128)S(1)}, f32[40,256]{1,0:T(8,128)S(1)}, u32[]{:S(2)}, u32[]{:S(2)}) collective-permute-start(f32[40,256]{1,0:T(8,128)S(1)} %get-tuple-element.128), channel_id=1, source_target_pairs={{4,3},{0,4},{5,2},{1,5},{6,1},{2,6},{7,0},{3,7},{12,11},{8,12},{13... | collective-permute-start | bytes 122888 | tf_op jit(solution)/shard_map/ppermute | solution.py:362
  87.1 1.9 %collective-permute-done.50.refs_0_ = f32[40,256]{1,0:T(8,128)S(1)} collective-permute-done((f32[40,256]{1,0:T(8,128)S(1)}, f32[40,256]{1,0:T(8,128)S(1)}, u32[]{:S(2)}, u32[]{:S(2)}) %collective-permute-start.50) | collective-permute-done | bytes 40992 | tf_op jit(solution)/shard_map/ppermute | solution.py:362
  91.1 1.6 %collective-permute-start.55 = (f32[56,256]{1,0:T(8,128)S(1)}, f32[56,256]{1,0:T(8,128)S(1)}, u32[]{:S(2)}, u32[]{:S(2)}) collective-permute-start(f32[56,256]{1,0:T(8,128)S(1)} %get-tuple-element.131), channel_id=1, source_target_pairs={{0,12},{8,4},{16,28},{24,20},{4,0},{12,8},{20,16},{28,24},{1,13},{... | collective-permute-start | bytes 172040 | tf_op jit(solution)/shard_map/ppermute | solution.py:359
  95.0 2.7 %collective-permute-start.58 = (f32[40,256]{1,0:T(8,128)S(1)}, f32[40,256]{1,0:T(8,128)S(1)}, u32[]{:S(2)}, u32[]{:S(2)}) collective-permute-start(f32[40,256]{1,0:T(8,128)S(1)} %get-tuple-element.136), channel_id=1, source_target_pairs={{4,3},{0,4},{5,2},{1,5},{6,1},{2,6},{7,0},{3,7},{12,11},{8,12},{13... | collective-permute-start | bytes 122888 | tf_op jit(solution)/shard_map/ppermute | solution.py:362
  98.7 1.9 %collective-permute-done.58.refs_0_ = f32[40,256]{1,0:T(8,128)S(1)} collective-permute-done((f32[40,256]{1,0:T(8,128)S(1)}, f32[40,256]{1,0:T(8,128)S(1)}, u32[]{:S(2)}, u32[]{:S(2)}) %collective-permute-start.58) | collective-permute-done | bytes 40992 | tf_op jit(solution)/shard_map/ppermute | solution.py:362
  107.0 2.7 %collective-permute-start.66 = (f32[40,256]{1,0:T(8,128)S(1)}, f32[40,256]{1,0:T(8,128)S(1)}, u32[]{:S(2)}, u32[]{:S(2)}) collective-permute-start(f32[40,256]{1,0:T(8,128)S(1)} %get-tuple-element.144), channel_id=1, source_target_pairs={{4,3},{0,4},{5,2},{1,5},{6,1},{2,6},{7,0},{3,7},{12,11},{8,12},{13... | collective-permute-start | bytes 122888 | tf_op jit(solution)/shard_map/ppermute | solution.py:362
  110.6 1.9 %collective-permute-done.66.refs_0_ = f32[40,256]{1,0:T(8,128)S(1)} collective-permute-done((f32[40,256]{1,0:T(8,128)S(1)}, f32[40,256]{1,0:T(8,128)S(1)}, u32[]{:S(2)}, u32[]{:S(2)}) %collective-permute-start.66) | collective-permute-done | bytes 40992 | tf_op jit(solution)/shard_map/ppermute | solution.py:362
  117.2 1.6 %collective-permute-start.75 = (f32[8,2]{1,0:T(8,128)S(1)}, f32[8,2]{1,0:T(8,128)S(1)}, u32[]{:S(2)}, u32[]{:S(2)}) collective-permute-start(f32[8,2]{1,0:T(8,128)S(1)} %get-tuple-element.154), channel_id=1, source_target_pairs={{0,4},{4,0},{8,12},{12,8},{16,20},{20,16},{24,28},{28,24},{1,5},{5... | collective-permute-start | bytes 200 | tf_op jit(solution)/shard_map/ppermute | solution.py:447
  (168 shorter events, 63.6 us)
Async XLA Ops:
  7.1 7.5 %collective-permute-start.5 = (bf16[32,256,256]{2,1,0:T(8,128)(2,1)}, bf16[32,256,256]{2,1,0:T(8,128)(2,1)S(1)}, u32[]{:S(2)}, u32[]{:S(2)}) collective-permute-start(bf16[32,256,256]{2,1,0:T(8,128)(2,1)} %bitcast.1), channel_id=1, source_target_pairs={{0,4},{4,0},{8,12},{12,8},{16,20},{20,16},{24,28},{28,24},{1,5},{5... | collective-permute-start | bytes 12582920 | tf_op jit(solution)/shard_map/ppermute | solution.py:374
  7.7 7.2 %collective-permute-start.1 = (f32[8,256]{1,0:T(8,128)S(1)}, f32[8,256]{1,0:T(8,128)S(1)}, u32[]{:S(2)}, u32[]{:S(2)}) collective-permute-start(f32[8,256]{1,0:T(8,128)S(1)} %get-tuple-element.80), channel_id=1, source_target_pairs={{4,3},{0,4},{5,2},{1,5},{6,1},{2,6},{7,0},{3,7},{12,11},{8,12},{13... | collective-permute-start | bytes 24584 | tf_op jit(solution)/shard_map/ppermute | solution.py:362
  7.9 7.0 %collective-permute-start.2 = (f32[8,256]{1,0:T(8,128)S(1)}, f32[8,256]{1,0:T(8,128)S(1)}, u32[]{:S(2)}, u32[]{:S(2)}) collective-permute-start(f32[8,256]{1,0:T(8,128)S(1)} %get-tuple-element.80), channel_id=1, source_target_pairs={{4,1},{0,4},{5,0},{1,5},{6,3},{2,6},{7,2},{3,7},{12,9},{8,12},{13,... | collective-permute-start | bytes 24584 | tf_op jit(solution)/shard_map/ppermute | solution.py:362
  11.5 3.5 %collective-permute-start.3 = (f32[8,256]{1,0:T(8,128)S(1)}, f32[8,256]{1,0:T(8,128)S(1)}, u32[]{:S(2)}, u32[]{:S(2)}) collective-permute-start(f32[8,256]{1,0:T(8,128)S(1)} %get-tuple-element.80), channel_id=1, source_target_pairs={{4,2},{0,4},{5,3},{1,5},{6,0},{2,6},{7,1},{3,7},{12,10},{8,12},{13... | collective-permute-start | bytes 24584 | tf_op jit(solution)/shard_map/ppermute | solution.py:362
  11.5 3.5 %collective-permute-start.4 = (f32[8,256]{1,0:T(8,128)S(1)}, f32[8,256]{1,0:T(8,128)S(1)}, u32[]{:S(2)}, u32[]{:S(2)}) collective-permute-start(f32[8,256]{1,0:T(8,128)S(1)} %get-tuple-element.80), channel_id=1, source_target_pairs={{4,0},{0,4},{5,1},{1,5},{6,2},{2,6},{7,3},{3,7},{12,8},{8,12},{13,... | collective-permute-start | bytes 24584 | tf_op jit(solution)/shard_map/ppermute | solution.py:362
  16.3 7.2 %collective-permute-start.6 = (f32[92,256]{1,0:T(8,128)S(1)}, f32[92,256]{1,0:T(8,128)S(1)}, u32[]{:S(2)}, u32[]{:S(2)}) collective-permute-start(f32[92,256]{1,0:T(8,128)S(1)} %get-tuple-element.86), channel_id=1, source_target_pairs={{0,28},{8,20},{16,12},{24,4},{4,0},{12,8},{20,16},{28,24},{1,29},{... | collective-permute-start | bytes 282632 | tf_op jit(solution)/shard_map/ppermute | solution.py:359
  21.3 4.3 %collective-permute-start.8 = (f32[92,256]{1,0:T(8,128)S(1)}, f32[92,256]{1,0:T(8,128)S(1)}, u32[]{:S(2)}, u32[]{:S(2)}) collective-permute-start(f32[92,256]{1,0:T(8,128)S(1)} %get-tuple-element.86), channel_id=1, source_target_pairs={{0,20},{8,28},{16,4},{24,12},{4,0},{12,8},{20,16},{28,24},{1,21},{... | collective-permute-start | bytes 282632 | tf_op jit(solution)/shard_map/ppermute | solution.py:359
  21.3 4.3 %collective-permute-start.9 = (f32[92,256]{1,0:T(8,128)S(1)}, f32[92,256]{1,0:T(8,128)S(1)}, u32[]{:S(2)}, u32[]{:S(2)}) collective-permute-start(f32[92,256]{1,0:T(8,128)S(1)} %get-tuple-element.86), channel_id=1, source_target_pairs={{0,4},{8,12},{16,20},{24,28},{4,0},{12,8},{20,16},{28,24},{1,5},{9... | collective-permute-start | bytes 282632 | tf_op jit(solution)/shard_map/ppermute | solution.py:359
  25.6 6.5 %collective-permute-start.10 = (f32[40,256]{1,0:T(8,128)S(1)}, f32[40,256]{1,0:T(8,128)S(1)}, u32[]{:S(2)}, u32[]{:S(2)}) collective-permute-start(f32[40,256]{1,0:T(8,128)S(1)} %get-tuple-element.88), channel_id=1, source_target_pairs={{4,3},{0,4},{5,2},{1,5},{6,1},{2,6},{7,0},{3,7},{12,11},{8,12},{13... | collective-permute-start | bytes 122888 | tf_op jit(solution)/shard_map/ppermute | solution.py:362
  28.5 3.6 %collective-permute-start.11 = (f32[40,256]{1,0:T(8,128)S(1)}, f32[40,256]{1,0:T(8,128)S(1)}, u32[]{:S(2)}, u32[]{:S(2)}) collective-permute-start(f32[40,256]{1,0:T(8,128)S(1)} %get-tuple-element.88), channel_id=1, source_target_pairs={{4,1},{0,4},{5,0},{1,5},{6,3},{2,6},{7,2},{3,7},{12,9},{8,12},{13,... | collective-permute-start | bytes 122888 | tf_op jit(solution)/shard_map/ppermute | solution.py:362
  28.6 4.2 %collective-permute-start.12 = (f32[40,256]{1,0:T(8,128)S(1)}, f32[40,256]{1,0:T(8,128)S(1)}, u32[]{:S(2)}, u32[]{:S(2)}) collective-permute-start(f32[40,256]{1,0:T(8,128)S(1)} %get-tuple-element.88), channel_id=1, source_target_pairs={{4,2},{0,4},{5,3},{1,5},{6,0},{2,6},{7,1},{3,7},{12,10},{8,12},{13... | collective-permute-start | bytes 122888 | tf_op jit(solution)/shard_map/ppermute | solution.py:362
  34.2 3.6 %collective-permute-start.16 = (f32[56,256]{1,0:T(8,128)S(1)}, f32[56,256]{1,0:T(8,128)S(1)}, u32[]{:S(2)}, u32[]{:S(2)}) collective-permute-start(f32[56,256]{1,0:T(8,128)S(1)} %get-tuple-element.91), channel_id=1, source_target_pairs={{0,20},{8,28},{16,4},{24,12},{4,0},{12,8},{20,16},{28,24},{1,21},{... | collective-permute-start | bytes 172040 | tf_op jit(solution)/shard_map/ppermute | solution.py:359
  37.8 5.6 %collective-permute-start.18 = (f32[40,256]{1,0:T(8,128)S(1)}, f32[40,256]{1,0:T(8,128)S(1)}, u32[]{:S(2)}, u32[]{:S(2)}) collective-permute-start(f32[40,256]{1,0:T(8,128)S(1)} %get-tuple-element.96), channel_id=1, source_target_pairs={{4,3},{0,4},{5,2},{1,5},{6,1},{2,6},{7,0},{3,7},{12,11},{8,12},{13... | collective-permute-start | bytes 122888 | tf_op jit(solution)/shard_map/ppermute | solution.py:362
  40.6 3.4 %collective-permute-start.19 = (f32[40,256]{1,0:T(8,128)S(1)}, f32[40,256]{1,0:T(8,128)S(1)}, u32[]{:S(2)}, u32[]{:S(2)}) collective-permute-start(f32[40,256]{1,0:T(8,128)S(1)} %get-tuple-element.96), channel_id=1, source_target_pairs={{4,1},{0,4},{5,0},{1,5},{6,3},{2,6},{7,2},{3,7},{12,9},{8,12},{13,... | collective-permute-start | bytes 122888 | tf_op jit(solution)/shard_map/ppermute | solution.py:362
  49.2 5.4 %collective-permute-start.26 = (f32[40,256]{1,0:T(8,128)S(1)}, f32[40,256]{1,0:T(8,128)S(1)}, u32[]{:S(2)}, u32[]{:S(2)}) collective-permute-start(f32[40,256]{1,0:T(8,128)S(1)} %get-tuple-element.104), channel_id=1, source_target_pairs={{4,3},{0,4},{5,2},{1,5},{6,1},{2,6},{7,0},{3,7},{12,11},{8,12},{13... | collective-permute-start | bytes 122888 | tf_op jit(solution)/shard_map/ppermute | solution.py:362
  60.6 5.6 %collective-permute-start.34 = (f32[40,256]{1,0:T(8,128)S(1)}, f32[40,256]{1,0:T(8,128)S(1)}, u32[]{:S(2)}, u32[]{:S(2)}) collective-permute-start(f32[40,256]{1,0:T(8,128)S(1)} %get-tuple-element.112), channel_id=1, source_target_pairs={{4,3},{0,4},{5,2},{1,5},{6,1},{2,6},{7,0},{3,7},{12,11},{8,12},{13... | collective-permute-start | bytes 122888 | tf_op jit(solution)/shard_map/ppermute | solution.py:362
  68.2 3.5 %collective-permute-start.39 = (f32[56,256]{1,0:T(8,128)S(1)}, f32[56,256]{1,0:T(8,128)S(1)}, u32[]{:S(2)}, u32[]{:S(2)}) collective-permute-start(f32[56,256]{1,0:T(8,128)S(1)} %get-tuple-element.115), channel_id=1, source_target_pairs={{0,12},{8,4},{16,28},{24,20},{4,0},{12,8},{20,16},{28,24},{1,13},{... | collective-permute-start | bytes 172040 | tf_op jit(solution)/shard_map/ppermute | solution.py:359
  72.2 5.5 %collective-permute-start.42 = (f32[40,256]{1,0:T(8,128)S(1)}, f32[40,256]{1,0:T(8,128)S(1)}, u32[]{:S(2)}, u32[]{:S(2)}) collective-permute-start(f32[40,256]{1,0:T(8,128)S(1)} %get-tuple-element.120), channel_id=1, source_target_pairs={{4,3},{0,4},{5,2},{1,5},{6,1},{2,6},{7,0},{3,7},{12,11},{8,12},{13... | collective-permute-start | bytes 122888 | tf_op jit(solution)/shard_map/ppermute | solution.py:362
  83.6 5.4 %collective-permute-start.50 = (f32[40,256]{1,0:T(8,128)S(1)}, f32[40,256]{1,0:T(8,128)S(1)}, u32[]{:S(2)}, u32[]{:S(2)}) collective-permute-start(f32[40,256]{1,0:T(8,128)S(1)} %get-tuple-element.128), channel_id=1, source_target_pairs={{4,3},{0,4},{5,2},{1,5},{6,1},{2,6},{7,0},{3,7},{12,11},{8,12},{13... | collective-permute-start | bytes 122888 | tf_op jit(solution)/shard_map/ppermute | solution.py:362
  86.2 3.4 %collective-permute-start.51 = (f32[40,256]{1,0:T(8,128)S(1)}, f32[40,256]{1,0:T(8,128)S(1)}, u32[]{:S(2)}, u32[]{:S(2)}) collective-permute-start(f32[40,256]{1,0:T(8,128)S(1)} %get-tuple-element.128), channel_id=1, source_target_pairs={{4,1},{0,4},{5,0},{1,5},{6,3},{2,6},{7,2},{3,7},{12,9},{8,12},{13,... | collective-permute-start | bytes 122888 | tf_op jit(solution)/shard_map/ppermute | solution.py:362
  95.0 5.5 %collective-permute-start.58 = (f32[40,256]{1,0:T(8,128)S(1)}, f32[40,256]{1,0:T(8,128)S(1)}, u32[]{:S(2)}, u32[]{:S(2)}) collective-permute-start(f32[40,256]{1,0:T(8,128)S(1)} %get-tuple-element.136), channel_id=1, source_target_pairs={{4,3},{0,4},{5,2},{1,5},{6,1},{2,6},{7,0},{3,7},{12,11},{8,12},{13... | collective-permute-start | bytes 122888 | tf_op jit(solution)/shard_map/ppermute | solution.py:362
  97.8 3.4 %collective-permute-start.59 = (f32[40,256]{1,0:T(8,128)S(1)}, f32[40,256]{1,0:T(8,128)S(1)}, u32[]{:S(2)}, u32[]{:S(2)}) collective-permute-start(f32[40,256]{1,0:T(8,128)S(1)} %get-tuple-element.136), channel_id=1, source_target_pairs={{4,1},{0,4},{5,0},{1,5},{6,3},{2,6},{7,2},{3,7},{12,9},{8,12},{13,... | collective-permute-start | bytes 122888 | tf_op jit(solution)/shard_map/ppermute | solution.py:362
  107.0 5.5 %collective-permute-start.66 = (f32[40,256]{1,0:T(8,128)S(1)}, f32[40,256]{1,0:T(8,128)S(1)}, u32[]{:S(2)}, u32[]{:S(2)}) collective-permute-start(f32[40,256]{1,0:T(8,128)S(1)} %get-tuple-element.144), channel_id=1, source_target_pairs={{4,3},{0,4},{5,2},{1,5},{6,1},{2,6},{7,0},{3,7},{12,11},{8,12},{13... | collective-permute-start | bytes 122888 | tf_op jit(solution)/shard_map/ppermute | solution.py:362
  109.7 3.5 %collective-permute-start.68 = (f32[40,256]{1,0:T(8,128)S(1)}, f32[40,256]{1,0:T(8,128)S(1)}, u32[]{:S(2)}, u32[]{:S(2)}) collective-permute-start(f32[40,256]{1,0:T(8,128)S(1)} %get-tuple-element.144), channel_id=1, source_target_pairs={{4,2},{0,4},{5,3},{1,5},{6,0},{2,6},{7,1},{3,7},{12,10},{8,12},{13... | collective-permute-start | bytes 122888 | tf_op jit(solution)/shard_map/ppermute | solution.py:362
  (59 other events, 140.6 us)

commit v3 on v2

v3 whole, which is shorter than its diff:
```python
import functools

import jax
import jax.numpy as jnp
from jax import lax
from jax.experimental import pallas as pl
from jax.experimental.pallas import tpu as pltpu
from jax.sharding import PartitionSpec as P


ITERS = 8
STEP_PRIMAL = 0.5
STEP_DUAL = 0.5

DUAL = 0

F32 = jnp.float32
BF16 = jnp.bfloat16


def is_dual_core():
    return lax.axis_index("row") % 2 == DUAL


def assemble(ref, parts, first, rows, stride, me):
    for j in range(len(parts)):
        piece = parts[0]
        for o in range(1, len(parts)):
            piece = jnp.where(me == (j ^ o), parts[o], piece)
        ref[pl.ds(first + j * stride, rows), :] = piece


def by_offset(refs, order):
    return [refs[order.index(o)] for o in range(len(order))]


def total_of(refs, rows):
    level = [ref[pl.ds(0, rows), :] for ref in refs]
    while len(level) > 1:
        level = [level[i] + level[i + 1] for i in range(0, len(level), 2)]
    return level[0]


def z_order(n):
    return [3, 1, 2, 0] if n == 4 else list(range(n))


def col_order(n):
    return [3, 1, 2, 0] if n == 4 else list(range(n))


def note_step(hist_ref, hist_out, index, step):
    hist_out[...] = hist_ref[...]
    hist_out[pl.ds(index, 1), :] = jnp.sum(step * step, axis=0, keepdims=True)


def update_dual(iteration, total, dual_ref, hist_ref, dual_out, hist_out):
    dual = dual_ref[...]
    dual_next = jnp.maximum(dual - STEP_DUAL * total, 0.0)
    dual_out[...] = dual_next
    note_step(hist_ref, hist_out, iteration - 1, dual_next - dual)
    return dual_next


def dual_body(iteration, n_msgs, slots, *refs):
    msgs = by_offset(refs[:n_msgs], col_order(n_msgs))
    (dual_ref, hist_ref, cost_ref, one_ref, extra_ref, *blk_refs) = refs[n_msgs : n_msgs + 7]
    (out_ref, dual_out, hist_out, prod_ref) = refs[n_msgs + 7 :]
    rows, _ = dual_out.shape
    blocks = cost_ref.shape[0]

    @pl.when(is_dual_core())
    def _():
        if iteration == 0:
            each = rows // (2 * n_msgs)
            me = lax.axis_index("col")
            for slab in range(2):
                parts = [m[pl.ds(slab * each, each), :] for m in msgs]
                assemble(dual_out, parts, slab * (rows // 2), each, each, me)
            dual_next = dual_out[...]
            hist_out[...] = jnp.zeros_like(hist_out)
            out_ref[pl.ds(blocks, extra_ref.shape[0]), :] = extra_ref[...]
        else:
            dual_next = update_dual(
                iteration, total_of(msgs, rows), dual_ref, hist_ref, dual_out, hist_out
            )
        half = dual_next.astype(BF16)
        slab_rows = rows // 2
        for r in range(rows):
            for s in range(slots):
                at = (r // slab_rows * slots + s) * slab_rows + r % slab_rows
                prod_ref[pl.ds(at, 1), :] = jnp.dot(
                    half[r : r + 1], blk_refs[r // slab_rows][r % slab_rows * slots + s], preferred_element_type=F32
                )
        prod = prod_ref[...]
        high = prod.astype(BF16)
        rest = prod - high.astype(F32)
        mid = rest.astype(BF16)
        low = (rest - mid.astype(F32)).astype(BF16)
        stacked = jnp.concatenate([high, mid, low], axis=0)
        grad = jnp.dot(one_ref[...], stacked, preferred_element_type=F32)
        out_ref[pl.ds(0, blocks), :] = grad - cost_ref[...]


def take(array, index, count, first, rows, stride):
    piece = array[first : first + rows]
    for j in range(1, count):
        at = first + j * stride
        piece = jnp.where(index == j, array[at : at + rows], piece)
    return piece


def last_body(iterations, n_msgs, d_rows, p_rows, *refs):
    msgs = by_offset(refs[:n_msgs], col_order(n_msgs))
    (dual_ref, hist_ref, primal_ref) = refs[n_msgs : n_msgs + 3]
    (out_ref, dual_out, away_ref, next_ref) = refs[n_msgs + 3 :]
    half = next_ref.shape[0] // 2
    dual_core = is_dual_core()

    @pl.when(dual_core)
    def _():
        rows, kept = next_ref.shape[0], hist_ref.shape[0]
        total = total_of(msgs, rows + kept)
        out_ref[pl.ds(0, kept), :] = total[rows:]
        hist_out = out_ref.at[pl.ds(kept, kept)]
        dual_next = update_dual(iterations, total[:rows], dual_ref, hist_ref, next_ref, hist_out)
        col = lax.axis_index("col")
        dual_out[...] = take(dual_next, col, n_msgs, 0, d_rows, d_rows)
        away_ref[pl.ds(0, d_rows), :] = take(dual_next, col, n_msgs, half, d_rows, d_rows)

    @pl.when(jnp.logical_not(dual_core))
    def _():
        away_ref[pl.ds(0, p_rows), :] = primal_ref[pl.ds(DUAL * p_rows, p_rows), :]


def norm_body(n_msgs, p_total, d_total, *refs):
    msgs = by_offset(refs[:n_msgs], z_order(n_msgs))
    norm_out = refs[n_msgs]
    kept = norm_out.shape[1]

    @pl.when(jnp.logical_not(is_dual_core()))
    def _():
        def norms(squares, total):
            column = jnp.sqrt(jnp.sum(squares, axis=1, keepdims=True) / total)
            wide = jnp.broadcast_to(column, (kept, 128))
            row = lax.broadcasted_iota(jnp.int32, wide.shape, 0)
            lane = lax.broadcasted_iota(jnp.int32, wide.shape, 1)
            return jnp.sum(jnp.where(row == lane, wide, 0.0), axis=0, keepdims=True)[:, :kept]

        total = total_of(msgs, 2 * kept)
        norm_out[...] = jnp.concatenate(
            [norms(msgs[0][pl.ds(0, kept), :], p_total), norms(total[kept:], d_total)], axis=0
        )


def finish_body(dual_ref, primal_ref, back_ref, own_ref, got_ref, primal_out, dual_out, norm_out):
    width = dual_ref.shape[1]
    d_rows, p_rows = dual_out.shape[0] // width, primal_out.shape[0] // width
    dual_core = is_dual_core()

    def give(out_ref, rows):
        for r in range(rows.shape[0]):
            out_ref[pl.ds(r * width, width)] = rows[r]

    @pl.when(dual_core)
    def _():
        give(dual_out, dual_ref[...])
        give(primal_out, back_ref[pl.ds(0, p_rows), :])
        norm_out[...] = got_ref[...]

    @pl.when(jnp.logical_not(dual_core))
    def _():
        give(dual_out, back_ref[pl.ds(0, d_rows), :])
        give(primal_out, primal_ref[pl.ds((1 - DUAL) * p_rows, p_rows), :])
        norm_out[...] = own_ref[...]


def pack_body(n, *refs):
    (sources, out_ref, held, sem) = (refs[:n], refs[n], refs[n + 1 : 2 * n + 1], refs[2 * n + 1])
    copies = [
        pltpu.make_async_copy(source, ref, sem.at[i])
        for i, (source, ref) in enumerate(zip(sources, held, strict=True))
    ]
    for copy in copies:
        copy.start()
    for copy in copies:
        copy.wait()
    (cols_ref, *vectors) = held
    width = out_ref.shape[1]
    at = 0
    for ref in vectors:
        for i in range(ref.shape[0] // width):
            out_ref[at, :] = ref[pl.ds(i * width, width)]
            at += 1
    out_ref[pl.ds(at, cols_ref.shape[0]), pl.ds(0, cols_ref.shape[1])] = cols_ref[...].astype(F32)


def pack_call(out, *arrays):
    n = len(arrays)
    return pl.pallas_call(
        functools.partial(pack_body, n),
        out_shape=out,
        in_specs=[pl.BlockSpec(memory_space=pltpu.HBM)] * n,
        out_specs=pl.BlockSpec(memory_space=pltpu.VMEM),
        scratch_shapes=[pltpu.VMEM(a.shape, a.dtype) for a in arrays]
        + [pltpu.SemaphoreType.DMA((n,))],
        compiler_params=pltpu.CompilerParams(vmem_limit_bytes=66985984),
    )(*arrays)


def setup_body(d_rows, p_rows, slab_rows, slots, n_z, n_col, *refs):
    (own_ref, other_ref, dual_out, extra_out, cost_out, right_out, one_out, pick_out) = refs[:8]
    column_ref = refs[8]
    dual_core = is_dual_core()
    first = jnp.where(dual_core, own_ref[...], other_ref[...])
    second = jnp.where(dual_core, other_ref[...], own_ref[...])
    z, col = lax.axis_index("row") // 2, lax.axis_index("col")
    at = 0
    for slab, part in enumerate((first, second)):
        dual_out[pl.ds(slab * d_rows, d_rows), :] = part[:d_rows]
    at += d_rows
    for slab, part in enumerate((first, second)):
        piece = part[at : at + d_rows]
        for j in range(n_col):
            right_out[pl.ds(slab * slab_rows + j * d_rows, d_rows), :] = jnp.where(
                col == j, piece, 0.0
            )
    at += d_rows
    for slab, part in enumerate((first, second)):
        piece = part[at : at + p_rows]
        for j in range(n_z):
            cost_out[pl.ds((2 * j + slab ^ DUAL) * p_rows, p_rows), :] = jnp.where(
                z == j, piece, 0.0
            )
    at += p_rows
    for k in range(3):
        for slab, part in enumerate((first, second)):
            extra_out[pl.ds((2 * k + slab ^ DUAL) * p_rows, p_rows), :] = part[at : at + p_rows]
        at += p_rows
    entries, blocks = pick_out.shape
    side, lanes = -(-blocks // 128) * 128, column_ref.shape[1]
    column_ref[...] = jnp.full(column_ref.shape, -1.0, F32)
    for k, (part, slot) in enumerate((p, s) for p in (first, second) for s in range(slots)):
        column_ref[pl.ds(0, 1), pl.ds(k * slab_rows, slab_rows)] = part[
            at + slot : at + slot + 1, :slab_rows
        ]
    iota = lax.broadcasted_iota(jnp.int32, (side, lanes), 0).astype(F32)
    column = jnp.broadcast_to(column_ref[pl.ds(0, 1), :], (side, lanes))
    hot = jnp.where(column == iota, 1.0, 0.0)
    pick_out[...] = hot.T[:entries, :blocks].astype(BF16)
    one = hot[:blocks, :entries]
    one_out[...] = jnp.concatenate([one] * 3, axis=1).astype(BF16)


def primal_body(iteration, last, n_msgs, slots, *refs):
    msgs = by_offset(refs[:n_msgs], z_order(n_msgs))
    (primal_ref, low_ref, up_ref, hist_ref, right_ref, pick_ref, *blk_refs) = refs[
        n_msgs : n_msgs + 8
    ]
    (out_ref, primal_out, *rest) = refs[n_msgs + 8 :]
    blk_refs = blk_refs[::-1]
    blocks = primal_ref.shape[0]
    rows = right_ref.shape[0]
    slab_rows = rows // 2
    hist_out = out_ref.at[pl.ds(rows, hist_ref.shape[0])] if last else rest[0]
    bounds_out = rest[1:]

    @pl.when(jnp.logical_not(is_dual_core()))
    def _():
        total = total_of(msgs, blocks)
        if iteration == 0:
            each = blocks // n_msgs
            me = lax.axis_index("row") // 2
            for k, ref in enumerate((primal_out, *bounds_out)):
                parts = [m[pl.ds(blocks + k * each, each), :] for m in msgs]
                assemble(ref, parts, 0, each, each, me)
            primal, low, up = primal_out[...], bounds_out[0][...], bounds_out[1][...]
            hist_out[...] = jnp.zeros_like(hist_out)
        else:
            primal, low, up = primal_ref[...], low_ref[...], up_ref[...]
        primal_next = jnp.minimum(up, jnp.maximum(low, primal + STEP_PRIMAL * total))
        if last:
            index = lax.axis_index("row") // 2
            each = primal_out.shape[0]
            primal_out[...] = take(primal_next, index, n_msgs, 0, each, each)
        else:
            primal_out[...] = primal_next
        note_step(hist_out if iteration == 0 else hist_ref, hist_out, iteration, primal_next - primal)
        ext = (2.0 * primal_next - primal).astype(BF16)
        picked = jnp.dot(pick_ref[...], ext, preferred_element_type=F32).astype(BF16)
        for r in range(rows):
            acc = -right_ref[pl.ds(r, 1), :]
            for s in range(slots):
                at = (r // slab_rows * slots + s) * slab_rows + r % slab_rows
                acc = acc + jnp.dot(
                    picked[at : at + 1],
                    blk_refs[r // slab_rows][r % slab_rows * slots + s],
                    preferred_element_type=F32,
                )
            out_ref[pl.ds(r, 1), :] = acc


def weights_body(in_ref, out_ref, sem):
    copy = pltpu.make_async_copy(in_ref, out_ref, sem)
    copy.start()
    copy.wait()

    @pl.when(jnp.logical_not(is_dual_core()))
    def _():
        def step(i, carry):
            for k in range(8):
                out_ref[i * 8 + k] = out_ref[i * 8 + k].T
            return carry

        lax.fori_loop(0, in_ref.shape[0] // 8, step, 0)


def weights_call(blocks):
    return pl.pallas_call(
        weights_body,
        out_shape=jax.ShapeDtypeStruct(blocks.shape, BF16),
        in_specs=[pl.BlockSpec(memory_space=pltpu.HBM)],
        out_specs=pl.BlockSpec(memory_space=pltpu.VMEM),
        scratch_shapes=[pltpu.SemaphoreType.DMA],
        compiler_params=pltpu.CompilerParams(vmem_limit_bytes=8 * 2**20),
    )(blocks)


def local_call(body, outs, scratch, n_in):
    return pl.pallas_call(
        body,
        out_shape=outs,
        in_specs=[pl.BlockSpec(memory_space=pltpu.VMEM)] * n_in,
        out_specs=[pl.BlockSpec(memory_space=pltpu.VMEM)] * len(outs),
        scratch_shapes=scratch,
        compiler_params=pltpu.CompilerParams(vmem_limit_bytes=4 * 2**20),
    )


def per_device(
    blocks, block_cols, objective, lower_bound, upper_bound, right_side, primal_init, dual_init
):
    slab_rows, slots, width = blocks.shape[0], blocks.shape[1], blocks.shape[2]
    n_row, n_col = lax.axis_size("row"), lax.axis_size("col")
    n_z = n_row // 2
    p_rows = primal_init.shape[0] // width
    d_rows = dual_init.shape[0] // width
    col_blocks = p_rows * n_row
    rows = 2 * slab_rows
    entries = rows * slots

    swap_pairs = [(r, r ^ 1) for r in range(n_row)]

    def over_z(src, o):
        away = [(2 * k + src, 2 * (k ^ o) + 1 - src) for k in range(n_z)]
        return away + [(2 * k + 1 - src, 2 * k + src) for k in range(n_z)]

    def over_col(src, o):
        pairs = []
        for k in range(n_z):
            for c in range(n_col):
                pairs.append(((2 * k + src) * n_col + c, (2 * k + 1 - src) * n_col + (c ^ o)))
                pairs.append(((2 * k + 1 - src) * n_col + c, (2 * k + src) * n_col + c))
        return pairs

    def to_primal(x):
        return [lax.ppermute(x, "row", over_z(DUAL, o)) for o in z_order(n_z)]

    def to_dual(x):
        return [lax.ppermute(x, ("row", "col"), over_col(1 - DUAL, o)) for o in col_order(n_col)]

    def shape(n, wide=width, dtype=F32):
        return jax.ShapeDtypeStruct((n, wide), dtype)

    mine = blocks.reshape(slab_rows * slots, width, width)
    own = pack_call(
        shape(2 * d_rows + 4 * p_rows + slots),
        block_cols.T, dual_init, right_side, objective, primal_init, lower_bound, upper_bound,
    )
    gated, own = lax.optimization_barrier((mine, own))
    other = lax.ppermute(own, "row", swap_pairs)
    theirs = lax.ppermute(gated, "row", swap_pairs)
    dual_part, extra, cost, right, one_three, pick = local_call(
        functools.partial(setup_body, d_rows, p_rows, slab_rows, slots, n_z, n_col),
        [
            shape(2 * d_rows),
            shape(6 * p_rows),
            shape(col_blocks),
            shape(rows),
            shape(col_blocks, 3 * entries, BF16),
            shape(entries, col_blocks, BF16),
        ],
        [pltpu.VMEM((8, -(-entries // 128) * 128), F32)],
        2,
    )(own, other)
    own_weights = weights_call(mine)
    dual_part, own_weights = lax.optimization_barrier((dual_part, own_weights))
    weights = (own_weights, weights_call(theirs))

    hist_rows = -(-ITERS // 8) * 8
    dual = right
    primal = cost
    bounds = (cost, cost)
    primal_hist = dual_hist = jnp.zeros((hist_rows, width), F32)
    products = pltpu.VMEM((entries, width), F32)

    arrived = to_dual(dual_part)
    for iteration in range(ITERS):
        first, last = iteration == 0, iteration == ITERS - 1
        message, dual, dual_hist = local_call(
            functools.partial(dual_body, iteration, n_col, slots),
            [shape(col_blocks + (6 * p_rows if first else 0)), shape(rows), shape(hist_rows)],
            [products],
            n_col + 7,
        )(*arrived, dual, dual_hist, cost, one_three, extra, *weights)
        arrived = to_primal(message)
        message, primal, *others = local_call(
            functools.partial(primal_body, iteration, last, n_z, slots),
            [
                shape(rows + (hist_rows if last else 0)),
                shape(2 * p_rows if last else col_blocks),
            ]
            + [shape(hist_rows)] * (not last)
            + [shape(col_blocks)] * (2 if first else 0),
            [],
            n_z + 8,
        )(*arrived, primal, *bounds, primal_hist, right, pick, *weights)
        if first:
            bounds = others[1:]
        if not last:
            primal_hist = others[0]
        arrived = to_dual(message)
    message, dual, away = local_call(
        functools.partial(last_body, ITERS, n_col, d_rows, p_rows),
        [shape(2 * hist_rows), shape(d_rows), shape(max(p_rows, d_rows))],
        [pltpu.VMEM((rows, width), F32)],
        n_col + 3,
    )(*arrived, dual, dual_hist, primal)
    back = lax.ppermute(away, "row", swap_pairs)
    arrived = to_primal(message)
    (norms,) = local_call(
        functools.partial(
            norm_body,
            n_z,
            float(primal_init.shape[0] * n_row * n_col),
            float(dual_init.shape[0] * n_row * n_col),
        ),
        [shape(2, hist_rows)],
        [],
        n_z,
    )(*arrived)
    primal_out, dual_out, norms = local_call(
        finish_body,
        [
            jax.ShapeDtypeStruct(primal_init.shape, F32),
            jax.ShapeDtypeStruct(dual_init.shape, F32),
            shape(2, hist_rows),
        ],
        [],
        5,
    )(dual, primal, back, norms, lax.ppermute(norms, "row", swap_pairs))
    return (primal_out, dual_out, norms.T[:ITERS])


def solution(mesh):
    in_specs = (
        P("row", "col", None, None),
        P("row", "col"),
        P(("col", "row")),
        P(("col", "row")),
        P(("col", "row")),
        P(("row", "col")),
        P(("col", "row")),
        P(("row", "col")),
    )
    out_specs = (P(("col", "row")), P(("row", "col")), P())
    return jax.shard_map(
        per_device, mesh=mesh, in_specs=in_specs, out_specs=out_specs, check_vma=False
    )
```

time: 121 us -> 119 us (0.983)
  local copies, waits for them, and re-layouts: 7.74 us -> 2.19 us
  starting transfers between devices: 58.8 us -> 60.9 us
    unnamed x16 -> x4, local copies, waits for them, and re-layouts: 7.74 us -> 2.19 us
    ppermute x1, waiting for transfers between devices: 0.88 us -> 4.47 us  [per_device(): other = lax.ppermute(own, 'row', swap_pairs)]
    ppermute x72, waiting for transfers between devices: 37.3 us -> 35.6 us  [the longest x36 19.3 us: to_dual(): lax.ppermute(x, ('row', 'col'), over_col(1 - DUAL, o))]
    pallas_call x1, Pallas kernels: 0.11 us -> 1.48 us  [pack_call(): pl.pallas_call(functools.partial(pack_body, n), out_shape=out, in_specs=[...]
    ppermute x1, starting transfers between devices: 1.61 us -> 2.92 us  [per_device(): lax.ppermute(norms, 'row', swap_pairs)]
  transfers between devices with their start and end apart: 76 -> 76, of which waited for: 44 -> 55; matrix products, arithmetic and copies ran while one was open for 0% -> 0% of each run, Pallas kernels for 1% -> 1%
where the time goes in v3:
time: 119 us; the launch traced here: 118 us
  starting transfers between devices  60.9 us (51%)
  waiting for transfers between devices  40.9 us (34%)
  Pallas kernels  13.7 us (12%)
  local copies, waits for them, and re-layouts  2.19 us (2%)
    ppermute x36, starting transfers between devices, to_dual(): lax.ppermute(x, ('row', 'col'), over_col(1 - DUAL, o))  46.6 us
    ppermute x36, waiting for transfers between devices, to_dual(): lax.ppermute(x, ('row', 'col'), over_col(1 - DUAL, o))  19.3 us
    ppermute x36, waiting for transfers between devices, to_primal(): return [lax.ppermute(x, 'row', over_z(DUAL, o)) for o in z_order(n_z)]  16.3 us
    pallas_call x8, Pallas kernels, per_device(): local_call(functools.partial(dual_body, iteration, n_col, slots), [shape(...  10.8 us
    ppermute x36, starting transfers between devices, to_primal(): return [lax.ppermute(x, 'row', over_z(DUAL, o)) for o in z_order(n_z)]  10.3 us
    ppermute x1, waiting for transfers between devices, per_device(): other = lax.ppermute(own, 'row', swap_pairs)  4.47 us
    ppermute x1, starting transfers between devices, per_device(): lax.ppermute(norms, 'row', swap_pairs)  2.92 us
  transfers between devices with their start and end apart: 76, of which 55 were waited for; matrix products, arithmetic and copies ran while one was open for 0% of the time, Pallas kernels for 1%

profile of v3, /device:TPU:0, one launch (start us, length us, event | category | flops | bytes accessed | tf_op | source)
XLA Modules:
  0.0 118.4 jit_solution(6101465340801217585)
XLA Ops:
  0.6 1.5 %shard_map.103.refs_0_ = f32[34,256]{1,0:T(8,128)} custom-call(s32[2,16]{1,0:T(2,128)} %bitcast.5, f32[1024]{0:T(1024)} %refs_1_.1, f32[1024]{0:T(1024)} %refs_2_.1, f32[1536]{0:T(1024)} %refs_3_.1, f32[1536]{0:T(1024)} %refs_4_.1, f32[1536]{0:T(1024)} %refs_5_.1, f32[1536]{0:T(1024)} %refs_6_.1), custom_call_target="tpu_custom_call" | custom-call | tf_op jit(solution)/shard_map/pallas_call | solution.py:200
  2.8 2.2 %copy-done = bf16[16,2,256,256]{3,2,1,0:T(8,128)(2,1)S(1)} copy-done((bf16[16,2,256,256]{3,2,1,0:T(8,128)(2,1)S(1)}, bf16[16,2,256,256]{3,2,1,0:T(8,128)(2,1)}, u32[]{:S(2)}) %copy-start) | copy-done | bytes 4194328
  5.3 4.5 %collective-permute-done.refs_1_ = f32[34,256]{1,0:T(8,128)S(1)} collective-permute-done((f32[34,256]{1,0:T(8,128)}, f32[34,256]{1,0:T(8,128)S(1)}, u32[]{:S(2)}, u32[]{:S(2)}) %collective-permute-start) | collective-permute-done | bytes 34848 | tf_op jit(solution)/shard_map/ppermute | solution.py:381
  10.3 3.5 %collective-permute-start.2 = (f32[8,256]{1,0:T(8,128)S(1)}, f32[8,256]{1,0:T(8,128)S(1)}, u32[]{:S(2)}, u32[]{:S(2)}) collective-permute-start(f32[8,256]{1,0:T(8,128)S(1)} %get-tuple-element.70), channel_id=1, source_target_pairs={{4,1},{0,4},{5,0},{1,5},{6,3},{2,6},{7,2},{3,7},{12,9},{8,12},{13,... | collective-permute-start | bytes 24584 | tf_op jit(solution)/shard_map/ppermute | solution.py:370
  15.5 1.5 %collective-permute-done.3.refs_2_ = f32[8,256]{1,0:T(8,128)S(1)} collective-permute-done((f32[8,256]{1,0:T(8,128)S(1)}, f32[8,256]{1,0:T(8,128)S(1)}, u32[]{:S(2)}, u32[]{:S(2)}) %collective-permute-start.3) | collective-permute-done | bytes 8224 | tf_op jit(solution)/shard_map/ppermute | solution.py:370
  17.0 1.4 %shard_map.107 = (f32[84,256]{1,0:T(8,128)S(1)}, f32[32,256]{1,0:T(8,128)S(1)}, f32[8,256]{1,0:T(8,128)S(1)}) custom-call(f32[8,256]{1,0:T(8,128)S(1)} %collective-permute-done.1.refs_0_, f32[8,256]{1,0:T(8,128)S(1)} %collective-permute-done.2.refs_1_, f32[8,256]{1,0:T(8,128)S(1)} %collective-permute-done.3.refs_2_, ...), custom_call_target="tpu_custom_call" | custom-call | tf_op jit(solution)/shard_map/pallas_call | solution.py:410
  23.5 3.2 %collective-permute-start.10 = (f32[32,256]{1,0:T(8,128)S(1)}, f32[32,256]{1,0:T(8,128)S(1)}, u32[]{:S(2)}, u32[]{:S(2)}) collective-permute-start(f32[32,256]{1,0:T(8,128)S(1)} %get-tuple-element.79), channel_id=1, source_target_pairs={{4,3},{0,4},{5,2},{1,5},{6,1},{2,6},{7,0},{3,7},{12,11},{8,12},{13... | collective-permute-start | bytes 98312 | tf_op jit(solution)/shard_map/ppermute | solution.py:370
  27.3 1.6 %collective-permute-start.13 = (f32[32,256]{1,0:T(8,128)S(1)}, f32[32,256]{1,0:T(8,128)S(1)}, u32[]{:S(2)}, u32[]{:S(2)}) collective-permute-start(f32[32,256]{1,0:T(8,128)S(1)} %get-tuple-element.79), channel_id=1, source_target_pairs={{4,0},{0,4},{5,1},{1,5},{6,2},{2,6},{7,3},{3,7},{12,8},{8,12},{13,... | collective-permute-start | bytes 98312 | tf_op jit(solution)/shard_map/ppermute | solution.py:370
  35.3 3.7 %collective-permute-start.18 = (f32[32,256]{1,0:T(8,128)S(1)}, f32[32,256]{1,0:T(8,128)S(1)}, u32[]{:S(2)}, u32[]{:S(2)}) collective-permute-start(f32[32,256]{1,0:T(8,128)S(1)} %get-tuple-element.87), channel_id=1, source_target_pairs={{4,3},{0,4},{5,2},{1,5},{6,1},{2,6},{7,0},{3,7},{12,11},{8,12},{13... | collective-permute-start | bytes 98312 | tf_op jit(solution)/shard_map/ppermute | solution.py:370
  46.6 4.0 %collective-permute-start.26 = (f32[32,256]{1,0:T(8,128)S(1)}, f32[32,256]{1,0:T(8,128)S(1)}, u32[]{:S(2)}, u32[]{:S(2)}) collective-permute-start(f32[32,256]{1,0:T(8,128)S(1)} %get-tuple-element.93), channel_id=1, source_target_pairs={{4,3},{0,4},{5,2},{1,5},{6,1},{2,6},{7,0},{3,7},{12,11},{8,12},{13... | collective-permute-start | bytes 98312 | tf_op jit(solution)/shard_map/ppermute | solution.py:370
  51.7 1.5 %collective-permute-done.26.refs_0_ = f32[32,256]{1,0:T(8,128)S(1)} collective-permute-done((f32[32,256]{1,0:T(8,128)S(1)}, f32[32,256]{1,0:T(8,128)S(1)}, u32[]{:S(2)}, u32[]{:S(2)}) %collective-permute-start.26) | collective-permute-done | bytes 32800 | tf_op jit(solution)/shard_map/ppermute | solution.py:370
  58.0 4.2 %collective-permute-start.34 = (f32[32,256]{1,0:T(8,128)S(1)}, f32[32,256]{1,0:T(8,128)S(1)}, u32[]{:S(2)}, u32[]{:S(2)}) collective-permute-start(f32[32,256]{1,0:T(8,128)S(1)} %get-tuple-element.99), channel_id=1, source_target_pairs={{4,3},{0,4},{5,2},{1,5},{6,1},{2,6},{7,0},{3,7},{12,11},{8,12},{13... | collective-permute-start | bytes 98312 | tf_op jit(solution)/shard_map/ppermute | solution.py:370
  63.5 1.4 %collective-permute-done.34.refs_0_ = f32[32,256]{1,0:T(8,128)S(1)} collective-permute-done((f32[32,256]{1,0:T(8,128)S(1)}, f32[32,256]{1,0:T(8,128)S(1)}, u32[]{:S(2)}, u32[]{:S(2)}) %collective-permute-start.34) | collective-permute-done | bytes 32800 | tf_op jit(solution)/shard_map/ppermute | solution.py:370
  65.7 1.3 %shard_map.115 = (f32[48,256]{1,0:T(8,128)S(1)}, f32[32,256]{1,0:T(8,128)S(1)}, f32[8,256]{1,0:T(8,128)S(1)}) custom-call(f32[32,256]{1,0:T(8,128)S(1)} %collective-permute-done.34.refs_0_, f32[32,256]{1,0:T(8,128)S(1)} %collective-permute-done.35.refs_1_, f32[32,256]{1,0:T(8,128)S(1)} %collective-permute-done.36.refs_2_, ...), custom_call_target="tpu_custom_call" | custom-call | tf_op jit(solution)/shard_map/pallas_call | solution.py:410
  69.7 4.1 %collective-permute-start.42 = (f32[32,256]{1,0:T(8,128)S(1)}, f32[32,256]{1,0:T(8,128)S(1)}, u32[]{:S(2)}, u32[]{:S(2)}) collective-permute-start(f32[32,256]{1,0:T(8,128)S(1)} %get-tuple-element.105), channel_id=1, source_target_pairs={{4,3},{0,4},{5,2},{1,5},{6,1},{2,6},{7,0},{3,7},{12,11},{8,12},{13... | collective-permute-start | bytes 98312 | tf_op jit(solution)/shard_map/ppermute | solution.py:370
  74.9 1.5 %collective-permute-done.42.refs_0_ = f32[32,256]{1,0:T(8,128)S(1)} collective-permute-done((f32[32,256]{1,0:T(8,128)S(1)}, f32[32,256]{1,0:T(8,128)S(1)}, u32[]{:S(2)}, u32[]{:S(2)}) %collective-permute-start.42) | collective-permute-done | bytes 32800 | tf_op jit(solution)/shard_map/ppermute | solution.py:370
  77.2 1.3 %shard_map.117 = (f32[48,256]{1,0:T(8,128)S(1)}, f32[32,256]{1,0:T(8,128)S(1)}, f32[8,256]{1,0:T(8,128)S(1)}) custom-call(f32[32,256]{1,0:T(8,128)S(1)} %collective-permute-done.42.refs_0_, f32[32,256]{1,0:T(8,128)S(1)} %collective-permute-done.43.refs_1_, f32[32,256]{1,0:T(8,128)S(1)} %collective-permute-done.44.refs_2_, ...), custom_call_target="tpu_custom_call" | custom-call | tf_op jit(solution)/shard_map/pallas_call | solution.py:410
  81.3 4.0 %collective-permute-start.50 = (f32[32,256]{1,0:T(8,128)S(1)}, f32[32,256]{1,0:T(8,128)S(1)}, u32[]{:S(2)}, u32[]{:S(2)}) collective-permute-start(f32[32,256]{1,0:T(8,128)S(1)} %get-tuple-element.111), channel_id=1, source_target_pairs={{4,3},{0,4},{5,2},{1,5},{6,1},{2,6},{7,0},{3,7},{12,11},{8,12},{13... | collective-permute-start | bytes 98312 | tf_op jit(solution)/shard_map/ppermute | solution.py:370
  86.5 1.4 %collective-permute-done.50.refs_0_ = f32[32,256]{1,0:T(8,128)S(1)} collective-permute-done((f32[32,256]{1,0:T(8,128)S(1)}, f32[32,256]{1,0:T(8,128)S(1)}, u32[]{:S(2)}, u32[]{:S(2)}) %collective-permute-start.50) | collective-permute-done | bytes 32800 | tf_op jit(solution)/shard_map/ppermute | solution.py:370
  92.7 4.1 %collective-permute-start.58 = (f32[32,256]{1,0:T(8,128)S(1)}, f32[32,256]{1,0:T(8,128)S(1)}, u32[]{:S(2)}, u32[]{:S(2)}) collective-permute-start(f32[32,256]{1,0:T(8,128)S(1)} %get-tuple-element.117), channel_id=1, source_target_pairs={{4,3},{0,4},{5,2},{1,5},{6,1},{2,6},{7,0},{3,7},{12,11},{8,12},{13... | collective-permute-start | bytes 98312 | tf_op jit(solution)/shard_map/ppermute | solution.py:370
  97.9 1.5 %collective-permute-done.58.refs_0_ = f32[32,256]{1,0:T(8,128)S(1)} collective-permute-done((f32[32,256]{1,0:T(8,128)S(1)}, f32[32,256]{1,0:T(8,128)S(1)}, u32[]{:S(2)}, u32[]{:S(2)}) %collective-permute-start.58) | collective-permute-done | bytes 32800 | tf_op jit(solution)/shard_map/ppermute | solution.py:370
  104.3 4.0 %collective-permute-start.66 = (f32[40,256]{1,0:T(8,128)S(1)}, f32[40,256]{1,0:T(8,128)S(1)}, u32[]{:S(2)}, u32[]{:S(2)}) collective-permute-start(f32[40,256]{1,0:T(8,128)S(1)} %get-tuple-element.123), channel_id=1, source_target_pairs={{4,3},{0,4},{5,2},{1,5},{6,1},{2,6},{7,0},{3,7},{12,11},{8,12},{13... | collective-permute-start | bytes 122888 | tf_op jit(solution)/shard_map/ppermute | solution.py:370
  109.5 1.5 %collective-permute-done.66.refs_0_ = f32[40,256]{1,0:T(8,128)S(1)} collective-permute-done((f32[40,256]{1,0:T(8,128)S(1)}, f32[40,256]{1,0:T(8,128)S(1)}, u32[]{:S(2)}, u32[]{:S(2)}) %collective-permute-start.66) | collective-permute-done | bytes 40992 | tf_op jit(solution)/shard_map/ppermute | solution.py:370
  114.1 2.9 %collective-permute-start.75 = (f32[2,8]{1,0:T(2,128)S(1)}, f32[2,8]{1,0:T(2,128)S(1)}, u32[]{:S(2)}, u32[]{:S(2)}) collective-permute-start(f32[2,8]{1,0:T(2,128)S(1)} %shard_map.124.own_ref), channel_id=1, source_target_pairs={{0,4},{4,0},{8,12},{12,8},{16,20},{20,16},{24,28},{28,24},{1,5},{5... | collective-permute-start | bytes 200 | tf_op jit(solution)/shard_map/ppermute | solution.py:461
  (156 shorter events, 55.7 us)
Async XLA Ops:
  2.1 12.4 %collective-permute-start.5 = (bf16[32,256,256]{2,1,0:T(8,128)(2,1)}, bf16[32,256,256]{2,1,0:T(8,128)(2,1)S(1)}, u32[]{:S(2)}, u32[]{:S(2)}) collective-permute-start(bf16[32,256,256]{2,1,0:T(8,128)(2,1)} %bitcast.3), channel_id=1, source_target_pairs={{0,4},{4,0},{8,12},{12,8},{16,20},{20,16},{24,28},{28,24},{1,5},{5... | collective-permute-start | bytes 12582920 | tf_op jit(solution)/shard_map/ppermute | solution.py:382
  2.7 7.1 %collective-permute-start = (f32[34,256]{1,0:T(8,128)}, f32[34,256]{1,0:T(8,128)S(1)}, u32[]{:S(2)}, u32[]{:S(2)}) collective-permute-start(f32[34,256]{1,0:T(8,128)} %shard_map.103.refs_0_), channel_id=1, source_target_pairs={{0,4},{4,0},{8,12},{12,8},{16,20},{20,16},{24,28},{28,24},{1,5},{5... | collective-permute-start | bytes 104456 | tf_op jit(solution)/shard_map/ppermute | solution.py:381
  9.9 4.9 %collective-permute-start.1 = (f32[8,256]{1,0:T(8,128)S(1)}, f32[8,256]{1,0:T(8,128)S(1)}, u32[]{:S(2)}, u32[]{:S(2)}) collective-permute-start(f32[8,256]{1,0:T(8,128)S(1)} %get-tuple-element.70), channel_id=1, source_target_pairs={{4,3},{0,4},{5,2},{1,5},{6,1},{2,6},{7,0},{3,7},{12,11},{8,12},{13... | collective-permute-start | bytes 24584 | tf_op jit(solution)/shard_map/ppermute | solution.py:370
  10.3 5.1 %collective-permute-start.2 = (f32[8,256]{1,0:T(8,128)S(1)}, f32[8,256]{1,0:T(8,128)S(1)}, u32[]{:S(2)}, u32[]{:S(2)}) collective-permute-start(f32[8,256]{1,0:T(8,128)S(1)} %get-tuple-element.70), channel_id=1, source_target_pairs={{4,1},{0,4},{5,0},{1,5},{6,3},{2,6},{7,2},{3,7},{12,9},{8,12},{13,... | collective-permute-start | bytes 24584 | tf_op jit(solution)/shard_map/ppermute | solution.py:370
  20.0 3.4 %collective-permute-start.8 = (f32[84,256]{1,0:T(8,128)S(1)}, f32[84,256]{1,0:T(8,128)S(1)}, u32[]{:S(2)}, u32[]{:S(2)}) collective-permute-start(f32[84,256]{1,0:T(8,128)S(1)} %get-tuple-element.77), channel_id=1, source_target_pairs={{0,20},{8,28},{16,4},{24,12},{4,0},{12,8},{20,16},{28,24},{1,21},{... | collective-permute-start | bytes 258056 | tf_op jit(solution)/shard_map/ppermute | solution.py:367
  23.5 6.4 %collective-permute-start.10 = (f32[32,256]{1,0:T(8,128)S(1)}, f32[32,256]{1,0:T(8,128)S(1)}, u32[]{:S(2)}, u32[]{:S(2)}) collective-permute-start(f32[32,256]{1,0:T(8,128)S(1)} %get-tuple-element.79), channel_id=1, source_target_pairs={{4,3},{0,4},{5,2},{1,5},{6,1},{2,6},{7,0},{3,7},{12,11},{8,12},{13... | collective-permute-start | bytes 98312 | tf_op jit(solution)/shard_map/ppermute | solution.py:370
  26.6 3.3 %collective-permute-start.11 = (f32[32,256]{1,0:T(8,128)S(1)}, f32[32,256]{1,0:T(8,128)S(1)}, u32[]{:S(2)}, u32[]{:S(2)}) collective-permute-start(f32[32,256]{1,0:T(8,128)S(1)} %get-tuple-element.79), channel_id=1, source_target_pairs={{4,1},{0,4},{5,0},{1,5},{6,3},{2,6},{7,2},{3,7},{12,9},{8,12},{13,... | collective-permute-start | bytes 98312 | tf_op jit(solution)/shard_map/ppermute | solution.py:370
  26.7 3.9 %collective-permute-start.12 = (f32[32,256]{1,0:T(8,128)S(1)}, f32[32,256]{1,0:T(8,128)S(1)}, u32[]{:S(2)}, u32[]{:S(2)}) collective-permute-start(f32[32,256]{1,0:T(8,128)S(1)} %get-tuple-element.79), channel_id=1, source_target_pairs={{4,2},{0,4},{5,3},{1,5},{6,0},{2,6},{7,1},{3,7},{12,10},{8,12},{13... | collective-permute-start | bytes 98312 | tf_op jit(solution)/shard_map/ppermute | solution.py:370
  35.3 6.3 %collective-permute-start.18 = (f32[32,256]{1,0:T(8,128)S(1)}, f32[32,256]{1,0:T(8,128)S(1)}, u32[]{:S(2)}, u32[]{:S(2)}) collective-permute-start(f32[32,256]{1,0:T(8,128)S(1)} %get-tuple-element.87), channel_id=1, source_target_pairs={{4,3},{0,4},{5,2},{1,5},{6,1},{2,6},{7,0},{3,7},{12,11},{8,12},{13... | collective-permute-start | bytes 98312 | tf_op jit(solution)/shard_map/ppermute | solution.py:370
  39.0 3.3 %collective-permute-start.19 = (f32[32,256]{1,0:T(8,128)S(1)}, f32[32,256]{1,0:T(8,128)S(1)}, u32[]{:S(2)}, u32[]{:S(2)}) collective-permute-start(f32[32,256]{1,0:T(8,128)S(1)} %get-tuple-element.87), channel_id=1, source_target_pairs={{4,1},{0,4},{5,0},{1,5},{6,3},{2,6},{7,2},{3,7},{12,9},{8,12},{13,... | collective-permute-start | bytes 98312 | tf_op jit(solution)/shard_map/ppermute | solution.py:370
  39.0 3.3 %collective-permute-start.20 = (f32[32,256]{1,0:T(8,128)S(1)}, f32[32,256]{1,0:T(8,128)S(1)}, u32[]{:S(2)}, u32[]{:S(2)}) collective-permute-start(f32[32,256]{1,0:T(8,128)S(1)} %get-tuple-element.87), channel_id=1, source_target_pairs={{4,2},{0,4},{5,3},{1,5},{6,0},{2,6},{7,1},{3,7},{12,10},{8,12},{13... | collective-permute-start | bytes 98312 | tf_op jit(solution)/shard_map/ppermute | solution.py:370
  46.6 6.6 %collective-permute-start.26 = (f32[32,256]{1,0:T(8,128)S(1)}, f32[32,256]{1,0:T(8,128)S(1)}, u32[]{:S(2)}, u32[]{:S(2)}) collective-permute-start(f32[32,256]{1,0:T(8,128)S(1)} %get-tuple-element.93), channel_id=1, source_target_pairs={{4,3},{0,4},{5,2},{1,5},{6,1},{2,6},{7,0},{3,7},{12,11},{8,12},{13... | collective-permute-start | bytes 98312 | tf_op jit(solution)/shard_map/ppermute | solution.py:370
  50.6 3.3 %collective-permute-start.27 = (f32[32,256]{1,0:T(8,128)S(1)}, f32[32,256]{1,0:T(8,128)S(1)}, u32[]{:S(2)}, u32[]{:S(2)}) collective-permute-start(f32[32,256]{1,0:T(8,128)S(1)} %get-tuple-element.93), channel_id=1, source_target_pairs={{4,1},{0,4},{5,0},{1,5},{6,3},{2,6},{7,2},{3,7},{12,9},{8,12},{13,... | collective-permute-start | bytes 98312 | tf_op jit(solution)/shard_map/ppermute | solution.py:370
  50.7 3.3 %collective-permute-start.28 = (f32[32,256]{1,0:T(8,128)S(1)}, f32[32,256]{1,0:T(8,128)S(1)}, u32[]{:S(2)}, u32[]{:S(2)}) collective-permute-start(f32[32,256]{1,0:T(8,128)S(1)} %get-tuple-element.93), channel_id=1, source_target_pairs={{4,2},{0,4},{5,3},{1,5},{6,0},{2,6},{7,1},{3,7},{12,10},{8,12},{13... | collective-permute-start | bytes 98312 | tf_op jit(solution)/shard_map/ppermute | solution.py:370
  58.0 6.8 %collective-permute-start.34 = (f32[32,256]{1,0:T(8,128)S(1)}, f32[32,256]{1,0:T(8,128)S(1)}, u32[]{:S(2)}, u32[]{:S(2)}) collective-permute-start(f32[32,256]{1,0:T(8,128)S(1)} %get-tuple-element.99), channel_id=1, source_target_pairs={{4,3},{0,4},{5,2},{1,5},{6,1},{2,6},{7,0},{3,7},{12,11},{8,12},{13... | collective-permute-start | bytes 98312 | tf_op jit(solution)/shard_map/ppermute | solution.py:370
  62.3 3.3 %collective-permute-start.35 = (f32[32,256]{1,0:T(8,128)S(1)}, f32[32,256]{1,0:T(8,128)S(1)}, u32[]{:S(2)}, u32[]{:S(2)}) collective-permute-start(f32[32,256]{1,0:T(8,128)S(1)} %get-tuple-element.99), channel_id=1, source_target_pairs={{4,1},{0,4},{5,0},{1,5},{6,3},{2,6},{7,2},{3,7},{12,9},{8,12},{13,... | collective-permute-start | bytes 98312 | tf_op jit(solution)/shard_map/ppermute | solution.py:370
  69.7 6.7 %collective-permute-start.42 = (f32[32,256]{1,0:T(8,128)S(1)}, f32[32,256]{1,0:T(8,128)S(1)}, u32[]{:S(2)}, u32[]{:S(2)}) collective-permute-start(f32[32,256]{1,0:T(8,128)S(1)} %get-tuple-element.105), channel_id=1, source_target_pairs={{4,3},{0,4},{5,2},{1,5},{6,1},{2,6},{7,0},{3,7},{12,11},{8,12},{13... | collective-permute-start | bytes 98312 | tf_op jit(solution)/shard_map/ppermute | solution.py:370
  81.3 6.6 %collective-permute-start.50 = (f32[32,256]{1,0:T(8,128)S(1)}, f32[32,256]{1,0:T(8,128)S(1)}, u32[]{:S(2)}, u32[]{:S(2)}) collective-permute-start(f32[32,256]{1,0:T(8,128)S(1)} %get-tuple-element.111), channel_id=1, source_target_pairs={{4,3},{0,4},{5,2},{1,5},{6,1},{2,6},{7,0},{3,7},{12,11},{8,12},{13... | collective-permute-start | bytes 98312 | tf_op jit(solution)/shard_map/ppermute | solution.py:370
  92.7 6.7 %collective-permute-start.58 = (f32[32,256]{1,0:T(8,128)S(1)}, f32[32,256]{1,0:T(8,128)S(1)}, u32[]{:S(2)}, u32[]{:S(2)}) collective-permute-start(f32[32,256]{1,0:T(8,128)S(1)} %get-tuple-element.117), channel_id=1, source_target_pairs={{4,3},{0,4},{5,2},{1,5},{6,1},{2,6},{7,0},{3,7},{12,11},{8,12},{13... | collective-permute-start | bytes 98312 | tf_op jit(solution)/shard_map/ppermute | solution.py:370
  104.3 6.7 %collective-permute-start.66 = (f32[40,256]{1,0:T(8,128)S(1)}, f32[40,256]{1,0:T(8,128)S(1)}, u32[]{:S(2)}, u32[]{:S(2)}) collective-permute-start(f32[40,256]{1,0:T(8,128)S(1)} %get-tuple-element.123), channel_id=1, source_target_pairs={{4,3},{0,4},{5,2},{1,5},{6,1},{2,6},{7,0},{3,7},{12,11},{8,12},{13... | collective-permute-start | bytes 122888 | tf_op jit(solution)/shard_map/ppermute | solution.py:370
  108.3 3.4 %collective-permute-start.67 = (f32[40,256]{1,0:T(8,128)S(1)}, f32[40,256]{1,0:T(8,128)S(1)}, u32[]{:S(2)}, u32[]{:S(2)}) collective-permute-start(f32[40,256]{1,0:T(8,128)S(1)} %get-tuple-element.123), channel_id=1, source_target_pairs={{4,1},{0,4},{5,0},{1,5},{6,3},{2,6},{7,2},{3,7},{12,9},{8,12},{13,... | collective-permute-start | bytes 122888 | tf_op jit(solution)/shard_map/ppermute | solution.py:370
  108.4 3.4 %collective-permute-start.68 = (f32[40,256]{1,0:T(8,128)S(1)}, f32[40,256]{1,0:T(8,128)S(1)}, u32[]{:S(2)}, u32[]{:S(2)}) collective-permute-start(f32[40,256]{1,0:T(8,128)S(1)} %get-tuple-element.123), channel_id=1, source_target_pairs={{4,2},{0,4},{5,3},{1,5},{6,0},{2,6},{7,1},{3,7},{12,10},{8,12},{13... | collective-permute-start | bytes 122888 | tf_op jit(solution)/shard_map/ppermute | solution.py:370
  112.8 4.2 %collective-permute-start.70 = (f32[6,256]{1,0:T(8,128)S(1)}, f32[6,256]{1,0:T(8,128)S(1)}, u32[]{:S(2)}, u32[]{:S(2)}) collective-permute-start(f32[6,256]{1,0:T(8,128)S(1)} %get-tuple-element.128), channel_id=1, source_target_pairs={{0,4},{4,0},{8,12},{12,8},{16,20},{20,16},{24,28},{28,24},{1,5},{5... | collective-permute-start | bytes 18440 | tf_op jit(solution)/shard_map/ppermute | solution.py:439
  114.1 3.7 %collective-permute-start.75 = (f32[2,8]{1,0:T(2,128)S(1)}, f32[2,8]{1,0:T(2,128)S(1)}, u32[]{:S(2)}, u32[]{:S(2)}) collective-permute-start(f32[2,8]{1,0:T(2,128)S(1)} %shard_map.124.own_ref), channel_id=1, source_target_pairs={{0,4},{4,0},{8,12},{12,8},{16,20},{20,16},{24,28},{28,24},{1,5},{5... | collective-permute-start | bytes 200 | tf_op jit(solution)/shard_map/ppermute | solution.py:461
  (54 other events, 130.4 us)

commit v4 on v3

--- a/solution.py
+++ b/solution.py
@@ -12,6 +12,7 @@
 STEP_PRIMAL = 0.5
 STEP_DUAL = 0.5
 
+VECTOR_ROWS = 7
 DUAL = 0
 
 F32 = jnp.float32
@@ -39,6 +40,21 @@
     while len(level) > 1:
         level = [level[i] + level[i + 1] for i in range(0, len(level), 2)]
     return level[0]
+
+
+def vector_rows(rows):
+    step = rows // VECTOR_ROWS if VECTOR_ROWS else rows
+    return [step // 2 + i * step for i in range(VECTOR_ROWS)]
+
+
+def weigh(pairs):
+    chunk = 16
+    total = None
+    for i in range(0, pairs[0][0].shape[0], chunk):
+        for block, column in pairs:
+            term = block[i : i + chunk].astype(F32) * column[i : i + chunk]
+            total = term if total is None else total + term
+    return jnp.sum(total, axis=0, keepdims=True)
 
 
 def z_order(n):
@@ -86,12 +102,18 @@
             )
         half = dual_next.astype(BF16)
         slab_rows = rows // 2
+        by_vector = vector_rows(rows)
+        turned = half[: 8 * (max(by_vector) // 8 + 1)].astype(F32).T if by_vector else None
         for r in range(rows):
             for s in range(slots):
                 at = (r // slab_rows * slots + s) * slab_rows + r % slab_rows
-                prod_ref[pl.ds(at, 1), :] = jnp.dot(
-                    half[r : r + 1], blk_refs[r // slab_rows][r % slab_rows * slots + s], preferred_element_type=F32
-                )
+                block = blk_refs[r // slab_rows][r % slab_rows * slots + s]
+                if r in by_vector:
+                    prod_ref[pl.ds(at, 1), :] = weigh(((block, turned[:, r : r + 1]),))
+                else:
+                    prod_ref[pl.ds(at, 1), :] = jnp.dot(
+                        half[r : r + 1], block, preferred_element_type=F32
+                    )
         prod = prod_ref[...]
         high = prod.astype(BF16)
         rest = prod - high.astype(F32)
@@ -287,16 +309,22 @@
             primal_out[...] = primal_next
         note_step(hist_out if iteration == 0 else hist_ref, hist_out, iteration, primal_next - primal)
         ext = (2.0 * primal_next - primal).astype(BF16)
-        picked = jnp.dot(pick_ref[...], ext, preferred_element_type=F32).astype(BF16)
+        found = jnp.dot(pick_ref[...], ext, preferred_element_type=F32)
+        picked = found.astype(BF16)
+        by_vector = vector_rows(rows)
+        turned = found.T if by_vector else None
         for r in range(rows):
             acc = -right_ref[pl.ds(r, 1), :]
+            pairs = []
             for s in range(slots):
                 at = (r // slab_rows * slots + s) * slab_rows + r % slab_rows
-                acc = acc + jnp.dot(
-                    picked[at : at + 1],
-                    blk_refs[r // slab_rows][r % slab_rows * slots + s],
-                    preferred_element_type=F32,
-                )
+                block = blk_refs[r // slab_rows][r % slab_rows * slots + s]
+                if r in by_vector:
+                    pairs.append((block, turned[:, at : at + 1]))
+                else:
+                    acc = acc + jnp.dot(picked[at : at + 1], block, preferred_element_type=F32)
+            if pairs:
+                acc = acc + weigh(pairs)
             out_ref[pl.ds(r, 1), :] = acc
 
 

time: 119 us -> 116 us (0.975)
  Pallas kernels: 13.7 us -> 12.4 us
    pallas_call x8, Pallas kernels: 10.8 us -> 9.5 us  [per_device(): local_call(functools.partial(dual_body, iteration, n_col, slots), [shape(...]
  transfers between devices with their start and end apart: 76 -> 76, of which waited for: 55 -> 54; matrix products, arithmetic and copies ran while one was open for 0% -> 0% of each run, Pallas kernels for 1% -> 1%
where the time goes in v4:
time: 116 us
  starting transfers between devices  60.1 us (52%)
  waiting for transfers between devices  40.3 us (35%)
  Pallas kernels  12.4 us (11%)
  local copies, waits for them, and re-layouts  2.19 us (2%)
    ppermute x36, starting transfers between devices, to_dual(): lax.ppermute(x, ('row', 'col'), over_col(1 - DUAL, o))  45.8 us
    ppermute x36, waiting for transfers between devices, to_dual(): lax.ppermute(x, ('row', 'col'), over_col(1 - DUAL, o))  18.7 us
    ppermute x36, waiting for transfers between devices, to_primal(): return [lax.ppermute(x, 'row', over_z(DUAL, o)) for o in z_order(n_z)]  16.3 us
    ppermute x36, starting transfers between devices, to_primal(): return [lax.ppermute(x, 'row', over_z(DUAL, o)) for o in z_order(n_z)]  10.4 us
    pallas_call x8, Pallas kernels, per_device(): local_call(functools.partial(dual_body, iteration, n_col, slots), [shape(...  9.5 us
    ppermute x1, waiting for transfers between devices, per_device(): other = lax.ppermute(own, 'row', swap_pairs)  4.47 us
    ppermute x1, starting transfers between devices, per_device(): lax.ppermute(norms, 'row', swap_pairs)  2.98 us
  transfers between devices with their start and end apart: 76, of which 54 were waited for; matrix products, arithmetic and copies ran while one was open for 0% of the time, Pallas kernels for 1%

profile of v4, /device:TPU:0, one launch (start us, length us, event | category | flops | bytes accessed | tf_op | source)
XLA Modules:
  0.0 115.8 jit_solution(5868208981672860989)
XLA Ops:
  0.6 1.5 %shard_map.103.refs_0_ = f32[34,256]{1,0:T(8,128)} custom-call(s32[2,16]{1,0:T(2,128)} %bitcast.5, f32[1024]{0:T(1024)} %refs_1_.1, f32[1024]{0:T(1024)} %refs_2_.1, f32[1536]{0:T(1024)} %refs_3_.1, f32[1536]{0:T(1024)} %refs_4_.1, f32[1536]{0:T(1024)} %refs_5_.1, f32[1536]{0:T(1024)} %refs_6_.1), custom_call_target="tpu_custom_call" | custom-call | tf_op jit(solution)/shard_map/pallas_call | solution.py:222
  2.8 2.2 %copy-done = bf16[16,2,256,256]{3,2,1,0:T(8,128)(2,1)S(1)} copy-done((bf16[16,2,256,256]{3,2,1,0:T(8,128)(2,1)S(1)}, bf16[16,2,256,256]{3,2,1,0:T(8,128)(2,1)}, u32[]{:S(2)}) %copy-start) | copy-done | bytes 4194328
  5.3 4.5 %collective-permute-done.refs_1_ = f32[34,256]{1,0:T(8,128)S(1)} collective-permute-done((f32[34,256]{1,0:T(8,128)}, f32[34,256]{1,0:T(8,128)S(1)}, u32[]{:S(2)}, u32[]{:S(2)}) %collective-permute-start) | collective-permute-done | bytes 34848 | tf_op jit(solution)/shard_map/ppermute | solution.py:409
  10.3 3.5 %collective-permute-start.2 = (f32[8,256]{1,0:T(8,128)S(1)}, f32[8,256]{1,0:T(8,128)S(1)}, u32[]{:S(2)}, u32[]{:S(2)}) collective-permute-start(f32[8,256]{1,0:T(8,128)S(1)} %get-tuple-element.70), channel_id=1, source_target_pairs={{4,1},{0,4},{5,0},{1,5},{6,3},{2,6},{7,2},{3,7},{12,9},{8,12},{13,... | collective-permute-start | bytes 24584 | tf_op jit(solution)/shard_map/ppermute | solution.py:398
  15.5 1.5 %collective-permute-done.3.refs_2_ = f32[8,256]{1,0:T(8,128)S(1)} collective-permute-done((f32[8,256]{1,0:T(8,128)S(1)}, f32[8,256]{1,0:T(8,128)S(1)}, u32[]{:S(2)}, u32[]{:S(2)}) %collective-permute-start.3) | collective-permute-done | bytes 8224 | tf_op jit(solution)/shard_map/ppermute | solution.py:398
  17.0 1.2 %shard_map.107 = (f32[84,256]{1,0:T(8,128)S(1)}, f32[32,256]{1,0:T(8,128)S(1)}, f32[8,256]{1,0:T(8,128)S(1)}) custom-call(f32[8,256]{1,0:T(8,128)S(1)} %collective-permute-done.1.refs_0_, f32[8,256]{1,0:T(8,128)S(1)} %collective-permute-done.2.refs_1_, f32[8,256]{1,0:T(8,128)S(1)} %collective-permute-done.3.refs_2_, ...), custom_call_target="tpu_custom_call" | custom-call | tf_op jit(solution)/shard_map/pallas_call | solution.py:438
  18.2 1.3 %collective-permute-start.6 = (f32[84,256]{1,0:T(8,128)S(1)}, f32[84,256]{1,0:T(8,128)S(1)}, u32[]{:S(2)}, u32[]{:S(2)}) collective-permute-start(f32[84,256]{1,0:T(8,128)S(1)} %get-tuple-element.77), channel_id=1, source_target_pairs={{0,28},{8,20},{16,12},{24,4},{4,0},{12,8},{20,16},{28,24},{1,29},{... | collective-permute-start | bytes 258056 | tf_op jit(solution)/shard_map/ppermute | solution.py:395
  23.5 2.9 %collective-permute-start.10 = (f32[32,256]{1,0:T(8,128)S(1)}, f32[32,256]{1,0:T(8,128)S(1)}, u32[]{:S(2)}, u32[]{:S(2)}) collective-permute-start(f32[32,256]{1,0:T(8,128)S(1)} %get-tuple-element.79), channel_id=1, source_target_pairs={{4,3},{0,4},{5,2},{1,5},{6,1},{2,6},{7,0},{3,7},{12,11},{8,12},{13... | collective-permute-start | bytes 98312 | tf_op jit(solution)/shard_map/ppermute | solution.py:398
  27.0 1.8 %collective-permute-start.13 = (f32[32,256]{1,0:T(8,128)S(1)}, f32[32,256]{1,0:T(8,128)S(1)}, u32[]{:S(2)}, u32[]{:S(2)}) collective-permute-start(f32[32,256]{1,0:T(8,128)S(1)} %get-tuple-element.79), channel_id=1, source_target_pairs={{4,0},{0,4},{5,1},{1,5},{6,2},{2,6},{7,3},{3,7},{12,8},{8,12},{13,... | collective-permute-start | bytes 98312 | tf_op jit(solution)/shard_map/ppermute | solution.py:398
  34.8 3.5 %collective-permute-start.18 = (f32[32,256]{1,0:T(8,128)S(1)}, f32[32,256]{1,0:T(8,128)S(1)}, u32[]{:S(2)}, u32[]{:S(2)}) collective-permute-start(f32[32,256]{1,0:T(8,128)S(1)} %get-tuple-element.87), channel_id=1, source_target_pairs={{4,3},{0,4},{5,2},{1,5},{6,1},{2,6},{7,0},{3,7},{12,11},{8,12},{13... | collective-permute-start | bytes 98312 | tf_op jit(solution)/shard_map/ppermute | solution.py:398
  38.4 1.4 %collective-permute-start.20 = (f32[32,256]{1,0:T(8,128)S(1)}, f32[32,256]{1,0:T(8,128)S(1)}, u32[]{:S(2)}, u32[]{:S(2)}) collective-permute-start(f32[32,256]{1,0:T(8,128)S(1)} %get-tuple-element.87), channel_id=1, source_target_pairs={{4,2},{0,4},{5,3},{1,5},{6,0},{2,6},{7,1},{3,7},{12,10},{8,12},{13... | collective-permute-start | bytes 98312 | tf_op jit(solution)/shard_map/ppermute | solution.py:398
  45.8 3.9 %collective-permute-start.26 = (f32[32,256]{1,0:T(8,128)S(1)}, f32[32,256]{1,0:T(8,128)S(1)}, u32[]{:S(2)}, u32[]{:S(2)}) collective-permute-start(f32[32,256]{1,0:T(8,128)S(1)} %get-tuple-element.93), channel_id=1, source_target_pairs={{4,3},{0,4},{5,2},{1,5},{6,1},{2,6},{7,0},{3,7},{12,11},{8,12},{13... | collective-permute-start | bytes 98312 | tf_op jit(solution)/shard_map/ppermute | solution.py:398
  50.9 1.5 %collective-permute-done.26.refs_0_ = f32[32,256]{1,0:T(8,128)S(1)} collective-permute-done((f32[32,256]{1,0:T(8,128)S(1)}, f32[32,256]{1,0:T(8,128)S(1)}, u32[]{:S(2)}, u32[]{:S(2)}) %collective-permute-start.26) | collective-permute-done | bytes 32800 | tf_op jit(solution)/shard_map/ppermute | solution.py:398
  56.9 3.9 %collective-permute-start.34 = (f32[32,256]{1,0:T(8,128)S(1)}, f32[32,256]{1,0:T(8,128)S(1)}, u32[]{:S(2)}, u32[]{:S(2)}) collective-permute-start(f32[32,256]{1,0:T(8,128)S(1)} %get-tuple-element.99), channel_id=1, source_target_pairs={{4,3},{0,4},{5,2},{1,5},{6,1},{2,6},{7,0},{3,7},{12,11},{8,12},{13... | collective-permute-start | bytes 98312 | tf_op jit(solution)/shard_map/ppermute | solution.py:398
  62.1 1.4 %collective-permute-done.34.refs_0_ = f32[32,256]{1,0:T(8,128)S(1)} collective-permute-done((f32[32,256]{1,0:T(8,128)S(1)}, f32[32,256]{1,0:T(8,128)S(1)}, u32[]{:S(2)}, u32[]{:S(2)}) %collective-permute-start.34) | collective-permute-done | bytes 32800 | tf_op jit(solution)/shard_map/ppermute | solution.py:398
  68.1 3.9 %collective-permute-start.42 = (f32[32,256]{1,0:T(8,128)S(1)}, f32[32,256]{1,0:T(8,128)S(1)}, u32[]{:S(2)}, u32[]{:S(2)}) collective-permute-start(f32[32,256]{1,0:T(8,128)S(1)} %get-tuple-element.105), channel_id=1, source_target_pairs={{4,3},{0,4},{5,2},{1,5},{6,1},{2,6},{7,0},{3,7},{12,11},{8,12},{13... | collective-permute-start | bytes 98312 | tf_op jit(solution)/shard_map/ppermute | solution.py:398
  73.2 1.5 %collective-permute-done.42.refs_0_ = f32[32,256]{1,0:T(8,128)S(1)} collective-permute-done((f32[32,256]{1,0:T(8,128)S(1)}, f32[32,256]{1,0:T(8,128)S(1)}, u32[]{:S(2)}, u32[]{:S(2)}) %collective-permute-start.42) | collective-permute-done | bytes 32800 | tf_op jit(solution)/shard_map/ppermute | solution.py:398
  79.3 3.9 %collective-permute-start.50 = (f32[32,256]{1,0:T(8,128)S(1)}, f32[32,256]{1,0:T(8,128)S(1)}, u32[]{:S(2)}, u32[]{:S(2)}) collective-permute-start(f32[32,256]{1,0:T(8,128)S(1)} %get-tuple-element.111), channel_id=1, source_target_pairs={{4,3},{0,4},{5,2},{1,5},{6,1},{2,6},{7,0},{3,7},{12,11},{8,12},{13... | collective-permute-start | bytes 98312 | tf_op jit(solution)/shard_map/ppermute | solution.py:398
  84.4 1.4 %collective-permute-done.50.refs_0_ = f32[32,256]{1,0:T(8,128)S(1)} collective-permute-done((f32[32,256]{1,0:T(8,128)S(1)}, f32[32,256]{1,0:T(8,128)S(1)}, u32[]{:S(2)}, u32[]{:S(2)}) %collective-permute-start.50) | collective-permute-done | bytes 32800 | tf_op jit(solution)/shard_map/ppermute | solution.py:398
  90.5 3.9 %collective-permute-start.58 = (f32[32,256]{1,0:T(8,128)S(1)}, f32[32,256]{1,0:T(8,128)S(1)}, u32[]{:S(2)}, u32[]{:S(2)}) collective-permute-start(f32[32,256]{1,0:T(8,128)S(1)} %get-tuple-element.117), channel_id=1, source_target_pairs={{4,3},{0,4},{5,2},{1,5},{6,1},{2,6},{7,0},{3,7},{12,11},{8,12},{13... | collective-permute-start | bytes 98312 | tf_op jit(solution)/shard_map/ppermute | solution.py:398
  95.6 1.5 %collective-permute-done.58.refs_0_ = f32[32,256]{1,0:T(8,128)S(1)} collective-permute-done((f32[32,256]{1,0:T(8,128)S(1)}, f32[32,256]{1,0:T(8,128)S(1)}, u32[]{:S(2)}, u32[]{:S(2)}) %collective-permute-start.58) | collective-permute-done | bytes 32800 | tf_op jit(solution)/shard_map/ppermute | solution.py:398
  101.7 3.9 %collective-permute-start.66 = (f32[40,256]{1,0:T(8,128)S(1)}, f32[40,256]{1,0:T(8,128)S(1)}, u32[]{:S(2)}, u32[]{:S(2)}) collective-permute-start(f32[40,256]{1,0:T(8,128)S(1)} %get-tuple-element.123), channel_id=1, source_target_pairs={{4,3},{0,4},{5,2},{1,5},{6,1},{2,6},{7,0},{3,7},{12,11},{8,12},{13... | collective-permute-start | bytes 122888 | tf_op jit(solution)/shard_map/ppermute | solution.py:398
  106.8 1.5 %collective-permute-done.66.refs_0_ = f32[40,256]{1,0:T(8,128)S(1)} collective-permute-done((f32[40,256]{1,0:T(8,128)S(1)}, f32[40,256]{1,0:T(8,128)S(1)}, u32[]{:S(2)}, u32[]{:S(2)}) %collective-permute-start.66) | collective-permute-done | bytes 40992 | tf_op jit(solution)/shard_map/ppermute | solution.py:398
  111.4 3.0 %collective-permute-start.75 = (f32[2,8]{1,0:T(2,128)S(1)}, f32[2,8]{1,0:T(2,128)S(1)}, u32[]{:S(2)}, u32[]{:S(2)}) collective-permute-start(f32[2,8]{1,0:T(2,128)S(1)} %shard_map.124.own_ref), channel_id=1, source_target_pairs={{0,4},{4,0},{8,12},{12,8},{16,20},{20,16},{24,28},{28,24},{1,5},{5... | collective-permute-start | bytes 200 | tf_op jit(solution)/shard_map/ppermute | solution.py:489
  (156 shorter events, 54.6 us)
Async XLA Ops:
  2.1 12.4 %collective-permute-start.5 = (bf16[32,256,256]{2,1,0:T(8,128)(2,1)}, bf16[32,256,256]{2,1,0:T(8,128)(2,1)S(1)}, u32[]{:S(2)}, u32[]{:S(2)}) collective-permute-start(bf16[32,256,256]{2,1,0:T(8,128)(2,1)} %bitcast.3), channel_id=1, source_target_pairs={{0,4},{4,0},{8,12},{12,8},{16,20},{20,16},{24,28},{28,24},{1,5},{5... | collective-permute-start | bytes 12582920 | tf_op jit(solution)/shard_map/ppermute | solution.py:410
  2.7 7.1 %collective-permute-start = (f32[34,256]{1,0:T(8,128)}, f32[34,256]{1,0:T(8,128)S(1)}, u32[]{:S(2)}, u32[]{:S(2)}) collective-permute-start(f32[34,256]{1,0:T(8,128)} %shard_map.103.refs_0_), channel_id=1, source_target_pairs={{0,4},{4,0},{8,12},{12,8},{16,20},{20,16},{24,28},{28,24},{1,5},{5... | collective-permute-start | bytes 104456 | tf_op jit(solution)/shard_map/ppermute | solution.py:409
  9.9 4.9 %collective-permute-start.1 = (f32[8,256]{1,0:T(8,128)S(1)}, f32[8,256]{1,0:T(8,128)S(1)}, u32[]{:S(2)}, u32[]{:S(2)}) collective-permute-start(f32[8,256]{1,0:T(8,128)S(1)} %get-tuple-element.70), channel_id=1, source_target_pairs={{4,3},{0,4},{5,2},{1,5},{6,1},{2,6},{7,0},{3,7},{12,11},{8,12},{13... | collective-permute-start | bytes 24584 | tf_op jit(solution)/shard_map/ppermute | solution.py:398
  10.3 5.1 %collective-permute-start.2 = (f32[8,256]{1,0:T(8,128)S(1)}, f32[8,256]{1,0:T(8,128)S(1)}, u32[]{:S(2)}, u32[]{:S(2)}) collective-permute-start(f32[8,256]{1,0:T(8,128)S(1)} %get-tuple-element.70), channel_id=1, source_target_pairs={{4,1},{0,4},{5,0},{1,5},{6,3},{2,6},{7,2},{3,7},{12,9},{8,12},{13,... | collective-permute-start | bytes 24584 | tf_op jit(solution)/shard_map/ppermute | solution.py:398
  18.2 3.4 %collective-permute-start.6 = (f32[84,256]{1,0:T(8,128)S(1)}, f32[84,256]{1,0:T(8,128)S(1)}, u32[]{:S(2)}, u32[]{:S(2)}) collective-permute-start(f32[84,256]{1,0:T(8,128)S(1)} %get-tuple-element.77), channel_id=1, source_target_pairs={{0,28},{8,20},{16,12},{24,4},{4,0},{12,8},{20,16},{28,24},{1,29},{... | collective-permute-start | bytes 258056 | tf_op jit(solution)/shard_map/ppermute | solution.py:395
  19.9 3.6 %collective-permute-start.8 = (f32[84,256]{1,0:T(8,128)S(1)}, f32[84,256]{1,0:T(8,128)S(1)}, u32[]{:S(2)}, u32[]{:S(2)}) collective-permute-start(f32[84,256]{1,0:T(8,128)S(1)} %get-tuple-element.77), channel_id=1, source_target_pairs={{0,20},{8,28},{16,4},{24,12},{4,0},{12,8},{20,16},{28,24},{1,21},{... | collective-permute-start | bytes 258056 | tf_op jit(solution)/shard_map/ppermute | solution.py:395
  23.5 6.3 %collective-permute-start.10 = (f32[32,256]{1,0:T(8,128)S(1)}, f32[32,256]{1,0:T(8,128)S(1)}, u32[]{:S(2)}, u32[]{:S(2)}) collective-permute-start(f32[32,256]{1,0:T(8,128)S(1)} %get-tuple-element.79), channel_id=1, source_target_pairs={{4,3},{0,4},{5,2},{1,5},{6,1},{2,6},{7,0},{3,7},{12,11},{8,12},{13... | collective-permute-start | bytes 98312 | tf_op jit(solution)/shard_map/ppermute | solution.py:398
  26.3 3.4 %collective-permute-start.11 = (f32[32,256]{1,0:T(8,128)S(1)}, f32[32,256]{1,0:T(8,128)S(1)}, u32[]{:S(2)}, u32[]{:S(2)}) collective-permute-start(f32[32,256]{1,0:T(8,128)S(1)} %get-tuple-element.79), channel_id=1, source_target_pairs={{4,1},{0,4},{5,0},{1,5},{6,3},{2,6},{7,2},{3,7},{12,9},{8,12},{13,... | collective-permute-start | bytes 98312 | tf_op jit(solution)/shard_map/ppermute | solution.py:398
  26.4 4.0 %collective-permute-start.12 = (f32[32,256]{1,0:T(8,128)S(1)}, f32[32,256]{1,0:T(8,128)S(1)}, u32[]{:S(2)}, u32[]{:S(2)}) collective-permute-start(f32[32,256]{1,0:T(8,128)S(1)} %get-tuple-element.79), channel_id=1, source_target_pairs={{4,2},{0,4},{5,3},{1,5},{6,0},{2,6},{7,1},{3,7},{12,10},{8,12},{13... | collective-permute-start | bytes 98312 | tf_op jit(solution)/shard_map/ppermute | solution.py:398
  27.0 3.4 %collective-permute-start.13 = (f32[32,256]{1,0:T(8,128)S(1)}, f32[32,256]{1,0:T(8,128)S(1)}, u32[]{:S(2)}, u32[]{:S(2)}) collective-permute-start(f32[32,256]{1,0:T(8,128)S(1)} %get-tuple-element.79), channel_id=1, source_target_pairs={{4,0},{0,4},{5,1},{1,5},{6,2},{2,6},{7,3},{3,7},{12,8},{8,12},{13,... | collective-permute-start | bytes 98312 | tf_op jit(solution)/shard_map/ppermute | solution.py:398
  34.8 6.3 %collective-permute-start.18 = (f32[32,256]{1,0:T(8,128)S(1)}, f32[32,256]{1,0:T(8,128)S(1)}, u32[]{:S(2)}, u32[]{:S(2)}) collective-permute-start(f32[32,256]{1,0:T(8,128)S(1)} %get-tuple-element.87), channel_id=1, source_target_pairs={{4,3},{0,4},{5,2},{1,5},{6,1},{2,6},{7,0},{3,7},{12,11},{8,12},{13... | collective-permute-start | bytes 98312 | tf_op jit(solution)/shard_map/ppermute | solution.py:398
  38.3 3.3 %collective-permute-start.19 = (f32[32,256]{1,0:T(8,128)S(1)}, f32[32,256]{1,0:T(8,128)S(1)}, u32[]{:S(2)}, u32[]{:S(2)}) collective-permute-start(f32[32,256]{1,0:T(8,128)S(1)} %get-tuple-element.87), channel_id=1, source_target_pairs={{4,1},{0,4},{5,0},{1,5},{6,3},{2,6},{7,2},{3,7},{12,9},{8,12},{13,... | collective-permute-start | bytes 98312 | tf_op jit(solution)/shard_map/ppermute | solution.py:398
  38.4 3.3 %collective-permute-start.20 = (f32[32,256]{1,0:T(8,128)S(1)}, f32[32,256]{1,0:T(8,128)S(1)}, u32[]{:S(2)}, u32[]{:S(2)}) collective-permute-start(f32[32,256]{1,0:T(8,128)S(1)} %get-tuple-element.87), channel_id=1, source_target_pairs={{4,2},{0,4},{5,3},{1,5},{6,0},{2,6},{7,1},{3,7},{12,10},{8,12},{13... | collective-permute-start | bytes 98312 | tf_op jit(solution)/shard_map/ppermute | solution.py:398
  45.8 6.6 %collective-permute-start.26 = (f32[32,256]{1,0:T(8,128)S(1)}, f32[32,256]{1,0:T(8,128)S(1)}, u32[]{:S(2)}, u32[]{:S(2)}) collective-permute-start(f32[32,256]{1,0:T(8,128)S(1)} %get-tuple-element.93), channel_id=1, source_target_pairs={{4,3},{0,4},{5,2},{1,5},{6,1},{2,6},{7,0},{3,7},{12,11},{8,12},{13... | collective-permute-start | bytes 98312 | tf_op jit(solution)/shard_map/ppermute | solution.py:398
  49.7 3.3 %collective-permute-start.27 = (f32[32,256]{1,0:T(8,128)S(1)}, f32[32,256]{1,0:T(8,128)S(1)}, u32[]{:S(2)}, u32[]{:S(2)}) collective-permute-start(f32[32,256]{1,0:T(8,128)S(1)} %get-tuple-element.93), channel_id=1, source_target_pairs={{4,1},{0,4},{5,0},{1,5},{6,3},{2,6},{7,2},{3,7},{12,9},{8,12},{13,... | collective-permute-start | bytes 98312 | tf_op jit(solution)/shard_map/ppermute | solution.py:398
  56.9 6.5 %collective-permute-start.34 = (f32[32,256]{1,0:T(8,128)S(1)}, f32[32,256]{1,0:T(8,128)S(1)}, u32[]{:S(2)}, u32[]{:S(2)}) collective-permute-start(f32[32,256]{1,0:T(8,128)S(1)} %get-tuple-element.99), channel_id=1, source_target_pairs={{4,3},{0,4},{5,2},{1,5},{6,1},{2,6},{7,0},{3,7},{12,11},{8,12},{13... | collective-permute-start | bytes 98312 | tf_op jit(solution)/shard_map/ppermute | solution.py:398
  68.1 6.7 %collective-permute-start.42 = (f32[32,256]{1,0:T(8,128)S(1)}, f32[32,256]{1,0:T(8,128)S(1)}, u32[]{:S(2)}, u32[]{:S(2)}) collective-permute-start(f32[32,256]{1,0:T(8,128)S(1)} %get-tuple-element.105), channel_id=1, source_target_pairs={{4,3},{0,4},{5,2},{1,5},{6,1},{2,6},{7,0},{3,7},{12,11},{8,12},{13... | collective-permute-start | bytes 98312 | tf_op jit(solution)/shard_map/ppermute | solution.py:398
  79.3 6.5 %collective-permute-start.50 = (f32[32,256]{1,0:T(8,128)S(1)}, f32[32,256]{1,0:T(8,128)S(1)}, u32[]{:S(2)}, u32[]{:S(2)}) collective-permute-start(f32[32,256]{1,0:T(8,128)S(1)} %get-tuple-element.111), channel_id=1, source_target_pairs={{4,3},{0,4},{5,2},{1,5},{6,1},{2,6},{7,0},{3,7},{12,11},{8,12},{13... | collective-permute-start | bytes 98312 | tf_op jit(solution)/shard_map/ppermute | solution.py:398
  90.5 6.7 %collective-permute-start.58 = (f32[32,256]{1,0:T(8,128)S(1)}, f32[32,256]{1,0:T(8,128)S(1)}, u32[]{:S(2)}, u32[]{:S(2)}) collective-permute-start(f32[32,256]{1,0:T(8,128)S(1)} %get-tuple-element.117), channel_id=1, source_target_pairs={{4,3},{0,4},{5,2},{1,5},{6,1},{2,6},{7,0},{3,7},{12,11},{8,12},{13... | collective-permute-start | bytes 98312 | tf_op jit(solution)/shard_map/ppermute | solution.py:398
  101.7 6.6 %collective-permute-start.66 = (f32[40,256]{1,0:T(8,128)S(1)}, f32[40,256]{1,0:T(8,128)S(1)}, u32[]{:S(2)}, u32[]{:S(2)}) collective-permute-start(f32[40,256]{1,0:T(8,128)S(1)} %get-tuple-element.123), channel_id=1, source_target_pairs={{4,3},{0,4},{5,2},{1,5},{6,1},{2,6},{7,0},{3,7},{12,11},{8,12},{13... | collective-permute-start | bytes 122888 | tf_op jit(solution)/shard_map/ppermute | solution.py:398
  105.6 3.4 %collective-permute-start.67 = (f32[40,256]{1,0:T(8,128)S(1)}, f32[40,256]{1,0:T(8,128)S(1)}, u32[]{:S(2)}, u32[]{:S(2)}) collective-permute-start(f32[40,256]{1,0:T(8,128)S(1)} %get-tuple-element.123), channel_id=1, source_target_pairs={{4,1},{0,4},{5,0},{1,5},{6,3},{2,6},{7,2},{3,7},{12,9},{8,12},{13,... | collective-permute-start | bytes 122888 | tf_op jit(solution)/shard_map/ppermute | solution.py:398
  105.6 3.4 %collective-permute-start.68 = (f32[40,256]{1,0:T(8,128)S(1)}, f32[40,256]{1,0:T(8,128)S(1)}, u32[]{:S(2)}, u32[]{:S(2)}) collective-permute-start(f32[40,256]{1,0:T(8,128)S(1)} %get-tuple-element.123), channel_id=1, source_target_pairs={{4,2},{0,4},{5,3},{1,5},{6,0},{2,6},{7,1},{3,7},{12,10},{8,12},{13... | collective-permute-start | bytes 122888 | tf_op jit(solution)/shard_map/ppermute | solution.py:398
  110.1 4.2 %collective-permute-start.70 = (f32[6,256]{1,0:T(8,128)S(1)}, f32[6,256]{1,0:T(8,128)S(1)}, u32[]{:S(2)}, u32[]{:S(2)}) collective-permute-start(f32[6,256]{1,0:T(8,128)S(1)} %get-tuple-element.128), channel_id=1, source_target_pairs={{0,4},{4,0},{8,12},{12,8},{16,20},{20,16},{24,28},{28,24},{1,5},{5... | collective-permute-start | bytes 18440 | tf_op jit(solution)/shard_map/ppermute | solution.py:467
  111.4 3.8 %collective-permute-start.75 = (f32[2,8]{1,0:T(2,128)S(1)}, f32[2,8]{1,0:T(2,128)S(1)}, u32[]{:S(2)}, u32[]{:S(2)}) collective-permute-start(f32[2,8]{1,0:T(2,128)S(1)} %shard_map.124.own_ref), channel_id=1, source_target_pairs={{0,4},{4,0},{8,12},{12,8},{16,20},{20,16},{24,28},{28,24},{1,5},{5... | collective-permute-start | bytes 200 | tf_op jit(solution)/shard_map/ppermute | solution.py:489
  (54 other events, 129.9 us)

commit v5 on v4

--- a/solution.py
+++ b/solution.py
@@ -336,11 +336,11 @@
     @pl.when(jnp.logical_not(is_dual_core()))
     def _():
         def step(i, carry):
-            for k in range(8):
-                out_ref[i * 8 + k] = out_ref[i * 8 + k].T
+            for k in range(16):
+                out_ref[i * 16 + k] = out_ref[i * 16 + k].T
             return carry
 
-        lax.fori_loop(0, in_ref.shape[0] // 8, step, 0)
+        lax.fori_loop(0, in_ref.shape[0] // 16, step, 0)
 
 
 def weights_call(blocks):

time: 116 us -> 116 us (level)
  no operation moved by 1% of the time
where the time goes in v5:
time: 116 us
  starting transfers between devices  59.5 us (51%)
  waiting for transfers between devices  40.8 us (35%)
  Pallas kernels  12.4 us (11%)
  local copies, waits for them, and re-layouts  2.19 us (2%)
    ppermute x36, starting transfers between devices, to_dual(): lax.ppermute(x, ('row', 'col'), over_col(1 - DUAL, o))  45.3 us
    ppermute x36, waiting for transfers between devices, to_dual(): lax.ppermute(x, ('row', 'col'), over_col(1 - DUAL, o))  19.2 us
    ppermute x36, waiting for transfers between devices, to_primal(): return [lax.ppermute(x, 'row', over_z(DUAL, o)) for o in z_order(n_z)]  16.3 us
    ppermute x36, starting transfers between devices, to_primal(): return [lax.ppermute(x, 'row', over_z(DUAL, o)) for o in z_order(n_z)]  10.3 us
    pallas_call x8, Pallas kernels, per_device(): local_call(functools.partial(dual_body, iteration, n_col, slots), [shape(...  9.5 us
    ppermute x1, waiting for transfers between devices, per_device(): other = lax.ppermute(own, 'row', swap_pairs)  4.47 us
    ppermute x1, starting transfers between devices, per_device(): lax.ppermute(norms, 'row', swap_pairs)  2.92 us
  transfers between devices with their start and end apart: 76, of which 54 were waited for; matrix products, arithmetic and copies ran while one was open for 0% of the time, Pallas kernels for 1%

profile of v5, /device:TPU:0, one launch (start us, length us, event | category | flops | bytes accessed | tf_op | source)
XLA Modules:
  0.0 115.7 jit_solution(11675567129253868578)
XLA Ops:
  0.6 1.5 %shard_map.103.refs_0_ = f32[34,256]{1,0:T(8,128)} custom-call(s32[2,16]{1,0:T(2,128)} %bitcast.5, f32[1024]{0:T(1024)} %refs_1_.1, f32[1024]{0:T(1024)} %refs_2_.1, f32[1536]{0:T(1024)} %refs_3_.1, f32[1536]{0:T(1024)} %refs_4_.1, f32[1536]{0:T(1024)} %refs_5_.1, f32[1536]{0:T(1024)} %refs_6_.1), custom_call_target="tpu_custom_call" | custom-call | tf_op jit(solution)/shard_map/pallas_call | solution.py:222
  2.8 2.2 %copy-done = bf16[16,2,256,256]{3,2,1,0:T(8,128)(2,1)S(1)} copy-done((bf16[16,2,256,256]{3,2,1,0:T(8,128)(2,1)S(1)}, bf16[16,2,256,256]{3,2,1,0:T(8,128)(2,1)}, u32[]{:S(2)}) %copy-start) | copy-done | bytes 4194328
  5.3 4.5 %collective-permute-done.refs_1_ = f32[34,256]{1,0:T(8,128)S(1)} collective-permute-done((f32[34,256]{1,0:T(8,128)}, f32[34,256]{1,0:T(8,128)S(1)}, u32[]{:S(2)}, u32[]{:S(2)}) %collective-permute-start) | collective-permute-done | bytes 34848 | tf_op jit(solution)/shard_map/ppermute | solution.py:409
  10.3 3.5 %collective-permute-start.2 = (f32[8,256]{1,0:T(8,128)S(1)}, f32[8,256]{1,0:T(8,128)S(1)}, u32[]{:S(2)}, u32[]{:S(2)}) collective-permute-start(f32[8,256]{1,0:T(8,128)S(1)} %get-tuple-element.70), channel_id=1, source_target_pairs={{4,1},{0,4},{5,0},{1,5},{6,3},{2,6},{7,2},{3,7},{12,9},{8,12},{13,... | collective-permute-start | bytes 24584 | tf_op jit(solution)/shard_map/ppermute | solution.py:398
  15.5 1.5 %collective-permute-done.3.refs_2_ = f32[8,256]{1,0:T(8,128)S(1)} collective-permute-done((f32[8,256]{1,0:T(8,128)S(1)}, f32[8,256]{1,0:T(8,128)S(1)}, u32[]{:S(2)}, u32[]{:S(2)}) %collective-permute-start.3) | collective-permute-done | bytes 8224 | tf_op jit(solution)/shard_map/ppermute | solution.py:398
  17.0 1.2 %shard_map.107 = (f32[84,256]{1,0:T(8,128)S(1)}, f32[32,256]{1,0:T(8,128)S(1)}, f32[8,256]{1,0:T(8,128)S(1)}) custom-call(f32[8,256]{1,0:T(8,128)S(1)} %collective-permute-done.1.refs_0_, f32[8,256]{1,0:T(8,128)S(1)} %collective-permute-done.2.refs_1_, f32[8,256]{1,0:T(8,128)S(1)} %collective-permute-done.3.refs_2_, ...), custom_call_target="tpu_custom_call" | custom-call | tf_op jit(solution)/shard_map/pallas_call | solution.py:438
  23.3 3.0 %collective-permute-start.10 = (f32[32,256]{1,0:T(8,128)S(1)}, f32[32,256]{1,0:T(8,128)S(1)}, u32[]{:S(2)}, u32[]{:S(2)}) collective-permute-start(f32[32,256]{1,0:T(8,128)S(1)} %get-tuple-element.79), channel_id=1, source_target_pairs={{4,3},{0,4},{5,2},{1,5},{6,1},{2,6},{7,0},{3,7},{12,11},{8,12},{13... | collective-permute-start | bytes 98312 | tf_op jit(solution)/shard_map/ppermute | solution.py:398
  27.0 1.6 %collective-permute-start.13 = (f32[32,256]{1,0:T(8,128)S(1)}, f32[32,256]{1,0:T(8,128)S(1)}, u32[]{:S(2)}, u32[]{:S(2)}) collective-permute-start(f32[32,256]{1,0:T(8,128)S(1)} %get-tuple-element.79), channel_id=1, source_target_pairs={{4,0},{0,4},{5,1},{1,5},{6,2},{2,6},{7,3},{3,7},{12,8},{8,12},{13,... | collective-permute-start | bytes 98312 | tf_op jit(solution)/shard_map/ppermute | solution.py:398
  34.8 3.5 %collective-permute-start.18 = (f32[32,256]{1,0:T(8,128)S(1)}, f32[32,256]{1,0:T(8,128)S(1)}, u32[]{:S(2)}, u32[]{:S(2)}) collective-permute-start(f32[32,256]{1,0:T(8,128)S(1)} %get-tuple-element.87), channel_id=1, source_target_pairs={{4,3},{0,4},{5,2},{1,5},{6,1},{2,6},{7,0},{3,7},{12,11},{8,12},{13... | collective-permute-start | bytes 98312 | tf_op jit(solution)/shard_map/ppermute | solution.py:398
  38.4 1.3 %collective-permute-start.20 = (f32[32,256]{1,0:T(8,128)S(1)}, f32[32,256]{1,0:T(8,128)S(1)}, u32[]{:S(2)}, u32[]{:S(2)}) collective-permute-start(f32[32,256]{1,0:T(8,128)S(1)} %get-tuple-element.87), channel_id=1, source_target_pairs={{4,2},{0,4},{5,3},{1,5},{6,0},{2,6},{7,1},{3,7},{12,10},{8,12},{13... | collective-permute-start | bytes 98312 | tf_op jit(solution)/shard_map/ppermute | solution.py:398
  45.8 3.9 %collective-permute-start.26 = (f32[32,256]{1,0:T(8,128)S(1)}, f32[32,256]{1,0:T(8,128)S(1)}, u32[]{:S(2)}, u32[]{:S(2)}) collective-permute-start(f32[32,256]{1,0:T(8,128)S(1)} %get-tuple-element.93), channel_id=1, source_target_pairs={{4,3},{0,4},{5,2},{1,5},{6,1},{2,6},{7,0},{3,7},{12,11},{8,12},{13... | collective-permute-start | bytes 98312 | tf_op jit(solution)/shard_map/ppermute | solution.py:398
  50.8 1.5 %collective-permute-done.26.refs_0_ = f32[32,256]{1,0:T(8,128)S(1)} collective-permute-done((f32[32,256]{1,0:T(8,128)S(1)}, f32[32,256]{1,0:T(8,128)S(1)}, u32[]{:S(2)}, u32[]{:S(2)}) %collective-permute-start.26) | collective-permute-done | bytes 32800 | tf_op jit(solution)/shard_map/ppermute | solution.py:398
  56.9 3.9 %collective-permute-start.34 = (f32[32,256]{1,0:T(8,128)S(1)}, f32[32,256]{1,0:T(8,128)S(1)}, u32[]{:S(2)}, u32[]{:S(2)}) collective-permute-start(f32[32,256]{1,0:T(8,128)S(1)} %get-tuple-element.99), channel_id=1, source_target_pairs={{4,3},{0,4},{5,2},{1,5},{6,1},{2,6},{7,0},{3,7},{12,11},{8,12},{13... | collective-permute-start | bytes 98312 | tf_op jit(solution)/shard_map/ppermute | solution.py:398
  62.0 1.4 %collective-permute-done.34.refs_0_ = f32[32,256]{1,0:T(8,128)S(1)} collective-permute-done((f32[32,256]{1,0:T(8,128)S(1)}, f32[32,256]{1,0:T(8,128)S(1)}, u32[]{:S(2)}, u32[]{:S(2)}) %collective-permute-start.34) | collective-permute-done | bytes 32800 | tf_op jit(solution)/shard_map/ppermute | solution.py:398
  68.1 3.9 %collective-permute-start.42 = (f32[32,256]{1,0:T(8,128)S(1)}, f32[32,256]{1,0:T(8,128)S(1)}, u32[]{:S(2)}, u32[]{:S(2)}) collective-permute-start(f32[32,256]{1,0:T(8,128)S(1)} %get-tuple-element.105), channel_id=1, source_target_pairs={{4,3},{0,4},{5,2},{1,5},{6,1},{2,6},{7,0},{3,7},{12,11},{8,12},{13... | collective-permute-start | bytes 98312 | tf_op jit(solution)/shard_map/ppermute | solution.py:398
  73.1 1.5 %collective-permute-done.42.refs_0_ = f32[32,256]{1,0:T(8,128)S(1)} collective-permute-done((f32[32,256]{1,0:T(8,128)S(1)}, f32[32,256]{1,0:T(8,128)S(1)}, u32[]{:S(2)}, u32[]{:S(2)}) %collective-permute-start.42) | collective-permute-done | bytes 32800 | tf_op jit(solution)/shard_map/ppermute | solution.py:398
  79.3 3.9 %collective-permute-start.50 = (f32[32,256]{1,0:T(8,128)S(1)}, f32[32,256]{1,0:T(8,128)S(1)}, u32[]{:S(2)}, u32[]{:S(2)}) collective-permute-start(f32[32,256]{1,0:T(8,128)S(1)} %get-tuple-element.111), channel_id=1, source_target_pairs={{4,3},{0,4},{5,2},{1,5},{6,1},{2,6},{7,0},{3,7},{12,11},{8,12},{13... | collective-permute-start | bytes 98312 | tf_op jit(solution)/shard_map/ppermute | solution.py:398
  84.4 1.4 %collective-permute-done.50.refs_0_ = f32[32,256]{1,0:T(8,128)S(1)} collective-permute-done((f32[32,256]{1,0:T(8,128)S(1)}, f32[32,256]{1,0:T(8,128)S(1)}, u32[]{:S(2)}, u32[]{:S(2)}) %collective-permute-start.50) | collective-permute-done | bytes 32800 | tf_op jit(solution)/shard_map/ppermute | solution.py:398
  90.5 3.9 %collective-permute-start.58 = (f32[32,256]{1,0:T(8,128)S(1)}, f32[32,256]{1,0:T(8,128)S(1)}, u32[]{:S(2)}, u32[]{:S(2)}) collective-permute-start(f32[32,256]{1,0:T(8,128)S(1)} %get-tuple-element.117), channel_id=1, source_target_pairs={{4,3},{0,4},{5,2},{1,5},{6,1},{2,6},{7,0},{3,7},{12,11},{8,12},{13... | collective-permute-start | bytes 98312 | tf_op jit(solution)/shard_map/ppermute | solution.py:398
  95.5 1.5 %collective-permute-done.58.refs_0_ = f32[32,256]{1,0:T(8,128)S(1)} collective-permute-done((f32[32,256]{1,0:T(8,128)S(1)}, f32[32,256]{1,0:T(8,128)S(1)}, u32[]{:S(2)}, u32[]{:S(2)}) %collective-permute-start.58) | collective-permute-done | bytes 32800 | tf_op jit(solution)/shard_map/ppermute | solution.py:398
  97.8 1.2 %shard_map.121 = (f32[48,256]{1,0:T(8,128)S(1)}, f32[32,256]{1,0:T(8,128)S(1)}, f32[8,256]{1,0:T(8,128)S(1)}) custom-call(f32[32,256]{1,0:T(8,128)S(1)} %collective-permute-done.58.refs_0_, f32[32,256]{1,0:T(8,128)S(1)} %collective-permute-done.59.refs_1_, f32[32,256]{1,0:T(8,128)S(1)} %collective-permute-done.60.refs_2_, ...), custom_call_target="tpu_custom_call" | custom-call | tf_op jit(solution)/shard_map/pallas_call | solution.py:438
  101.7 3.9 %collective-permute-start.66 = (f32[40,256]{1,0:T(8,128)S(1)}, f32[40,256]{1,0:T(8,128)S(1)}, u32[]{:S(2)}, u32[]{:S(2)}) collective-permute-start(f32[40,256]{1,0:T(8,128)S(1)} %get-tuple-element.123), channel_id=1, source_target_pairs={{4,3},{0,4},{5,2},{1,5},{6,1},{2,6},{7,0},{3,7},{12,11},{8,12},{13... | collective-permute-start | bytes 122888 | tf_op jit(solution)/shard_map/ppermute | solution.py:398
  106.8 1.5 %collective-permute-done.66.refs_0_ = f32[40,256]{1,0:T(8,128)S(1)} collective-permute-done((f32[40,256]{1,0:T(8,128)S(1)}, f32[40,256]{1,0:T(8,128)S(1)}, u32[]{:S(2)}, u32[]{:S(2)}) %collective-permute-start.66) | collective-permute-done | bytes 40992 | tf_op jit(solution)/shard_map/ppermute | solution.py:398
  111.4 2.9 %collective-permute-start.75 = (f32[2,8]{1,0:T(2,128)S(1)}, f32[2,8]{1,0:T(2,128)S(1)}, u32[]{:S(2)}, u32[]{:S(2)}) collective-permute-start(f32[2,8]{1,0:T(2,128)S(1)} %shard_map.124.own_ref), channel_id=1, source_target_pairs={{0,4},{4,0},{8,12},{12,8},{16,20},{20,16},{24,28},{28,24},{1,5},{5... | collective-permute-start | bytes 200 | tf_op jit(solution)/shard_map/ppermute | solution.py:489
  (156 shorter events, 54.8 us)
Async XLA Ops:
  2.1 12.4 %collective-permute-start.5 = (bf16[32,256,256]{2,1,0:T(8,128)(2,1)}, bf16[32,256,256]{2,1,0:T(8,128)(2,1)S(1)}, u32[]{:S(2)}, u32[]{:S(2)}) collective-permute-start(bf16[32,256,256]{2,1,0:T(8,128)(2,1)} %bitcast.3), channel_id=1, source_target_pairs={{0,4},{4,0},{8,12},{12,8},{16,20},{20,16},{24,28},{28,24},{1,5},{5... | collective-permute-start | bytes 12582920 | tf_op jit(solution)/shard_map/ppermute | solution.py:410
  2.7 7.1 %collective-permute-start = (f32[34,256]{1,0:T(8,128)}, f32[34,256]{1,0:T(8,128)S(1)}, u32[]{:S(2)}, u32[]{:S(2)}) collective-permute-start(f32[34,256]{1,0:T(8,128)} %shard_map.103.refs_0_), channel_id=1, source_target_pairs={{0,4},{4,0},{8,12},{12,8},{16,20},{20,16},{24,28},{28,24},{1,5},{5... | collective-permute-start | bytes 104456 | tf_op jit(solution)/shard_map/ppermute | solution.py:409
  9.9 4.9 %collective-permute-start.1 = (f32[8,256]{1,0:T(8,128)S(1)}, f32[8,256]{1,0:T(8,128)S(1)}, u32[]{:S(2)}, u32[]{:S(2)}) collective-permute-start(f32[8,256]{1,0:T(8,128)S(1)} %get-tuple-element.70), channel_id=1, source_target_pairs={{4,3},{0,4},{5,2},{1,5},{6,1},{2,6},{7,0},{3,7},{12,11},{8,12},{13... | collective-permute-start | bytes 24584 | tf_op jit(solution)/shard_map/ppermute | solution.py:398
  10.3 5.1 %collective-permute-start.2 = (f32[8,256]{1,0:T(8,128)S(1)}, f32[8,256]{1,0:T(8,128)S(1)}, u32[]{:S(2)}, u32[]{:S(2)}) collective-permute-start(f32[8,256]{1,0:T(8,128)S(1)} %get-tuple-element.70), channel_id=1, source_target_pairs={{4,1},{0,4},{5,0},{1,5},{6,3},{2,6},{7,2},{3,7},{12,9},{8,12},{13,... | collective-permute-start | bytes 24584 | tf_op jit(solution)/shard_map/ppermute | solution.py:398
  19.9 3.5 %collective-permute-start.8 = (f32[84,256]{1,0:T(8,128)S(1)}, f32[84,256]{1,0:T(8,128)S(1)}, u32[]{:S(2)}, u32[]{:S(2)}) collective-permute-start(f32[84,256]{1,0:T(8,128)S(1)} %get-tuple-element.77), channel_id=1, source_target_pairs={{0,20},{8,28},{16,4},{24,12},{4,0},{12,8},{20,16},{28,24},{1,21},{... | collective-permute-start | bytes 258056 | tf_op jit(solution)/shard_map/ppermute | solution.py:395
  23.3 6.3 %collective-permute-start.10 = (f32[32,256]{1,0:T(8,128)S(1)}, f32[32,256]{1,0:T(8,128)S(1)}, u32[]{:S(2)}, u32[]{:S(2)}) collective-permute-start(f32[32,256]{1,0:T(8,128)S(1)} %get-tuple-element.79), channel_id=1, source_target_pairs={{4,3},{0,4},{5,2},{1,5},{6,1},{2,6},{7,0},{3,7},{12,11},{8,12},{13... | collective-permute-start | bytes 98312 | tf_op jit(solution)/shard_map/ppermute | solution.py:398
  26.3 3.3 %collective-permute-start.11 = (f32[32,256]{1,0:T(8,128)S(1)}, f32[32,256]{1,0:T(8,128)S(1)}, u32[]{:S(2)}, u32[]{:S(2)}) collective-permute-start(f32[32,256]{1,0:T(8,128)S(1)} %get-tuple-element.79), channel_id=1, source_target_pairs={{4,1},{0,4},{5,0},{1,5},{6,3},{2,6},{7,2},{3,7},{12,9},{8,12},{13,... | collective-permute-start | bytes 98312 | tf_op jit(solution)/shard_map/ppermute | solution.py:398
  26.4 3.9 %collective-permute-start.12 = (f32[32,256]{1,0:T(8,128)S(1)}, f32[32,256]{1,0:T(8,128)S(1)}, u32[]{:S(2)}, u32[]{:S(2)}) collective-permute-start(f32[32,256]{1,0:T(8,128)S(1)} %get-tuple-element.79), channel_id=1, source_target_pairs={{4,2},{0,4},{5,3},{1,5},{6,0},{2,6},{7,1},{3,7},{12,10},{8,12},{13... | collective-permute-start | bytes 98312 | tf_op jit(solution)/shard_map/ppermute | solution.py:398
  34.8 6.1 %collective-permute-start.18 = (f32[32,256]{1,0:T(8,128)S(1)}, f32[32,256]{1,0:T(8,128)S(1)}, u32[]{:S(2)}, u32[]{:S(2)}) collective-permute-start(f32[32,256]{1,0:T(8,128)S(1)} %get-tuple-element.87), channel_id=1, source_target_pairs={{4,3},{0,4},{5,2},{1,5},{6,1},{2,6},{7,0},{3,7},{12,11},{8,12},{13... | collective-permute-start | bytes 98312 | tf_op jit(solution)/shard_map/ppermute | solution.py:398
  38.3 3.3 %collective-permute-start.19 = (f32[32,256]{1,0:T(8,128)S(1)}, f32[32,256]{1,0:T(8,128)S(1)}, u32[]{:S(2)}, u32[]{:S(2)}) collective-permute-start(f32[32,256]{1,0:T(8,128)S(1)} %get-tuple-element.87), channel_id=1, source_target_pairs={{4,1},{0,4},{5,0},{1,5},{6,3},{2,6},{7,2},{3,7},{12,9},{8,12},{13,... | collective-permute-start | bytes 98312 | tf_op jit(solution)/shard_map/ppermute | solution.py:398
  38.4 3.3 %collective-permute-start.20 = (f32[32,256]{1,0:T(8,128)S(1)}, f32[32,256]{1,0:T(8,128)S(1)}, u32[]{:S(2)}, u32[]{:S(2)}) collective-permute-start(f32[32,256]{1,0:T(8,128)S(1)} %get-tuple-element.87), channel_id=1, source_target_pairs={{4,2},{0,4},{5,3},{1,5},{6,0},{2,6},{7,1},{3,7},{12,10},{8,12},{13... | collective-permute-start | bytes 98312 | tf_op jit(solution)/shard_map/ppermute | solution.py:398
  45.8 6.5 %collective-permute-start.26 = (f32[32,256]{1,0:T(8,128)S(1)}, f32[32,256]{1,0:T(8,128)S(1)}, u32[]{:S(2)}, u32[]{:S(2)}) collective-permute-start(f32[32,256]{1,0:T(8,128)S(1)} %get-tuple-element.93), channel_id=1, source_target_pairs={{4,3},{0,4},{5,2},{1,5},{6,1},{2,6},{7,0},{3,7},{12,11},{8,12},{13... | collective-permute-start | bytes 98312 | tf_op jit(solution)/shard_map/ppermute | solution.py:398
  49.7 3.3 %collective-permute-start.27 = (f32[32,256]{1,0:T(8,128)S(1)}, f32[32,256]{1,0:T(8,128)S(1)}, u32[]{:S(2)}, u32[]{:S(2)}) collective-permute-start(f32[32,256]{1,0:T(8,128)S(1)} %get-tuple-element.93), channel_id=1, source_target_pairs={{4,1},{0,4},{5,0},{1,5},{6,3},{2,6},{7,2},{3,7},{12,9},{8,12},{13,... | collective-permute-start | bytes 98312 | tf_op jit(solution)/shard_map/ppermute | solution.py:398
  49.7 3.3 %collective-permute-start.28 = (f32[32,256]{1,0:T(8,128)S(1)}, f32[32,256]{1,0:T(8,128)S(1)}, u32[]{:S(2)}, u32[]{:S(2)}) collective-permute-start(f32[32,256]{1,0:T(8,128)S(1)} %get-tuple-element.93), channel_id=1, source_target_pairs={{4,2},{0,4},{5,3},{1,5},{6,0},{2,6},{7,1},{3,7},{12,10},{8,12},{13... | collective-permute-start | bytes 98312 | tf_op jit(solution)/shard_map/ppermute | solution.py:398
  56.9 6.5 %collective-permute-start.34 = (f32[32,256]{1,0:T(8,128)S(1)}, f32[32,256]{1,0:T(8,128)S(1)}, u32[]{:S(2)}, u32[]{:S(2)}) collective-permute-start(f32[32,256]{1,0:T(8,128)S(1)} %get-tuple-element.99), channel_id=1, source_target_pairs={{4,3},{0,4},{5,2},{1,5},{6,1},{2,6},{7,0},{3,7},{12,11},{8,12},{13... | collective-permute-start | bytes 98312 | tf_op jit(solution)/shard_map/ppermute | solution.py:398
  60.8 3.3 %collective-permute-start.35 = (f32[32,256]{1,0:T(8,128)S(1)}, f32[32,256]{1,0:T(8,128)S(1)}, u32[]{:S(2)}, u32[]{:S(2)}) collective-permute-start(f32[32,256]{1,0:T(8,128)S(1)} %get-tuple-element.99), channel_id=1, source_target_pairs={{4,1},{0,4},{5,0},{1,5},{6,3},{2,6},{7,2},{3,7},{12,9},{8,12},{13,... | collective-permute-start | bytes 98312 | tf_op jit(solution)/shard_map/ppermute | solution.py:398
  68.1 6.5 %collective-permute-start.42 = (f32[32,256]{1,0:T(8,128)S(1)}, f32[32,256]{1,0:T(8,128)S(1)}, u32[]{:S(2)}, u32[]{:S(2)}) collective-permute-start(f32[32,256]{1,0:T(8,128)S(1)} %get-tuple-element.105), channel_id=1, source_target_pairs={{4,3},{0,4},{5,2},{1,5},{6,1},{2,6},{7,0},{3,7},{12,11},{8,12},{13... | collective-permute-start | bytes 98312 | tf_op jit(solution)/shard_map/ppermute | solution.py:398
  79.3 6.5 %collective-permute-start.50 = (f32[32,256]{1,0:T(8,128)S(1)}, f32[32,256]{1,0:T(8,128)S(1)}, u32[]{:S(2)}, u32[]{:S(2)}) collective-permute-start(f32[32,256]{1,0:T(8,128)S(1)} %get-tuple-element.111), channel_id=1, source_target_pairs={{4,3},{0,4},{5,2},{1,5},{6,1},{2,6},{7,0},{3,7},{12,11},{8,12},{13... | collective-permute-start | bytes 98312 | tf_op jit(solution)/shard_map/ppermute | solution.py:398
  90.5 6.5 %collective-permute-start.58 = (f32[32,256]{1,0:T(8,128)S(1)}, f32[32,256]{1,0:T(8,128)S(1)}, u32[]{:S(2)}, u32[]{:S(2)}) collective-permute-start(f32[32,256]{1,0:T(8,128)S(1)} %get-tuple-element.117), channel_id=1, source_target_pairs={{4,3},{0,4},{5,2},{1,5},{6,1},{2,6},{7,0},{3,7},{12,11},{8,12},{13... | collective-permute-start | bytes 98312 | tf_op jit(solution)/shard_map/ppermute | solution.py:398
  101.7 6.6 %collective-permute-start.66 = (f32[40,256]{1,0:T(8,128)S(1)}, f32[40,256]{1,0:T(8,128)S(1)}, u32[]{:S(2)}, u32[]{:S(2)}) collective-permute-start(f32[40,256]{1,0:T(8,128)S(1)} %get-tuple-element.123), channel_id=1, source_target_pairs={{4,3},{0,4},{5,2},{1,5},{6,1},{2,6},{7,0},{3,7},{12,11},{8,12},{13... | collective-permute-start | bytes 122888 | tf_op jit(solution)/shard_map/ppermute | solution.py:398
  105.6 3.4 %collective-permute-start.67 = (f32[40,256]{1,0:T(8,128)S(1)}, f32[40,256]{1,0:T(8,128)S(1)}, u32[]{:S(2)}, u32[]{:S(2)}) collective-permute-start(f32[40,256]{1,0:T(8,128)S(1)} %get-tuple-element.123), channel_id=1, source_target_pairs={{4,1},{0,4},{5,0},{1,5},{6,3},{2,6},{7,2},{3,7},{12,9},{8,12},{13,... | collective-permute-start | bytes 122888 | tf_op jit(solution)/shard_map/ppermute | solution.py:398
  105.6 3.4 %collective-permute-start.68 = (f32[40,256]{1,0:T(8,128)S(1)}, f32[40,256]{1,0:T(8,128)S(1)}, u32[]{:S(2)}, u32[]{:S(2)}) collective-permute-start(f32[40,256]{1,0:T(8,128)S(1)} %get-tuple-element.123), channel_id=1, source_target_pairs={{4,2},{0,4},{5,3},{1,5},{6,0},{2,6},{7,1},{3,7},{12,10},{8,12},{13... | collective-permute-start | bytes 122888 | tf_op jit(solution)/shard_map/ppermute | solution.py:398
  110.1 4.2 %collective-permute-start.70 = (f32[6,256]{1,0:T(8,128)S(1)}, f32[6,256]{1,0:T(8,128)S(1)}, u32[]{:S(2)}, u32[]{:S(2)}) collective-permute-start(f32[6,256]{1,0:T(8,128)S(1)} %get-tuple-element.128), channel_id=1, source_target_pairs={{0,4},{4,0},{8,12},{12,8},{16,20},{20,16},{24,28},{28,24},{1,5},{5... | collective-permute-start | bytes 18440 | tf_op jit(solution)/shard_map/ppermute | solution.py:467
  111.4 3.7 %collective-permute-start.75 = (f32[2,8]{1,0:T(2,128)S(1)}, f32[2,8]{1,0:T(2,128)S(1)}, u32[]{:S(2)}, u32[]{:S(2)}) collective-permute-start(f32[2,8]{1,0:T(2,128)S(1)} %shard_map.124.own_ref), channel_id=1, source_target_pairs={{0,4},{4,0},{8,12},{12,8},{16,20},{20,16},{24,28},{28,24},{1,5},{5... | collective-permute-start | bytes 200 | tf_op jit(solution)/shard_map/ppermute | solution.py:489
  (54 other events, 130.4 us)
